TPU v7x, 256 devices: a whole 4x4x8 slice. The times are simulated.
256 devices in a mesh: tm: 16 (over z, core), space: 16 (over y, x).
Axes of the slice: x: 4, y: 4, z: 8, core: 2. Of those that a mesh axis runs over, the one named last changes fastest.
Arguments:
- initial: float32 [2, 512, 512], P(None, 'space'), may hold values from 0.2 to 1
- guess: float32 [256, 2, 512, 512], P('tm', None, 'space'), may hold values from 0 to 1
- kappa: float32 [2, 512, 512], P(None, 'space'), may hold values from 0.005 to 0.05
- feed: float32 [512, 512], P('space'), may hold values from 0.002 to 0.01
- kill: float32 [512, 512], P('space'), may hold values from 0.002 to 0.008
- react: float32 [512, 512], P('space'), may hold values from 0.002 to 0.008
Outputs:
- solution: float32 [256, 2, 512, 512], P('tm', None, 'space')
All inputs are finite; a program needn't handle non-finite values.
Results may differ from a plain program's by a relative error of at most 0.00002.
Values sent between devices are 32-bit elements; how exact they have to be, the bound alone decides.
No kernel may reach another device: no remote copies, remote signals or barrier semaphores. Data moves between devices by JAX's collectives and lax.ppermute only.
A program may use at most 128 MiB of HBM per device.

v0:
```python
import jax
import jax.numpy as jnp
from jax import lax
from jax.sharding import Mesh
from jax.sharding import PartitionSpec as P

SPAN = 8
SPACE = ("space_0", "space_1")
TM = ("tm_0", "tm_1")
TM_SPACE = ("tm_0", "tm_1", "space_0", "space_1")


def padded_2(block, sides, width):
    for axis, dim in sides:
        count = lax.axis_size(axis)
        forward = [(i, i + 1) for i in range(count - 1)]
        backward = [(target, source) for source, target in forward]
        low = lax.ppermute(
            lax.slice_in_dim(block, block.shape[dim] - width, None, axis=dim), axis, forward
        )
        high = lax.ppermute(lax.slice_in_dim(block, 0, width, axis=dim), axis, backward)
        block = jnp.concatenate([low, block, high], axis=dim)
    return block


def shifted(block, axis, distance):
    devices = range(lax.axis_size(axis))
    route = [(i - distance, i) for i in devices if i - distance in devices]
    return lax.ppermute(block, axis, route)


def in_order(parts, dim):
    shape = list(parts.shape[1:])
    shape[dim] *= parts.shape[0]
    return jnp.moveaxis(parts, 0, dim).reshape(shape)


def gather_in_order(x, axes, turns):
    parts = x[None]
    for k in turns:
        parts = lax.all_gather(parts, axes[k], axis=0, tiled=True)
    carried = [lax.axis_size(axes[k]) for k in reversed(turns)]
    parts = parts.reshape(*carried, *x.shape)
    turned = sorted(range(len(turns)), key=lambda place: turns[len(turns) - 1 - place])
    return parts.transpose(*turned, *range(len(turns), parts.ndim)).reshape(-1, *x.shape)


def gather_axes(x, axes, turns, dim):
    return in_order(gather_in_order(x, axes, turns), dim)


def coarsen(field):
    shape = field.shape
    blocks = field.reshape(shape[:-2] + (shape[-2] // 2, 2, shape[-1] // 2, 2))
    return blocks.mean(axis=(-3, -1))


def refine(field):
    return jnp.repeat(jnp.repeat(field, 2, axis=-2), 2, axis=-1)


def advance(state, row_padded, coeffs):
    spread, supply, removal, coupling = coeffs
    padded = jnp.pad(row_padded, [(0, 0)] * (row_padded.ndim - 1) + [(1, 1)])
    laplace = (
        padded[..., :-2, 1:-1]
        + padded[..., 2:, 1:-1]
        + padded[..., 1:-1, :-2]
        + padded[..., 1:-1, 2:]
        - 4.0 * state
    )
    first_species = state[..., 0, :, :]
    second_species = state[..., 1, :, :]
    coupled = coupling * first_species * second_species * second_species
    next_first = (
        first_species + spread[0] * laplace[..., 0, :, :] - coupled + supply * (1.0 - first_species)
    )
    next_second = (
        second_species
        + spread[1] * laplace[..., 1, :, :]
        + coupled
        - (supply + removal) * second_species
    )
    return jnp.stack([next_first, next_second], axis=-3)


def margin_advance(state, coeffs, inside_mask):
    row_padded = jnp.pad(state, [(0, 0)] * (state.ndim - 2) + [(1, 1), (0, 0)])
    return advance(state, row_padded, coeffs) * inside_mask


def inside_rows(strip_rows, margin):
    global_rows = (
        lax.axis_index(SPACE) * strip_rows
        - margin
        + jnp.arange(strip_rows + 2 * margin, dtype=jnp.int32)
    )
    inside_mask = (global_rows >= 0) & (global_rows < strip_rows * lax.axis_size(SPACE))
    return inside_mask.astype(jnp.float32)[:, None]


def split_coeffs(packed):
    return (packed[0:2], packed[2], packed[3], packed[4])


def pack_coeffs(coeffs):
    return jnp.concatenate([coeffs[0], coeffs[1][None], coeffs[2][None], coeffs[3][None]])


def local(initial, guess, kappa, feed, kill, react):
    group = SPAN // 2
    time_index = lax.axis_index(TM)
    opening = time_index == 0
    member = time_index % group
    holder = member == group - 1
    level_zero = (kappa, feed, kill, react)
    spread_one = coarsen(kappa)
    supply_one = coarsen(feed)
    removal_one = coarsen(kill)
    coupling_one = coarsen(react)
    level_one = (2.0 * spread_one, 8.0 * supply_one, 8.0 * removal_one, 8.0 * coupling_one)
    level_two = (
        4.0 * coarsen(spread_one),
        64.0 * coarsen(supply_one),
        64.0 * coarsen(removal_one),
        64.0 * coarsen(coupling_one),
    )
    start_one = coarsen(initial)
    start_two = coarsen(start_one)
    strip_rows = initial.shape[-2]
    mid_rows = strip_rows // 2
    margin = SPAN - 1

    def fine_step(state):
        row_padded = padded_2(state, ((SPACE, 2),), 1)
        return advance(state, row_padded, level_zero)

    def fine_relax(series):
        incoming = shifted(series[-1], TM, 1)
        incoming = jnp.where(opening, initial, incoming)
        current = jnp.stack([incoming, series[SPAN - 1]])
        early = []
        later = []
        widened = padded_2(current, ((SPACE, 2),), margin)
        for position in range(SPAN - 1):
            widened = margin_advance(widened, fine_wide_coeffs, fine_mask)
            early.append(widened[0, :, margin : margin + strip_rows])
            later.append(widened[1, :, margin : margin + strip_rows])
        return (jnp.stack(early + [series[SPAN - 1]] + later + [series[-1]]), incoming)

    def mid_relax(values):
        predicted = values[1]
        for section in range(group):
            incoming = shifted(values[1], TM, 1)
            incoming = jnp.where(opening, start_one, incoming)
            widened = padded_2(incoming, ((SPACE, 1),), 2)
            first_wide = margin_advance(widened, mid_wide_coeffs, mid_mask) + mid_wide_forcing[0]
            second_wide = (
                margin_advance(first_wide, mid_wide_coeffs, mid_mask) + mid_wide_forcing[1]
            )
            fresh_first = first_wide[:, 2 : 2 + mid_rows]
            predicted = second_wide[:, 2 : 2 + mid_rows]
            fresh_second = predicted if section < group - 1 else values[1]
            values = jnp.where(member == section, jnp.stack([fresh_first, fresh_second]), values)
        return (values, predicted)

    fine_wide = padded_2(pack_coeffs(level_zero), ((SPACE, 1),), margin)
    fine_wide_coeffs = split_coeffs(fine_wide)
    fine_mask = inside_rows(strip_rows, margin)
    mid_mask = inside_rows(mid_rows, 2)
    series, incoming = fine_relax(guess)
    updated = fine_step(jnp.stack([series[SPAN - 2], series[-2]]))
    series = series.at[SPAN - 1].set(updated[0]).at[-1].set(updated[1])
    series, incoming = fine_relax(series)
    ends = jnp.stack([series[SPAN - 1], series[-1]])
    residual = fine_step(jnp.stack([series[SPAN - 2], series[-2]])) - ends
    restricted = coarsen(ends)
    earlier = jnp.stack([coarsen(incoming), restricted[0]])
    row_padded = padded_2(earlier, ((SPACE, 2),), 1)
    forcing_one = coarsen(residual) + restricted - advance(earlier, row_padded, level_one)
    mid_packed = jnp.concatenate(
        [pack_coeffs(level_one), forcing_one.reshape((4,) + forcing_one.shape[-2:])]
    )
    mid_wide = padded_2(mid_packed, ((SPACE, 1),), 2)
    mid_wide_coeffs = split_coeffs(mid_wide)
    mid_wide_forcing = mid_wide[5:9].reshape((2, 2) + mid_wide.shape[-2:])
    middle, predicted = mid_relax(restricted)
    coarse_values = coarsen(middle[1])
    coarse_right = coarsen(predicted - middle[1]) + coarse_values
    tm_count = lax.axis_size(TM)
    space_count = lax.axis_size(SPACE)
    rows_two = coarse_values.shape[-2]
    cols_two = coarse_values.shape[-1]
    quarter = cols_two // group
    reach = tm_count // group
    stacked = jnp.concatenate([coarse_values, coarse_right])
    held_piece = stacked[..., (group - 1) * quarter :]
    for distance in range(1, group):
        sent_part = stacked[..., (group - 1 - distance) * quarter : (group - distance) * quarter]
        arriving = shifted(sent_part, TM, -distance)
        held_piece = jnp.where(member == group - 1 - distance, arriving, held_piece)
    gathered = gather_axes(held_piece[None], TM_SPACE, (0, 2, 3, 1), 0)
    arranged = gathered.reshape((tm_count // group, group, space_count, 4, rows_two, quarter))
    arranged = jnp.transpose(arranged, (0, 3, 2, 4, 1, 5)).reshape(
        (tm_count // group, 4, space_count * rows_two, cols_two)
    )
    padded_held = jnp.pad(arranged, ((0, 0), (0, 0), (reach, reach), (0, 0)))
    window = lax.dynamic_slice_in_dim(
        padded_held, lax.axis_index(SPACE) * rows_two, rows_two + 2 * reach, 2
    )
    held_values = window[:, 0:2]
    held_right = window[:, 2:4]
    packed = jnp.concatenate([pack_coeffs(level_two), start_two])
    widened = padded_2(packed, ((SPACE, 1),), reach)
    wide_coeffs = split_coeffs(widened)
    wide_start = widened[5:7]
    coarse_mask = inside_rows(rows_two, reach)

    def wide_step(state):
        return margin_advance(state, wide_coeffs, coarse_mask)

    coarse_prev = jnp.concatenate([wide_start[None], held_values[:-1]])
    forcing_two = held_right - wide_step(coarse_prev)

    def march(previous, forcing_step):
        following = wide_step(previous) + forcing_step
        return (following, following)

    unused, solved = lax.scan(march, wide_start, forcing_two)
    own_point = time_index // group
    wide_change = lax.dynamic_index_in_dim(solved, own_point, 0, False) - lax.dynamic_index_in_dim(
        held_values, own_point, 0, False
    )
    correction = wide_change[:, reach : reach + rows_two]
    middle = middle.at[1].set(jnp.where(holder, middle[1] + refine(correction), middle[1]))
    middle, predicted = mid_relax(middle)
    change = refine(middle - restricted)
    series = series.at[SPAN - 1].add(change[0]).at[-1].add(change[1])
    series, incoming = fine_relax(series)
    return series


def solution(mesh):
    split = Mesh(mesh.devices.reshape(8, 2, 4, 4), ("tm_0", "tm_1", "space_0", "space_1"))
    placed = (
        P(None, SPACE, None),
        P(TM, None, SPACE, None),
        P(None, SPACE, None),
        P(SPACE, None),
        P(SPACE, None),
        P(SPACE, None),
    )
    return jax.shard_map(
        local, mesh=split, in_specs=placed, out_specs=P(TM, None, SPACE, None), check_vma=False
    )
```

profile of v0, /device:TPU:134, one launch (start us, length us, event | category | flops | bytes accessed | tf_op | source)
XLA Modules:
  0.0 520.0 jit_solution(8484025513956494548)
XLA Ops:
  10.3 3.4 collective-permute-start.3
  17.1 6.4 %reshape.425 = f32[16,2,256,2]{3,2,1,0:T(8,128)} reshape(f32[32,512]{1,0:T(8,128)} %param.21) | data formatting | bytes 131072 | tf_op jit(solution)/shard_map/reshape | solution.py:54
  23.5 5.5 %reshape.426 = f32[16,2,256,2]{3,2,1,0:T(8,128)} reshape(f32[32,512]{1,0:T(8,128)S(1)} %copy-done.4) | data formatting | bytes 131072 | tf_op jit(solution)/shard_map/reshape | solution.py:54
  29.1 5.6 %reshape.427 = f32[16,2,256,2]{3,2,1,0:T(8,128)} reshape(f32[32,512]{1,0:T(8,128)S(1)} %copy-done.3) | data formatting | bytes 131072 | tf_op jit(solution)/shard_map/reshape | solution.py:54
  34.6 9.8 %reshape.424 = f32[2,16,2,256,2]{4,3,2,1,0:T(8,128)} reshape(f32[2,32,512]{2,1,0:T(8,128)S(1)} %copy-done.1) | data formatting | bytes 262144 | tf_op jit(solution)/shard_map/reshape | solution.py:54
  52.9 4.6 reduce_sum.137
  57.8 5.5 %collective-permute-start.1 = (f32[2,2,7,512]{3,1,2,0:T(2,128)S(1)}, f32[2,2,7,512]{3,1,2,0:T(2,128)S(1)}, u32[]{:S(2)}, u32[]{:S(2)}) collective-permute-start(f32[2,2,7,512]{3,1,2,0:T(2,128)S(1)} %copy.483), channel_id=1, source_target_pairs={{0,1},{1,2},{2,3},{3,4},{4,5},{5,6},{6,7},{7,8},{8,9},{9,10},{10,1... | collective-permute-start | bytes 172040 | tf_op jit(solution)/shard_map/ppermute | solution.py:18
  65.6 6.0 %collective-permute-done.2 = f32[2,2,7,512]{3,1,2,0:T(2,128)S(1)} collective-permute-done((f32[2,2,7,512]{3,1,2,0:T(2,128)S(1)}, f32[2,2,7,512]{3,1,2,0:T(2,128)S(1)}, u32[]{:S(2)}, u32[]{:S(2)}) %collective-permute-start.2) | collective-permute-done | bytes 57376 | tf_op jit(solution)/shard_map/ppermute | solution.py:21
  77.7 3.9 collective-permute-start.6
  81.7 9.8 %reshape.422 = f32[2,16,2,256,2]{4,3,2,1,0:T(8,128)} reshape(f32[2,32,512]{2,1,0:T(8,128)S(1)} %copy-done.2) | data formatting | bytes 262144 | tf_op jit(solution)/shard_map/reshape | solution.py:54
  91.5 4.6 reduce_sum.135
  96.7 18.1 %reshape.423 = f32[2,2,16,2,256,2]{5,4,3,2,1,0:T(8,128)} reshape(f32[2,2,32,512]{3,2,1,0:T(8,128)S(1)} %pad_maximum_fusion.4) | data formatting | bytes 524288 | tf_op jit(solution)/shard_map/reshape | solution.py:54
  114.8 8.0 %reduce_sum.136 = f32[2,2,16,256]{3,2,1,0:T(8,128)S(1)} reduce(f32[2,2,16,2,256,2]{5,4,3,2,1,0:T(8,128)} %reshape.423, f32[]{:T(128)} %constant.259.clone.1), dimensions={3,5}, to_apply=%region_1.2 | reduce | flops 49152 | bytes 327684 | tf_op jit(solution)/shard_map/reduce_sum | solution.py:55
  129.3 4.0 collective-permute-start.8
  135.8 9.8 %stack.349 = f32[1,2,16,2,256,2]{5,4,3,2,1,0:T(8,128)} reshape(f32[1,2,32,512]{3,2,1,0:T(8,128)S(1)} %get-tuple-element.295) | data formatting | bytes 262144 | tf_op jit(solution)/shard_map/stack | solution.py:175
  145.6 9.7 %stack.348 = f32[1,2,16,2,256,2]{5,4,3,2,1,0:T(8,128)} reshape(f32[1,2,32,512]{3,2,1,0:T(8,128)S(1)} %get-tuple-element.296) | data formatting | bytes 262144 | tf_op jit(solution)/shard_map/stack | solution.py:175
  155.3 5.2 %copy.505 = f32[1,2,16,2,256,2]{4,2,5,3,1,0:T(8,128)S(1)} copy(f32[1,2,16,2,256,2]{5,4,3,2,1,0:T(8,128)} %stack.348) | data formatting | bytes 262144 | tf_op jit(solution)/shard_map/stack | solution.py:175
  160.5 5.2 %copy.506 = f32[1,2,16,2,256,2]{4,2,5,3,1,0:T(8,128)S(1)} copy(f32[1,2,16,2,256,2]{5,4,3,2,1,0:T(8,128)} %stack.349) | data formatting | bytes 262144 | tf_op jit(solution)/shard_map/stack | solution.py:175
  165.8 9.8 %reshape.428 = f32[2,16,2,256,2]{4,3,2,1,0:T(8,128)} reshape(f32[2,32,512]{2,1,0:T(8,128)S(1)} %broadcast_select_fusion) | data formatting | bytes 262144 | tf_op jit(solution)/shard_map/reshape | solution.py:54
  175.6 4.6 reduce_sum.142
  180.2 6.0 %collective-permute-start.15 = (f32[2,2,1,256]{3,2,1,0:T(1,128)S(1)}, f32[2,2,1,256]{3,2,1,0:T(1,128)S(1)}, u32[]{:S(2)}, u32[]{:S(2)}) collective-permute-start(f32[2,2,1,256]{3,2,1,0:T(1,128)S(1)} %get-tuple-element.342), channel_id=1, source_target_pairs={{0,1},{1,2},{2,3},{3,4},{4,5},{5,6},{6,7},{7,8},{8,9},{9,10},{10,1... | collective-permute-start | bytes 12296 | tf_op jit(solution)/shard_map/ppermute | solution.py:18
  188.3 6.0 %collective-permute-start.11 = (f32[2,2,7,512]{3,1,2,0:T(2,128)S(1)}, f32[2,2,7,512]{3,1,2,0:T(2,128)S(1)}, u32[]{:S(2)}, u32[]{:S(2)}) collective-permute-start(f32[2,2,7,512]{3,1,2,0:T(2,128)S(1)} %copy.493), channel_id=1, source_target_pairs={{0,1},{1,2},{2,3},{3,4},{4,5},{5,6},{6,7},{7,8},{8,9},{9,10},{10,1... | collective-permute-start | bytes 172040 | tf_op jit(solution)/shard_map/ppermute | solution.py:18
  196.6 6.0 %collective-permute-done.12 = f32[2,2,7,512]{3,1,2,0:T(2,128)S(1)} collective-permute-done((f32[2,2,7,512]{3,1,2,0:T(2,128)S(1)}, f32[2,2,7,512]{3,1,2,0:T(2,128)S(1)}, u32[]{:S(2)}, u32[]{:S(2)}) %collective-permute-start.12) | collective-permute-done | bytes 57376 | tf_op jit(solution)/shard_map/ppermute | solution.py:21
  208.7 4.1 collective-permute-start.14
  212.9 3.5 collective-permute-done.14
  216.9 9.8 %stack.345 = f32[2,1,16,2,256,2]{5,4,3,2,0,1:T(8,128)} reshape(f32[2,1,32,512]{3,2,1,0:T(8,128)S(1)} %get-tuple-element.276) | data formatting | bytes 262144 | tf_op jit(solution)/shard_map/stack | solution.py:84
  226.7 5.2 %copy.503 = f32[2,1,16,2,256,2]{4,2,5,3,1,0:T(8,128)S(1)} copy(f32[2,1,16,2,256,2]{5,4,3,2,0,1:T(8,128)} %stack.345) | data formatting | bytes 262144 | tf_op jit(solution)/shard_map/stack | solution.py:84
  231.9 9.8 %stack.346 = f32[2,1,16,2,256,2]{5,4,3,2,0,1:T(8,128)} reshape(f32[2,1,32,512]{3,2,1,0:T(8,128)S(1)} %get-tuple-element.277) | data formatting | bytes 262144 | tf_op jit(solution)/shard_map/stack | solution.py:84
  241.7 5.2 %copy.504 = f32[2,1,16,2,256,2]{4,2,5,3,1,0:T(8,128)S(1)} copy(f32[2,1,16,2,256,2]{5,4,3,2,0,1:T(8,128)} %stack.346) | data formatting | bytes 262144 | tf_op jit(solution)/shard_map/stack | solution.py:84
  249.0 3.9 collective-permute-start.18
  253.0 3.7 collective-permute-done.18
  259.1 4.5 collective-permute-done.19
  265.5 3.9 collective-permute-start.21
  269.5 3.7 collective-permute-done.21
  275.6 3.4 div.63
  282.9 3.9 collective-permute-start.24
  299.4 4.1 collective-permute-start.27
  307.3 3.4 reshape_squeeze.3
  312.9 3.4 reshape.429
  324.1 3.4 div.70
  329.6 25.1 %all-gather = f32[32,8,32]{2,1,0:T(8,128)S(1)} all-gather(f32[4,8,32]{2,1,0:T(8,128)S(1)} %fusion.421), channel_id=2, replica_groups=mesh['tm_0'=8,'tm_1'=2,'space_0'=4,'space_1'=4] {'tm_0'}, dimensions={0}, use_global_device_ids=true | all-gather | bytes 36864 | tf_op jit(solution)/shard_map/all_gather | solution.py:41
  354.7 13.0 %all_gather.13 = f32[32,1,4,8,32]{4,3,2,1,0:T(8,128)S(1)} all-gather(f32[8,1,4,8,32]{4,3,2,1,0:T(8,128)S(1)} %bitcast.180), channel_id=1, replica_groups=mesh['tm_0'=8,'tm_1'=2,'space_0'=4,'space_1'=4] {'space_0'}, dimensions={0}, use_global_device_ids=true | all-gather | bytes 163840 | tf_op jit(solution)/shard_map/all_gather | solution.py:41
  367.7 16.7 %all_gather.14 = f32[128,1,4,8,32]{4,3,2,1,0:T(8,128)} all-gather(f32[32,1,4,8,32]{4,3,2,1,0:T(8,128)S(1)} %all_gather.13), channel_id=1, replica_groups=mesh['tm_0'=8,'tm_1'=2,'space_0'=4,'space_1'=4] {'space_1'}, dimensions={0}, use_global_device_ids=true | all-gather | bytes 655360 | tf_op jit(solution)/shard_map/all_gather | solution.py:41
  384.4 3.4 copy.510
  390.2 3.8 collective-permute-start.29
  394.1 3.9 collective-permute-done.29
  398.0 4.3 all-gather.3.cloned.1.call-done
  402.3 5.4 %copy.511 = f32[256,1,4,8,32]{4,3,2,0,1:T(8,128)} copy(f32[256,1,4,8,32]{0,4,3,2,1:T(8,128)} %all-gather.3.cloned.1.call-done) | data formatting | bytes 2097152 | tf_op jit(solution)/shard_map/all_gather | solution.py:41
  410.3 4.7 copy.513
  415.1 3.7 reshape.431
  422.8 4.2 collective-permute-done.33
  432.9 5.1 collective-permute-done.35
  440.4 4.5 collective-permute-done.36
  446.9 3.9 collective-permute-start.38
  450.8 3.7 collective-permute-done.38
  456.9 4.5 collective-permute-done.39
  463.4 3.9 collective-permute-start.41
  467.3 3.7 collective-permute-done.41
  473.4 4.5 collective-permute-done.42
  479.9 3.9 collective-permute-start.44
  483.8 3.7 collective-permute-done.44
  490.9 5.0 collective-permute-done.45
  498.0 4.2 collective-permute-start.47
  502.2 3.9 collective-permute-done.47
  (432 shorter events, 125.0 us)
Async XLA Ops:
  6.5 395.8 %all-gather.3.cloned.1.call-start = ((), (), s32[]{:S(2)}) async-start(), calls=%async_computation | async-start | bytes 1572864 | tf_op jit(solution)/shard_map/all_gather | solution.py:41
  7.5 50.2 %collective-permute-start = (f32[2,32,512]{2,1,0:T(8,128)S(1)}, f32[2,32,512]{2,1,0:T(8,128)S(1)}, u32[]{:S(2)}, u32[]{:S(2)}) collective-permute-start(f32[2,32,512]{2,1,0:T(8,128)S(1)} %get-tuple-element.232), channel_id=1, source_target_pairs={{0,16},{16,32},{32,48},{48,64},{64,80},{80,96},{96,112},{112,128},... | collective-permute-start | bytes 393224 | tf_op jit(solution)/shard_map/ppermute | solution.py:29
  10.3 47.2 %collective-permute-start.3 = (f32[5,7,512]{2,1,0:T(8,128)S(1)}, f32[5,7,512]{2,1,0:T(8,128)S(1)}, u32[]{:S(2)}, u32[]{:S(2)}) collective-permute-start(f32[5,7,512]{2,1,0:T(8,128)S(1)} %get-tuple-element.289), channel_id=1, source_target_pairs={{0,1},{1,2},{2,3},{3,4},{4,5},{5,6},{6,7},{7,8},{8,9},{9,10},{10,1... | collective-permute-start | bytes 215048 | tf_op jit(solution)/shard_map/ppermute | solution.py:18
  13.8 43.8 %collective-permute-start.4 = (f32[5,7,512]{2,1,0:T(8,128)S(1)}, f32[5,7,512]{2,1,0:T(8,128)S(1)}, u32[]{:S(2)}, u32[]{:S(2)}) collective-permute-start(f32[5,7,512]{2,1,0:T(8,128)S(1)} %get-tuple-element.290), channel_id=1, source_target_pairs={{1,0},{2,1},{3,2},{4,3},{5,4},{6,5},{7,6},{8,7},{9,8},{10,9},{11,1... | collective-permute-start | bytes 215048 | tf_op jit(solution)/shard_map/ppermute | solution.py:21
  17.1 6.4 %copy-start.4 = (f32[32,512]{1,0:T(8,128)S(1)}, f32[32,512]{1,0:T(8,128)}, u32[]{:S(2)}) copy-start(f32[32,512]{1,0:T(8,128)} %param.22) | copy-start | bytes 196612
  23.5 5.5 %copy-start.3 = (f32[32,512]{1,0:T(8,128)S(1)}, f32[32,512]{1,0:T(8,128)}, u32[]{:S(2)}) copy-start(f32[32,512]{1,0:T(8,128)} %param.23) | copy-start | bytes 196612
  29.1 5.6 %copy-start.1 = (f32[2,32,512]{2,1,0:T(8,128)S(1)}, f32[2,32,512]{2,1,0:T(8,128)}, u32[]{:S(2)}) copy-start(f32[2,32,512]{2,1,0:T(8,128)} %param.20) | copy-start | bytes 393220
  52.9 4.7 copy-start
  52.9 4.8 copy-start.2
  57.8 7.8 %collective-permute-start.1 = (f32[2,2,7,512]{3,1,2,0:T(2,128)S(1)}, f32[2,2,7,512]{3,1,2,0:T(2,128)S(1)}, u32[]{:S(2)}, u32[]{:S(2)}) collective-permute-start(f32[2,2,7,512]{3,1,2,0:T(2,128)S(1)} %copy.483), channel_id=1, source_target_pairs={{0,1},{1,2},{2,3},{3,4},{4,5},{5,6},{6,7},{7,8},{8,9},{9,10},{10,1... | collective-permute-start | bytes 172040 | tf_op jit(solution)/shard_map/ppermute | solution.py:18
  63.4 8.2 %collective-permute-start.2 = (f32[2,2,7,512]{3,1,2,0:T(2,128)S(1)}, f32[2,2,7,512]{3,1,2,0:T(2,128)S(1)}, u32[]{:S(2)}, u32[]{:S(2)}) collective-permute-start(f32[2,2,7,512]{3,1,2,0:T(2,128)S(1)} %copy.484), channel_id=1, source_target_pairs={{1,0},{2,1},{3,2},{4,3},{5,4},{6,5},{7,6},{8,7},{9,8},{10,9},{11,1... | collective-permute-start | bytes 172040 | tf_op jit(solution)/shard_map/ppermute | solution.py:21
  75.8 20.3 %collective-permute-start.5 = (f32[2,2,1,512]{3,1,2,0:T(2,128)S(1)}, f32[2,2,1,512]{3,1,2,0:T(2,128)S(1)}, u32[]{:S(2)}, u32[]{:S(2)}) collective-permute-start(f32[2,2,1,512]{3,1,2,0:T(2,128)S(1)} %copy.487), channel_id=1, source_target_pairs={{0,1},{1,2},{2,3},{3,4},{4,5},{5,6},{6,7},{7,8},{8,9},{9,10},{10,1... | collective-permute-start | bytes 24584 | tf_op jit(solution)/shard_map/ppermute | solution.py:18
  77.7 18.4 %collective-permute-start.6 = (f32[2,2,1,512]{3,1,2,0:T(2,128)S(1)}, f32[2,2,1,512]{3,1,2,0:T(2,128)S(1)}, u32[]{:S(2)}, u32[]{:S(2)}) collective-permute-start(f32[2,2,1,512]{3,1,2,0:T(2,128)S(1)} %copy.489), channel_id=1, source_target_pairs={{1,0},{2,1},{3,2},{4,3},{5,4},{6,5},{7,6},{8,7},{9,8},{10,9},{11,1... | collective-permute-start | bytes 24584 | tf_op jit(solution)/shard_map/ppermute | solution.py:21
  122.8 6.4 %collective-permute-start.7 = (f32[2,16,256]{2,1,0:T(8,128)S(1)}, f32[2,16,256]{2,1,0:T(8,128)S(1)}, u32[]{:S(2)}, u32[]{:S(2)}) collective-permute-start(f32[2,16,256]{2,1,0:T(8,128)S(1)} %get-tuple-element.345), channel_id=1, source_target_pairs={{0,16},{16,32},{32,48},{48,64},{64,80},{80,96},{96,112},{112,128},... | collective-permute-start | bytes 98312 | tf_op jit(solution)/shard_map/ppermute | solution.py:29
  124.8 41.0 %collective-permute-start.10 = (f32[2,32,512]{2,1,0:T(8,128)S(1)}, f32[2,32,512]{2,1,0:T(8,128)S(1)}, u32[]{:S(2)}, u32[]{:S(2)}) collective-permute-start(f32[2,32,512]{2,1,0:T(8,128)S(1)} %bitcast.176), channel_id=1, source_target_pairs={{0,16},{16,32},{32,48},{48,64},{64,80},{80,96},{96,112},{112,128},... | collective-permute-start | bytes 393224 | tf_op jit(solution)/shard_map/ppermute | solution.py:29
  129.3 36.4 %collective-permute-start.8 = (f32[2,2,256]{2,1,0:T(2,128)S(1)}, f32[2,2,256]{2,1,0:T(2,128)S(1)}, u32[]{:S(2)}, u32[]{:S(2)}) collective-permute-start(f32[2,2,256]{2,1,0:T(2,128)S(1)} %get-tuple-element.375), channel_id=1, source_target_pairs={{0,1},{1,2},{2,3},{3,4},{4,5},{5,6},{6,7},{7,8},{8,9},{9,10},{10,1... | collective-permute-start | bytes 12296 | tf_op jit(solution)/shard_map/ppermute | solution.py:18
  133.3 32.4 %collective-permute-start.9 = (f32[2,2,256]{2,1,0:T(2,128)S(1)}, f32[2,2,256]{2,1,0:T(2,128)S(1)}, u32[]{:S(2)}, u32[]{:S(2)}) collective-permute-start(f32[2,2,256]{2,1,0:T(2,128)S(1)} %get-tuple-element.376), channel_id=1, source_target_pairs={{1,0},{2,1},{3,2},{4,3},{5,4},{6,5},{7,6},{8,7},{9,8},{10,9},{11,1... | collective-permute-start | bytes 12296 | tf_op jit(solution)/shard_map/ppermute | solution.py:21
  180.2 16.1 %collective-permute-start.15 = (f32[2,2,1,256]{3,2,1,0:T(1,128)S(1)}, f32[2,2,1,256]{3,2,1,0:T(1,128)S(1)}, u32[]{:S(2)}, u32[]{:S(2)}) collective-permute-start(f32[2,2,1,256]{3,2,1,0:T(1,128)S(1)} %get-tuple-element.342), channel_id=1, source_target_pairs={{0,1},{1,2},{2,3},{3,4},{4,5},{5,6},{6,7},{7,8},{8,9},{9,10},{10,1... | collective-permute-start | bytes 12296 | tf_op jit(solution)/shard_map/ppermute | solution.py:18
  186.3 10.0 %collective-permute-start.16 = (f32[2,2,1,256]{3,2,1,0:T(1,128)S(1)}, f32[2,2,1,256]{3,2,1,0:T(1,128)S(1)}, u32[]{:S(2)}, u32[]{:S(2)}) collective-permute-start(f32[2,2,1,256]{3,2,1,0:T(1,128)S(1)} %get-tuple-element.343), channel_id=1, source_target_pairs={{1,0},{2,1},{3,2},{4,3},{5,4},{6,5},{7,6},{8,7},{9,8},{10,9},{11,1... | collective-permute-start | bytes 12296 | tf_op jit(solution)/shard_map/ppermute | solution.py:21
  188.3 8.3 %collective-permute-start.11 = (f32[2,2,7,512]{3,1,2,0:T(2,128)S(1)}, f32[2,2,7,512]{3,1,2,0:T(2,128)S(1)}, u32[]{:S(2)}, u32[]{:S(2)}) collective-permute-start(f32[2,2,7,512]{3,1,2,0:T(2,128)S(1)} %copy.493), channel_id=1, source_target_pairs={{0,1},{1,2},{2,3},{3,4},{4,5},{5,6},{6,7},{7,8},{8,9},{9,10},{10,1... | collective-permute-start | bytes 172040 | tf_op jit(solution)/shard_map/ppermute | solution.py:18
  194.4 8.2 %collective-permute-start.12 = (f32[2,2,7,512]{3,1,2,0:T(2,128)S(1)}, f32[2,2,7,512]{3,1,2,0:T(2,128)S(1)}, u32[]{:S(2)}, u32[]{:S(2)}) collective-permute-start(f32[2,2,7,512]{3,1,2,0:T(2,128)S(1)} %copy.494), channel_id=1, source_target_pairs={{1,0},{2,1},{3,2},{4,3},{5,4},{6,5},{7,6},{8,7},{9,8},{10,9},{11,1... | collective-permute-start | bytes 172040 | tf_op jit(solution)/shard_map/ppermute | solution.py:21
  206.8 6.1 %collective-permute-start.13 = (f32[2,2,1,512]{3,1,2,0:T(2,128)S(1)}, f32[2,2,1,512]{3,1,2,0:T(2,128)S(1)}, u32[]{:S(2)}, u32[]{:S(2)}) collective-permute-start(f32[2,2,1,512]{3,1,2,0:T(2,128)S(1)} %copy.497), channel_id=1, source_target_pairs={{0,1},{1,2},{2,3},{3,4},{4,5},{5,6},{6,7},{7,8},{8,9},{9,10},{10,1... | collective-permute-start | bytes 24584 | tf_op jit(solution)/shard_map/ppermute | solution.py:18
  208.7 7.7 %collective-permute-start.14 = (f32[2,2,1,512]{3,1,2,0:T(2,128)S(1)}, f32[2,2,1,512]{3,1,2,0:T(2,128)S(1)}, u32[]{:S(2)}, u32[]{:S(2)}) collective-permute-start(f32[2,2,1,512]{3,1,2,0:T(2,128)S(1)} %copy.499), channel_id=1, source_target_pairs={{1,0},{2,1},{3,2},{4,3},{5,4},{6,5},{7,6},{8,7},{9,8},{10,9},{11,1... | collective-permute-start | bytes 24584 | tf_op jit(solution)/shard_map/ppermute | solution.py:21
  247.1 6.0 %collective-permute-start.17 = (f32[9,2,256]{2,1,0:T(2,128)S(1)}, f32[9,2,256]{2,1,0:T(2,128)S(1)}, u32[]{:S(2)}, u32[]{:S(2)}) collective-permute-start(f32[9,2,256]{2,1,0:T(2,128)S(1)} %get-tuple-element.300), channel_id=1, source_target_pairs={{0,1},{1,2},{2,3},{3,4},{4,5},{5,6},{6,7},{7,8},{8,9},{9,10},{10,1... | collective-permute-start | bytes 55304 | tf_op jit(solution)/shard_map/ppermute | solution.py:18
  249.0 7.8 %collective-permute-start.18 = (f32[9,2,256]{2,1,0:T(2,128)S(1)}, f32[9,2,256]{2,1,0:T(2,128)S(1)}, u32[]{:S(2)}, u32[]{:S(2)}) collective-permute-start(f32[9,2,256]{2,1,0:T(2,128)S(1)} %get-tuple-element.301), channel_id=1, source_target_pairs={{1,0},{2,1},{3,2},{4,3},{5,4},{6,5},{7,6},{8,7},{9,8},{10,9},{11,1... | collective-permute-start | bytes 55304 | tf_op jit(solution)/shard_map/ppermute | solution.py:21
  257.1 6.4 %collective-permute-start.19 = (f32[2,16,256]{2,1,0:T(8,128)S(1)}, f32[2,16,256]{2,1,0:T(8,128)S(1)}, u32[]{:S(2)}, u32[]{:S(2)}) collective-permute-start(f32[2,16,256]{2,1,0:T(8,128)S(1)} %slice_bitcast_fusion.18), channel_id=1, source_target_pairs={{0,16},{16,32},{32,48},{48,64},{64,80},{80,96},{96,112},{112,128},... | collective-permute-start | bytes 98312 | tf_op jit(solution)/shard_map/ppermute | solution.py:29
  263.6 5.9 %collective-permute-start.20 = (f32[2,2,256]{2,1,0:T(2,128)S(1)}, f32[2,2,256]{2,1,0:T(2,128)S(1)}, u32[]{:S(2)}, u32[]{:S(2)}) collective-permute-start(f32[2,2,256]{2,1,0:T(2,128)S(1)} %get-tuple-element.371), channel_id=1, source_target_pairs={{0,1},{1,2},{2,3},{3,4},{4,5},{5,6},{6,7},{7,8},{8,9},{9,10},{10,1... | collective-permute-start | bytes 12296 | tf_op jit(solution)/shard_map/ppermute | solution.py:18
  265.5 7.6 %collective-permute-start.21 = (f32[2,2,256]{2,1,0:T(2,128)S(1)}, f32[2,2,256]{2,1,0:T(2,128)S(1)}, u32[]{:S(2)}, u32[]{:S(2)}) collective-permute-start(f32[2,2,256]{2,1,0:T(2,128)S(1)} %get-tuple-element.372), channel_id=1, source_target_pairs={{1,0},{2,1},{3,2},{4,3},{5,4},{6,5},{7,6},{8,7},{9,8},{10,9},{11,1... | collective-permute-start | bytes 12296 | tf_op jit(solution)/shard_map/ppermute | solution.py:21
  273.6 7.3 %collective-permute-start.22 = (f32[2,16,256]{2,1,0:T(8,128)S(1)}, f32[2,16,256]{2,1,0:T(8,128)S(1)}, u32[]{:S(2)}, u32[]{:S(2)}) collective-permute-start(f32[2,16,256]{2,1,0:T(8,128)S(1)} %slice_bitcast_fusion.16), channel_id=1, source_target_pairs={{0,16},{16,32},{32,48},{48,64},{64,80},{80,96},{96,112},{112,128},... | collective-permute-start | bytes 98312 | tf_op jit(solution)/shard_map/ppermute | solution.py:29
  281.0 7.1 %collective-permute-start.23 = (f32[2,2,256]{2,1,0:T(2,128)S(1)}, f32[2,2,256]{2,1,0:T(2,128)S(1)}, u32[]{:S(2)}, u32[]{:S(2)}) collective-permute-start(f32[2,2,256]{2,1,0:T(2,128)S(1)} %get-tuple-element.369), channel_id=1, source_target_pairs={{0,1},{1,2},{2,3},{3,4},{4,5},{5,6},{6,7},{7,8},{8,9},{9,10},{10,1... | collective-permute-start | bytes 12296 | tf_op jit(solution)/shard_map/ppermute | solution.py:18
  282.9 7.6 %collective-permute-start.24 = (f32[2,2,256]{2,1,0:T(2,128)S(1)}, f32[2,2,256]{2,1,0:T(2,128)S(1)}, u32[]{:S(2)}, u32[]{:S(2)}) collective-permute-start(f32[2,2,256]{2,1,0:T(2,128)S(1)} %get-tuple-element.370), channel_id=1, source_target_pairs={{1,0},{2,1},{3,2},{4,3},{5,4},{6,5},{7,6},{8,7},{9,8},{10,9},{11,1... | collective-permute-start | bytes 12296 | tf_op jit(solution)/shard_map/ppermute | solution.py:21
  291.0 6.4 %collective-permute-start.25 = (f32[2,16,256]{2,1,0:T(8,128)S(1)}, f32[2,16,256]{2,1,0:T(8,128)S(1)}, u32[]{:S(2)}, u32[]{:S(2)}) collective-permute-start(f32[2,16,256]{2,1,0:T(8,128)S(1)} %get-tuple-element.340), channel_id=1, source_target_pairs={{0,16},{16,32},{32,48},{48,64},{64,80},{80,96},{96,112},{112,128},... | collective-permute-start | bytes 98312 | tf_op jit(solution)/shard_map/ppermute | solution.py:29
  297.5 7.3 %collective-permute-start.26 = (f32[2,2,256]{2,1,0:T(2,128)S(1)}, f32[2,2,256]{2,1,0:T(2,128)S(1)}, u32[]{:S(2)}, u32[]{:S(2)}) collective-permute-start(f32[2,2,256]{2,1,0:T(2,128)S(1)} %get-tuple-element.367), channel_id=1, source_target_pairs={{0,1},{1,2},{2,3},{3,4},{4,5},{5,6},{6,7},{7,8},{8,9},{9,10},{10,1... | collective-permute-start | bytes 12296 | tf_op jit(solution)/shard_map/ppermute | solution.py:18
  299.4 7.6 %collective-permute-start.27 = (f32[2,2,256]{2,1,0:T(2,128)S(1)}, f32[2,2,256]{2,1,0:T(2,128)S(1)}, u32[]{:S(2)}, u32[]{:S(2)}) collective-permute-start(f32[2,2,256]{2,1,0:T(2,128)S(1)} %get-tuple-element.368), channel_id=1, source_target_pairs={{1,0},{2,1},{3,2},{4,3},{5,4},{6,5},{7,6},{8,7},{9,8},{10,9},{11,1... | collective-permute-start | bytes 12296 | tf_op jit(solution)/shard_map/ppermute | solution.py:21
  318.3 11.1 %collective-permute-start.30 = (f32[4,8,32]{2,1,0:T(8,128)S(1)}, f32[4,8,32]{2,1,0:T(8,128)S(1)}, u32[]{:S(2)}, u32[]{:S(2)}) collective-permute-start(f32[4,8,32]{2,1,0:T(8,128)S(1)} %get-tuple-element.387), channel_id=1, source_target_pairs={{48,0},{64,16},{80,32},{96,48},{112,64},{128,80},{144,96},{160,112... | collective-permute-start | bytes 12296 | tf_op jit(solution)/shard_map/ppermute | solution.py:29
  320.3 9.2 %collective-permute-start.31 = (f32[4,8,32]{2,1,0:T(8,128)S(1)}, f32[4,8,32]{2,1,0:T(8,128)S(1)}, u32[]{:S(2)}, u32[]{:S(2)}) collective-permute-start(f32[4,8,32]{2,1,0:T(8,128)S(1)} %get-tuple-element.386), channel_id=1, source_target_pairs={{32,0},{48,16},{64,32},{80,48},{96,64},{112,80},{128,96},{144,112}... | collective-permute-start | bytes 12296 | tf_op jit(solution)/shard_map/ppermute | solution.py:29
  322.2 7.3 %collective-permute-start.32 = (f32[4,8,32]{2,1,0:T(8,128)S(1)}, f32[4,8,32]{2,1,0:T(8,128)S(1)}, u32[]{:S(2)}, u32[]{:S(2)}) collective-permute-start(f32[4,8,32]{2,1,0:T(8,128)S(1)} %get-tuple-element.385), channel_id=1, source_target_pairs={{16,0},{32,16},{48,32},{64,48},{80,64},{96,80},{112,96},{128,112},... | collective-permute-start | bytes 12296 | tf_op jit(solution)/shard_map/ppermute | solution.py:29
  387.9 6.2 %collective-permute-start.28 = (f32[7,4,128]{2,1,0:T(4,128)S(1)}, f32[7,4,128]{2,1,0:T(4,128)S(1)}, u32[]{:S(2)}, u32[]{:S(2)}) collective-permute-start(f32[7,4,128]{2,1,0:T(4,128)S(1)} %get-tuple-element.377), channel_id=1, source_target_pairs={{0,1},{1,2},{2,3},{3,4},{4,5},{5,6},{6,7},{7,8},{8,9},{9,10},{10,1... | collective-permute-start | bytes 43016 | tf_op jit(solution)/shard_map/ppermute | solution.py:18
  390.2 7.7 %collective-permute-start.29 = (f32[7,4,128]{2,1,0:T(4,128)S(1)}, f32[7,4,128]{2,1,0:T(4,128)S(1)}, u32[]{:S(2)}, u32[]{:S(2)}) collective-permute-start(f32[7,4,128]{2,1,0:T(4,128)S(1)} %get-tuple-element.378), channel_id=1, source_target_pairs={{1,0},{2,1},{3,2},{4,3},{5,4},{6,5},{7,6},{8,7},{9,8},{10,9},{11,1... | collective-permute-start | bytes 43016 | tf_op jit(solution)/shard_map/ppermute | solution.py:21
  420.5 6.4 %collective-permute-start.33 = (f32[2,16,256]{2,1,0:T(8,128)S(1)}, f32[2,16,256]{2,1,0:T(8,128)S(1)}, u32[]{:S(2)}, u32[]{:S(2)}) collective-permute-start(f32[2,16,256]{2,1,0:T(8,128)S(1)} %add_select_fusion.1), channel_id=1, source_target_pairs={{0,16},{16,32},{32,48},{48,64},{64,80},{80,96},{96,112},{112,128},... | collective-permute-start | bytes 98312 | tf_op jit(solution)/shard_map/ppermute | solution.py:29
  427.0 5.9 %collective-permute-start.34 = (f32[2,2,256]{2,1,0:T(2,128)S(1)}, f32[2,2,256]{2,1,0:T(2,128)S(1)}, u32[]{:S(2)}, u32[]{:S(2)}) collective-permute-start(f32[2,2,256]{2,1,0:T(2,128)S(1)} %get-tuple-element.360), channel_id=1, source_target_pairs={{0,1},{1,2},{2,3},{3,4},{4,5},{5,6},{6,7},{7,8},{8,9},{9,10},{10,1... | collective-permute-start | bytes 12296 | tf_op jit(solution)/shard_map/ppermute | solution.py:18
  430.4 7.6 %collective-permute-start.35 = (f32[2,2,256]{2,1,0:T(2,128)S(1)}, f32[2,2,256]{2,1,0:T(2,128)S(1)}, u32[]{:S(2)}, u32[]{:S(2)}) collective-permute-start(f32[2,2,256]{2,1,0:T(2,128)S(1)} %get-tuple-element.361), channel_id=1, source_target_pairs={{1,0},{2,1},{3,2},{4,3},{5,4},{6,5},{7,6},{8,7},{9,8},{10,9},{11,1... | collective-permute-start | bytes 12296 | tf_op jit(solution)/shard_map/ppermute | solution.py:21
  438.5 6.4 %collective-permute-start.36 = (f32[2,16,256]{2,1,0:T(8,128)S(1)}, f32[2,16,256]{2,1,0:T(8,128)S(1)}, u32[]{:S(2)}, u32[]{:S(2)}) collective-permute-start(f32[2,16,256]{2,1,0:T(8,128)S(1)} %slice_bitcast_fusion.12), channel_id=1, source_target_pairs={{0,16},{16,32},{32,48},{48,64},{64,80},{80,96},{96,112},{112,128},... | collective-permute-start | bytes 98312 | tf_op jit(solution)/shard_map/ppermute | solution.py:29
  444.9 5.9 %collective-permute-start.37 = (f32[2,2,256]{2,1,0:T(2,128)S(1)}, f32[2,2,256]{2,1,0:T(2,128)S(1)}, u32[]{:S(2)}, u32[]{:S(2)}) collective-permute-start(f32[2,2,256]{2,1,0:T(2,128)S(1)} %get-tuple-element.358), channel_id=1, source_target_pairs={{0,1},{1,2},{2,3},{3,4},{4,5},{5,6},{6,7},{7,8},{8,9},{9,10},{10,1... | collective-permute-start | bytes 12296 | tf_op jit(solution)/shard_map/ppermute | solution.py:18
  446.9 7.6 %collective-permute-start.38 = (f32[2,2,256]{2,1,0:T(2,128)S(1)}, f32[2,2,256]{2,1,0:T(2,128)S(1)}, u32[]{:S(2)}, u32[]{:S(2)}) collective-permute-start(f32[2,2,256]{2,1,0:T(2,128)S(1)} %get-tuple-element.359), channel_id=1, source_target_pairs={{1,0},{2,1},{3,2},{4,3},{5,4},{6,5},{7,6},{8,7},{9,8},{10,9},{11,1... | collective-permute-start | bytes 12296 | tf_op jit(solution)/shard_map/ppermute | solution.py:21
  455.0 6.4 %collective-permute-start.39 = (f32[2,16,256]{2,1,0:T(8,128)S(1)}, f32[2,16,256]{2,1,0:T(8,128)S(1)}, u32[]{:S(2)}, u32[]{:S(2)}) collective-permute-start(f32[2,16,256]{2,1,0:T(8,128)S(1)} %slice_bitcast_fusion.10), channel_id=1, source_target_pairs={{0,16},{16,32},{32,48},{48,64},{64,80},{80,96},{96,112},{112,128},... | collective-permute-start | bytes 98312 | tf_op jit(solution)/shard_map/ppermute | solution.py:29
  461.5 5.9 %collective-permute-start.40 = (f32[2,2,256]{2,1,0:T(2,128)S(1)}, f32[2,2,256]{2,1,0:T(2,128)S(1)}, u32[]{:S(2)}, u32[]{:S(2)}) collective-permute-start(f32[2,2,256]{2,1,0:T(2,128)S(1)} %get-tuple-element.356), channel_id=1, source_target_pairs={{0,1},{1,2},{2,3},{3,4},{4,5},{5,6},{6,7},{7,8},{8,9},{9,10},{10,1... | collective-permute-start | bytes 12296 | tf_op jit(solution)/shard_map/ppermute | solution.py:18
  463.4 7.6 %collective-permute-start.41 = (f32[2,2,256]{2,1,0:T(2,128)S(1)}, f32[2,2,256]{2,1,0:T(2,128)S(1)}, u32[]{:S(2)}, u32[]{:S(2)}) collective-permute-start(f32[2,2,256]{2,1,0:T(2,128)S(1)} %get-tuple-element.357), channel_id=1, source_target_pairs={{1,0},{2,1},{3,2},{4,3},{5,4},{6,5},{7,6},{8,7},{9,8},{10,9},{11,1... | collective-permute-start | bytes 12296 | tf_op jit(solution)/shard_map/ppermute | solution.py:21
  471.5 6.4 %collective-permute-start.42 = (f32[2,16,256]{2,1,0:T(8,128)S(1)}, f32[2,16,256]{2,1,0:T(8,128)S(1)}, u32[]{:S(2)}, u32[]{:S(2)}) collective-permute-start(f32[2,16,256]{2,1,0:T(8,128)S(1)} %get-tuple-element.338), channel_id=1, source_target_pairs={{0,16},{16,32},{32,48},{48,64},{64,80},{80,96},{96,112},{112,128},... | collective-permute-start | bytes 98312 | tf_op jit(solution)/shard_map/ppermute | solution.py:29
  478.0 5.9 %collective-permute-start.43 = (f32[2,2,256]{2,1,0:T(2,128)S(1)}, f32[2,2,256]{2,1,0:T(2,128)S(1)}, u32[]{:S(2)}, u32[]{:S(2)}) collective-permute-start(f32[2,2,256]{2,1,0:T(2,128)S(1)} %get-tuple-element.354), channel_id=1, source_target_pairs={{0,1},{1,2},{2,3},{3,4},{4,5},{5,6},{6,7},{7,8},{8,9},{9,10},{10,1... | collective-permute-start | bytes 12296 | tf_op jit(solution)/shard_map/ppermute | solution.py:18
  479.9 7.6 %collective-permute-start.44 = (f32[2,2,256]{2,1,0:T(2,128)S(1)}, f32[2,2,256]{2,1,0:T(2,128)S(1)}, u32[]{:S(2)}, u32[]{:S(2)}) collective-permute-start(f32[2,2,256]{2,1,0:T(2,128)S(1)} %get-tuple-element.355), channel_id=1, source_target_pairs={{1,0},{2,1},{3,2},{4,3},{5,4},{6,5},{7,6},{8,7},{9,8},{10,9},{11,1... | collective-permute-start | bytes 12296 | tf_op jit(solution)/shard_map/ppermute | solution.py:21
  488.4 7.5 %collective-permute-start.45 = (f32[2,32,512]{2,1,0:T(8,128)S(1)}, f32[2,32,512]{2,1,0:T(8,128)S(1)}, u32[]{:S(2)}, u32[]{:S(2)}) collective-permute-start(f32[2,32,512]{2,1,0:T(8,128)S(1)} %bitcast.179), channel_id=1, source_target_pairs={{0,16},{16,32},{32,48},{48,64},{64,80},{80,96},{96,112},{112,128},... | collective-permute-start | bytes 393224 | tf_op jit(solution)/shard_map/ppermute | solution.py:29
  496.0 6.2 %collective-permute-start.46 = (f32[2,2,7,512]{3,1,2,0:T(2,128)S(1)}, f32[2,2,7,512]{3,1,2,0:T(2,128)S(1)}, u32[]{:S(2)}, u32[]{:S(2)}) collective-permute-start(f32[2,2,7,512]{3,1,2,0:T(2,128)S(1)} %copy.523), channel_id=1, source_target_pairs={{0,1},{1,2},{2,3},{3,4},{4,5},{5,6},{6,7},{7,8},{8,9},{9,10},{10,1... | collective-permute-start | bytes 172040 | tf_op jit(solution)/shard_map/ppermute | solution.py:18
  498.0 8.2 %collective-permute-start.47 = (f32[2,2,7,512]{3,1,2,0:T(2,128)S(1)}, f32[2,2,7,512]{3,1,2,0:T(2,128)S(1)}, u32[]{:S(2)}, u32[]{:S(2)}) collective-permute-start(f32[2,2,7,512]{3,1,2,0:T(2,128)S(1)} %copy.524), channel_id=1, source_target_pairs={{1,0},{2,1},{3,2},{4,3},{5,4},{6,5},{7,6},{8,7},{9,8},{10,9},{11,1... | collective-permute-start | bytes 172040 | tf_op jit(solution)/shard_map/ppermute | solution.py:21
  510.6 1.3 copy-start.5
Sparse Core Ops, SparseCore 0:
  388.0 14.2 all-gather.2
where the time goes:
time: 528 us; the launch traced here: 520 us
  local copies, waits for them, and re-layouts  169 us (32%)
  starting transfers between devices  135 us (26%)
  waiting for transfers between devices  87.7 us (17%)
  other arithmetic  56.9 us (11%)
  blocking collectives  54.8 us (10%)
  between operations  16.5 us (3%)
    reshape x8, local copies, waits for them, and re-layouts, coarsen(): blocks = field.reshape(shape[:-2] + (shape[-2] // 2, 2, shape[-1] // 2, 2))  68.5 us
    ppermute x17, starting transfers between devices, padded_2(): lax.ppermute(lax.slice_in_dim(block, 0, width, axis=dim), axis, backward)  56.9 us
    all_gather x3, blocking collectives, gather_in_order(): parts = lax.all_gather(parts, axes[k], axis=0, tiled=True)  54.8 us
    ppermute x17, waiting for transfers between devices, padded_2(): lax.ppermute(lax.slice_in_dim(block, 0, width, axis=dim), axis, backward)  51.3 us
    ppermute x17, starting transfers between devices, padded_2(): lax.ppermute(lax.slice_in_dim(block, block.shape[dim] - width, None, axis...  49.9 us
    reduce_sum x15, other arithmetic, coarsen(): return blocks.mean(axis=(-3, -1))  38.5 us
    ppermute x14, waiting for transfers between devices, shifted(): return lax.ppermute(block, axis, route)  32 us
    another operation x4, local copies, waits for them, and re-layouts, advance(): return jnp.stack([next_first, next_second], axis=-3)  30.1 us
  transfers between devices with their start and end apart: 49, of which 22 were waited for; matrix products, arithmetic and copies ran while one was open for 20% of the time, Pallas kernels for 0%

commit v1 on v0

v1 whole, which is shorter than its diff:
```python
import jax
import jax.numpy as jnp
from jax import lax
from jax.experimental import pallas as pl
from jax.experimental.pallas import tpu as pltpu
from jax.sharding import Mesh
from jax.sharding import PartitionSpec as P

F32 = jnp.float32
AXES = ("k", "m", "space")
VMEM = pl.BlockSpec(memory_space=pltpu.VMEM)
SMEM = pl.BlockSpec(memory_space=pltpu.SMEM)
N_TM = 16
N_SPACE = 16
GROUP = 4
STRIP = 32


def exact_dot(x, matrix):
    high = x.astype(jnp.bfloat16)
    rest = x - high.astype(F32)
    middle = rest.astype(jnp.bfloat16)
    low = (rest - middle.astype(F32)).astype(jnp.bfloat16)

    def part(piece):
        return lax.dot_general(
            piece, matrix, (((1,), (0,)), ((), ())), preferred_element_type=F32
        )

    return part(low) + part(middle) + part(high)


def down_matrix(fine):
    rows = lax.broadcasted_iota(jnp.int32, (fine, fine // 2), 0)
    cols = lax.broadcasted_iota(jnp.int32, (fine, fine // 2), 1)
    inside = (rows == 2 * cols) | (rows == 2 * cols + 1)
    return jnp.where(inside, F32(0.25), F32(0.0)).astype(jnp.bfloat16)


def up_matrix(fine):
    rows = lax.broadcasted_iota(jnp.int32, (fine // 2, fine), 0)
    cols = lax.broadcasted_iota(jnp.int32, (fine // 2, fine), 1)
    inside = (cols == 2 * rows) | (cols == 2 * rows + 1)
    return jnp.where(inside, F32(1.0), F32(0.0)).astype(jnp.bfloat16)


def split_tiles(x):
    return [x[:, 128 * k : 128 * k + 128] for k in range(x.shape[1] // 128)]


def side_sums(tiles, lane_first, lane_last):
    right_going = [pltpu.roll(t, 1, 1) for t in tiles]
    left_going = [pltpu.roll(t, 127, 1) for t in tiles]
    zero = jnp.zeros_like(tiles[0])
    out = []
    for k in range(len(tiles)):
        before = right_going[k - 1] if k > 0 else zero
        after = left_going[k + 1] if k < len(tiles) - 1 else zero
        out.append(
            jnp.where(lane_first, before, right_going[k])
            + jnp.where(lane_last, after, left_going[k])
        )
    return out


def advance(load, store, coeffs, blocks, force=None):
    sub = lax.broadcasted_iota(jnp.int32, (8, 128), 0)
    lane = lax.broadcasted_iota(jnp.int32, (8, 128), 1)
    first_row, last_row = sub == 0, sub == 7
    first_lane, last_lane = lane == 0, lane == 127
    held = {}

    def fetch(i):
        if i not in held:
            species = []
            for x in load(i):
                tiles = split_tiles(x)
                species.append(
                    (
                        tiles,
                        [pltpu.roll(t, 1, 0) for t in tiles],
                        [pltpu.roll(t, 7, 0) for t in tiles],
                    )
                )
            held[i] = species
        return held[i]

    low, high = blocks
    for i in range(low, high):
        here = fetch(i)
        above = fetch(max(i - 1, low))
        below = fetch(min(i + 1, high - 1))
        held.pop(i - 2, None)
        c = coeffs(i)
        sums = []
        for q in range(2):
            tiles, down, up = here[q]
            sides = side_sums(tiles, first_lane, last_lane)
            sums.append(
                [
                    jnp.where(first_row, above[q][1][k], down[k])
                    + jnp.where(last_row, below[q][2][k], up[k])
                    + sides[k]
                    for k in range(len(tiles))
                ]
            )
        next_a, next_b = [], []
        spread_a, spread_b, supply, keep_a, keep_b, coupling = [split_tiles(x) for x in c]
        for k in range(len(sums[0])):
            a, b = here[0][0][k], here[1][0][k]
            coupled = coupling[k] * a * b * b
            next_a.append(keep_a[k] * a + spread_a[k] * sums[0][k] + (supply[k] - coupled))
            next_b.append(keep_b[k] * b + spread_b[k] * sums[1][k] + coupled)
        out = [jnp.concatenate(next_a, axis=1), jnp.concatenate(next_b, axis=1)]
        if force is not None:
            extra = force(i)
            out = [out[0] + extra[0], out[1] + extra[1]]
        store(i, out)


def derived(spread_a, spread_b, supply, removal, coupling):
    return (
        spread_a,
        spread_b,
        supply,
        1.0 - supply - 4.0 * spread_a,
        1.0 - supply - removal - 4.0 * spread_b,
        coupling,
    )


def block(i):
    return slice(8 * i, 8 * i + 8)


class Rows:
    def __init__(self, ref):
        self.ref, self.used = ref, 0

    def coarsen(self, x):
        count = x.shape[0]
        parts = []
        for tile in split_tiles(x):
            n = self.used
            self.used += 1
            self.ref[n, 0:count] = tile
            even = self.ref[n, pl.ds(0, count // 2, stride=2)]
            parts.append(even + self.ref[n, pl.ds(1, count // 2, stride=2)])
        return jnp.concatenate(parts, axis=1)

    def repeat(self, x):
        count = x.shape[0]
        parts = []
        for tile in split_tiles(x):
            n = self.used
            self.used += 1
            self.ref[n, pl.ds(0, count, stride=2)] = tile
            self.ref[n, pl.ds(1, count, stride=2)] = tile
            parts.append(self.ref[n, 0 : 2 * count])
        return jnp.concatenate(parts, axis=1)


def fine_kernel(
    where_ref, shift_ref, dlo_ref, dhi_ref, nlo_ref, nhi_ref, own_ref, coef_ref,
    a01_ref, a2_ref, w01_ref, w2_ref, send_ref, fine_ref,
    s0, s1, raw, tall, mid_state, mid_coef, cells,
):
    rows = Rows(cells)
    opening = where_ref[0] == 0
    for c in range(2):
        for q in range(2):
            s0[c, q, 0:16] = dlo_ref[2 * c + q]
            s0[c, q, 16:48] = shift_ref[2 * c + q]
            s0[c, q, 48:64] = dhi_ref[2 * c + q]
    for q in range(2):
        s0[2, q, 0:16] = nlo_ref[5 + q]
        s0[2, q, 16:48] = own_ref[q]
        s0[2, q, 48:64] = nhi_ref[5 + q]
    for f in range(5):
        raw[f, 0:16] = nlo_ref[f]
        raw[f, 16:48] = coef_ref[f]
        raw[f, 48:64] = nhi_ref[f]
    for i in range(8):
        r = block(i)
        parts = derived(*[raw[f, r] for f in range(5)])
        for n in range(6):
            tall[n, r] = parts[n]
        if 1 <= i < 7:
            for n in range(6):
                fine_ref[n, block(i - 1)] = parts[n]

    def coeffs(i):
        return [tall[n, block(i)] for n in range(6)]

    def run(source, target, chain, blocks):
        def load(i):
            return [source[chain, q, block(i)] for q in range(2)]

        def store(i, values):
            for q in range(2):
                target[chain, q, block(i)] = values[q]

        advance(load, store, coeffs, blocks)

    def first_pair(n, carry):
        for source, target in ((s0, s1), (s1, s0)):
            run(source, target, 0, (0, 8))
            run(source, target, 1, (0, 8))
            run(source, target, 2, (1, 7))
        return carry

    lax.fori_loop(0, 4, first_pair, 0)

    for q in range(2):
        s0[0, q, 0:16] = jnp.where(opening, dlo_ref[q], s0[0, q, 0:16])
        s0[0, q, 16:48] = jnp.where(opening, shift_ref[q], s0[0, q, 16:48])
        s0[0, q, 48:64] = jnp.where(opening, dhi_ref[q], s0[0, q, 48:64])
    for q in range(2):
        for c in range(2):
            a01_ref[c, q] = s0[c, q, 8:56]
        a2_ref[q] = s0[2, q, 16:48]

    down = down_matrix(512)
    stacked = jnp.concatenate([rows.coarsen(raw[f]) for f in range(5)], axis=0)
    coarse = exact_dot(stacked, down)
    for f in range(5):
        send_ref[6 + f] = coarse[32 * f + 8 : 32 * f + 24]
    for i in range(4):
        at = [coarse[32 * f + 8 * i : 32 * f + 8 * i + 8] for f in range(5)]
        parts = derived(2.0 * at[0], 2.0 * at[1], 8.0 * at[2], 8.0 * at[3], 8.0 * at[4])
        for n in range(6):
            mid_coef[n, block(i)] = parts[n]
    stacked = jnp.concatenate(
        [rows.coarsen(s0[c, q]) for c in range(2) for q in range(2)]
        + [rows.coarsen(s0[2, q, 16:48]) for q in range(2)],
        axis=0,
    )
    coarse = exact_dot(stacked, down)
    for c in range(2):
        for q in range(2):
            mid_state[c, q] = coarse[32 * (2 * c + q) : 32 * (2 * c + q) + 32]
    for q in range(2):
        w2_ref[q] = coarse[128 + 16 * q : 144 + 16 * q]
    for c in range(2):
        for q in range(2):
            w01_ref[c, q] = mid_state[c, q, 4:28]
    for q in range(2):
        send_ref[4 + q] = mid_state[0, q, 8:24]

    def second_pair(n, carry):
        for source, target in ((s0, s1), (s1, s0)):
            run(source, target, 0, (1, 7))
            run(source, target, 1, (1, 7))
        return carry

    lax.fori_loop(0, 4, second_pair, 0)

    for q in range(2):
        s0[0, q, 16:48] = s0[0, q, 16:48] - a01_ref[1, q, 8:40]
        s0[1, q, 16:48] = s0[1, q, 16:48] - a2_ref[q]
    stacked = jnp.concatenate(
        [rows.coarsen(s0[c, q, 16:48]) for c in range(2) for q in range(2)], axis=0
    )
    coarse = exact_dot(stacked, down)
    for c in range(2):
        for q in range(2):
            at = coarse[16 * (2 * c + q) : 16 * (2 * c + q) + 16]
            end = mid_state[1, q, 8:24] if c == 0 else w2_ref[q]
            send_ref[2 * c + q] = at + end

    for c in range(2):

        def load(i):
            return [mid_state[c, q, block(i)] for q in range(2)]

        def store(i, values):
            if 1 <= i < 3:
                for q in range(2):
                    send_ref[2 * c + q, block(i - 1)] = (
                        send_ref[2 * c + q, block(i - 1)] - values[q]
                    )

        advance(load, store, lambda i: [mid_coef[n, block(i)] for n in range(6)], (0, 4))


def wide_mid_coefs(raw, coef_ref, lo_ref, hi_ref, mid_coef):
    for f in range(5):
        raw[f, 0:16] = lo_ref[6 + f]
        raw[f, 16:32] = coef_ref[6 + f]
        raw[f, 32:48] = hi_ref[6 + f]
    at = [raw[f, 4:44] for f in range(5)]
    parts = derived(2.0 * at[0], 2.0 * at[1], 8.0 * at[2], 8.0 * at[3], 8.0 * at[4])
    for n in range(6):
        mid_coef[n] = parts[n]


def mid_kernel(
    gathered_ref, own_ref, lo_ref, hi_ref, out_ref, coef_out_ref, raw, state, cells,
):
    rows = Rows(cells)
    wide_mid_coefs(raw, own_ref, lo_ref, hi_ref, coef_out_ref)

    def coeffs(i):
        return [coef_out_ref[n, block(i)] for n in range(6)]

    for step in range(8):
        holder, place = step // 2, step % 2

        def load(i):
            if step == 0:
                return [gathered_ref[0, 4 + q, block(i)] for q in range(2)]
            return [state[(step + 1) % 2, q, block(i)] for q in range(2)]

        def force(i):
            return [gathered_ref[holder, 2 * place + q, block(i)] for q in range(2)]

        def store(i, values):
            for q in range(2):
                state[step % 2, q, block(i)] = values[q]

        advance(load, store, coeffs, (0, 5), force)
    stacked = jnp.concatenate(
        [rows.coarsen(state[1, q, 12:28]) for q in range(2)]
        + [rows.coarsen(gathered_ref[0, 4 + q, 12:28]) for q in range(2)],
        axis=0,
    )
    coarse = exact_dot(stacked, down_matrix(256))
    for f in range(4):
        out_ref[f] = coarse[8 * f : 8 * f + 8]


def final_kernel(
    where_ref, gathered_ref, top_ref, pred_ref, mid_coef, own_ref, lo_ref, hi_ref,
    a01_ref, a2_ref, w01_ref, w2_ref, fine_ref,
    out_ref,
    raw, low_coef, yz, series, cells, fine,
):
    rows = Rows(cells)
    k, m = where_ref[1], where_ref[2]
    for f in range(5):
        raw[f, 0:16] = lo_ref[6 + f]
        raw[f, 16:32] = own_ref[6 + f]
        raw[f, 32:48] = hi_ref[6 + f]
    down = down_matrix(256)
    up_low = up_matrix(256)
    stacked = jnp.concatenate([rows.coarsen(raw[f]) for f in range(5)], axis=0)
    coarse = exact_dot(stacked, down)
    at = [coarse[24 * f : 24 * f + 24] for f in range(5)]
    parts = derived(4.0 * at[0], 4.0 * at[1], 64.0 * at[2], 64.0 * at[3], 64.0 * at[4])
    for n in range(6):
        low_coef[n] = parts[n]

    def low_step(slot, target):
        def load(i):
            return [yz[slot, q, block(i)] for q in range(2)]

        def store(i, values):
            for q in range(2):
                yz[target, q, block(i)] = values[q]

        advance(load, store, lambda i: [low_coef[n, block(i)] for n in range(6)], (0, 3))

    for q in range(2):
        yz[0, q] = jnp.zeros((24, 128), F32)
    for back in (2, 1, 0):
        behind = k - 1 - back
        follows = jnp.where(behind > 0, F32(1.0), F32(0.0))
        for q in range(2):
            for piece in range(3):
                yz[1, q, block(piece)] = top_ref[back, piece, 2 + q]
        low_step(0, 2)
        low_step(1, 3)
        for q in range(2):
            for piece in range(3):
                r = block(piece)
                yz[0, q, r] = top_ref[back, piece, q] + follows * (yz[2, q, r] - yz[3, q, r])
    stacked = jnp.concatenate(
        [rows.coarsen(gathered_ref[0, 4 + q]) for q in range(2)]
        + [rows.coarsen(w2_ref[q]) for q in range(2)]
        + [jnp.zeros((8, 256), F32)],
        axis=0,
    )
    coarse = exact_dot(stacked, down)
    inner = jnp.where(k > 0, F32(1.0), F32(0.0))
    fixes = []
    for q in range(2):
        z = coarse[20 * q : 20 * q + 20]
        yz[1, q] = jnp.zeros((24, 128), F32)
        yz[1, q, 2:22] = z
        fixes.append(inner * (yz[0, q, 2:22] - z))
    low_step(0, 2)
    low_step(1, 3)
    for q in range(2):
        r = block(1)
        end = pred_ref[q] + inner * (yz[2, q, r] - yz[3, q, r])
        fixes.append(end - coarse[40 + 8 * q : 48 + 8 * q])
    fixes.append(jnp.zeros((8, 128), F32))
    refined = exact_dot(jnp.concatenate(fixes, axis=0), up_low)
    for q in range(2):
        series[0, q] = gathered_ref[0, 4 + q] + rows.repeat(refined[20 * q : 20 * q + 20])
        end = rows.repeat(refined[40 + 8 * q : 48 + 8 * q])
        series[8, q, 12:28] = w2_ref[q] + end

    for step in range(7):
        holder, place = step // 2, step % 2

        def load(i):
            return [series[step, q, block(i)] for q in range(2)]

        def force(i):
            return [gathered_ref[holder, 2 * place + q, block(i)] for q in range(2)]

        def store(i, values):
            for q in range(2):
                series[step + 1, q, block(i)] = values[q]

        advance(
            load, store, lambda i: [mid_coef[n, block(i)] for n in range(6)], (0, 5), force
        )

    changes = []
    for c in range(2):
        for q in range(2):
            changes.append(series[2 * m + c, q, 8:32] - w01_ref[c, q])
    for q in range(2):
        changes.append(series[2 * m + 2, q, 12:28] - w2_ref[q])
    refined = exact_dot(jnp.concatenate(changes, axis=0), up_matrix(512))
    for c in range(2):
        for q in range(2):
            n = 2 * c + q
            fine[0, c, q] = a01_ref[c, q] + rows.repeat(refined[24 * n : 24 * n + 24])
    for q in range(2):
        out_ref[15, q] = a2_ref[q] + rows.repeat(refined[96 + 16 * q : 112 + 16 * q])
        out_ref[7, q] = fine[0, 1, q, 8:40]

    def fine_step(source, target, position):
        for c in range(2):

            def load(i):
                return [fine[source, c, q, block(i)] for q in range(2)]

            def store(i, values):
                for q in range(2):
                    fine[target, c, q, block(i)] = values[q]
                    if 1 <= i < 5:
                        out_ref[8 * c + position, q, block(i - 1)] = values[q]

            advance(load, store, lambda i: [fine_ref[n, block(i)] for n in range(6)], (0, 6))

    def pair(n, carry):
        fine_step(0, 1, 2 * n)
        fine_step(1, 0, 2 * n + 1)
        return carry

    lax.fori_loop(0, 3, pair, 0)
    fine_step(0, 1, 6)


def struct(*shape):
    return jax.ShapeDtypeStruct(shape, F32)


def scratch(*shape):
    return pltpu.VMEM(shape, F32)


def device(t, s):
    return t * N_SPACE + s


def send(x, dt, ds):
    pairs = [
        (device(t, s), device((t + dt) % N_TM, s + ds))
        for t in range(N_TM)
        for s in range(N_SPACE)
        if 0 <= s + ds < N_SPACE
    ]
    return lax.ppermute(x, AXES, pairs)


def from_group_behind(x, ds):
    pairs = []
    for k in range(GROUP):
        for m in range(k):
            for s in range(N_SPACE):
                if 0 <= s + ds < N_SPACE:
                    pairs.append((device(4 * (k - 1 - m) + m, s + ds), device(4 * k + m, s)))
    return lax.ppermute(x, AXES, pairs)


def local(initial, guess, kappa, feed, kill, react):
    k, m = lax.axis_index("k"), lax.axis_index("m")
    t = GROUP * k + m
    where = jnp.stack([t, k, m]).astype(jnp.int32)
    coef = jnp.concatenate([kappa, feed[None], kill[None], react[None]])
    first_end = guess[7]
    ends = jnp.concatenate([first_end, guess[15]])
    sent = jnp.where(t == N_TM - 1, jnp.concatenate([initial, initial]), ends)
    beside = jnp.concatenate([coef, first_end])
    nlo = send(beside[:, 16:], 0, 1)
    nhi = send(beside[:, :16], 0, -1)
    dlo = send(sent[:, 16:], 1, 1)
    dhi = send(sent[:, :16], 1, -1)
    shift = send(sent, 1, 0)
    a01, a2, w01, w2, packed, fine = pl.pallas_call(
        fine_kernel,
        out_shape=(
            struct(2, 2, 48, 512), struct(2, 32, 512), struct(2, 2, 24, 256),
            struct(2, 16, 256), struct(11, 16, 256), struct(6, 48, 512),
        ),
        in_specs=[SMEM] + [VMEM] * 7,
        out_specs=(VMEM,) * 6,
        scratch_shapes=[
            scratch(3, 2, 64, 512), scratch(3, 2, 64, 512), scratch(5, 64, 512),
            scratch(6, 64, 512), scratch(2, 2, 32, 256), scratch(6, 32, 256), scratch(60, 64, 128),
        ],
    )(where, shift, dlo, dhi, nlo, nhi, first_end, coef)
    lo = send(packed, 0, 1)
    hi = send(packed, 0, -1)
    window = jnp.concatenate([lo[:6, 4:], packed[:6], hi[:6, :12]], axis=1)
    gathered = lax.all_gather(window, "m", axis=0, tiled=False)
    pred, mid_coef = pl.pallas_call(
        mid_kernel,
        out_shape=(struct(4, 8, 128), struct(6, 40, 256)),
        in_specs=[VMEM] * 4,
        out_specs=(VMEM,) * 2,
        scratch_shapes=[scratch(5, 48, 256), scratch(2, 2, 40, 256), scratch(8, 16, 128)],
    )(gathered, packed, lo, hi)
    pieces = [from_group_behind(pred, ds) for ds in (-1, 0, 1)]
    top = lax.all_gather(jnp.stack(pieces), "m", axis=0, tiled=False)
    return pl.pallas_call(
        final_kernel,
        out_shape=struct(16, 2, 32, 512),
        in_specs=[SMEM] + [VMEM] * 12,
        out_specs=VMEM,
        scratch_shapes=[
            scratch(5, 48, 256), scratch(6, 24, 128), scratch(4, 2, 24, 128),
            scratch(9, 2, 40, 256), scratch(50, 48, 128), scratch(2, 2, 2, 48, 512),
        ],
    )(where, gathered, top, pred, mid_coef, packed, lo, hi, a01, a2, w01, w2, fine)


def solution(mesh):
    split = Mesh(mesh.devices.reshape(4, 4, 16), AXES)
    tm = ("k", "m")
    placed = (
        P(None, "space", None),
        P(tm, None, "space", None),
        P(None, "space", None),
        P("space", None),
        P("space", None),
        P("space", None),
    )
    return jax.shard_map(
        local, mesh=split, in_specs=placed, out_specs=P(tm, None, "space", None), check_vma=False
    )
```

time: 528 us -> 97.2 us (0.18)
  the two profiles are of different devices: /device:TPU:134 before, /device:TPU:81 now
where the time goes in v1:
time: 97.2 us; the launch traced here: 96.3 us
  blocking collectives  29.3 us (30%)
  starting transfers between devices  27.8 us (29%)
  Pallas kernels  18 us (19%)
  waiting for transfers between devices  12.5 us (13%)
  local copies, waits for them, and re-layouts  6.1 us (6%)
  other arithmetic  2.42 us (2%)
    ppermute x7, starting transfers between devices, send(): return lax.ppermute(x, AXES, pairs)  23.9 us
    all_gather x1, blocking collectives, local(): top = lax.all_gather(jnp.stack(pieces), 'm', axis=0, tiled=False)  16.1 us
    all_gather x1, blocking collectives, local(): gathered = lax.all_gather(window, 'm', axis=0, tiled=False)  13.1 us
    ppermute x7, waiting for transfers between devices, send(): return lax.ppermute(x, AXES, pairs)  11.4 us
    pallas_call x1, Pallas kernels, local(): pl.pallas_call(fine_kernel, out_shape=(struct(2, 2, 48, 512), struct(2, 3...  8.47 us
    pallas_call x1, Pallas kernels, local(): pl.pallas_call(final_kernel, out_shape=struct(16, 2, 32, 512), in_specs=[...  6.77 us
    ppermute x3, starting transfers between devices, from_group_behind(): return lax.ppermute(x, AXES, pairs)  3.86 us
    unnamed x28, local copies, waits for them, and re-layouts  3.17 us
  transfers between devices with their start and end apart: 10, of which 4 were waited for; matrix products, arithmetic and copies ran while one was open for 5% of the time, Pallas kernels for 0%

profile of v1, /device:TPU:81, one launch (start us, length us, event | category | flops | bytes accessed | tf_op | source)
XLA Modules:
  0.0 96.3 jit_solution(1024518303275392196)
XLA Ops:
  0.0 0.0 copy-start.3
  0.0 0.0 copy-start.4
  0.0 0.0 copy-start.5
  0.0 0.0 copy-start.6
  0.0 1.0 %slice_bitcast_fusion.1 = (f32[2,32,512]{2,1,0:T(8,128)S(1)}, f32[2,32,512]{2,1,0:T(8,128)S(1)}) fusion(f32[16,2,32,512]{3,2,1,0:T(8,128)} %param.7), kind=kLoop, calls=%fused_computation.4 | loop fusion | bytes 524288 | tf_op jit(solution)/shard_map/squeeze | solution.py:496
  1.1 0.0 copy-start
  1.1 1.0 %maximum_select_fusion = f32[4,32,512]{2,1,0:T(8,128)S(1)} fusion(f32[2,32,512]{2,1,0:T(8,128)} %param.6, f32[2,32,512]{2,1,0:T(8,128)S(1)} %get-tuple-element.22, f32[2,32,512]{2,1,0:T(8,128)S(1)} %get-tuple-element.21.own_ref, pred[]{:T(512)S(6)} %eq.3), kind=kLoop, calls=%fused_computation.1 | loop fusion | flops 196608 | bytes 655361 | tf_op jit(solution)/shard_map/jit(_where)/select_n | solution.py:498
  2.1 2.2 %collective-permute-start = (f32[4,32,512]{2,1,0:T(8,128)S(1)}, f32[4,32,512]{2,1,0:T(8,128)S(1)}, u32[]{:S(2)}, u32[]{:S(2)}) collective-permute-start(f32[4,32,512]{2,1,0:T(8,128)S(1)} %maximum_select_fusion), channel_id=1, source_target_pairs={{0,16},{1,17},{2,18},{3,19},{4,20},{5,21},{6,22},{7,23},{8,24},{9,... | collective-permute-start | bytes 786440 | tf_op jit(solution)/shard_map/ppermute | solution.py:478
  4.4 4.0 %collective-permute-start.2 = (f32[4,16,512]{2,1,0:T(8,128)S(1)}, f32[4,16,512]{2,1,0:T(8,128)S(1)}, u32[]{:S(2)}, u32[]{:S(2)}) collective-permute-start(f32[4,16,512]{2,1,0:T(8,128)S(1)} %get-tuple-element.25), channel_id=1, source_target_pairs={{1,16},{2,17},{3,18},{4,19},{5,20},{6,21},{7,22},{8,23},{9,24},{10... | collective-permute-start | bytes 393224 | tf_op jit(solution)/shard_map/ppermute | solution.py:478
  8.4 4.1 %collective-permute-start.1 = (f32[4,16,512]{2,1,0:T(8,128)S(1)}, f32[4,16,512]{2,1,0:T(8,128)S(1)}, u32[]{:S(2)}, u32[]{:S(2)}) collective-permute-start(f32[4,16,512]{2,1,0:T(8,128)S(1)} %get-tuple-element.26), channel_id=1, source_target_pairs={{0,17},{1,18},{2,19},{3,20},{4,21},{5,22},{6,23},{7,24},{8,25},{9,... | collective-permute-start | bytes 393224 | tf_op jit(solution)/shard_map/ppermute | solution.py:478
  12.5 0.9 constant_dynamic-update-slice_fusion.4
  13.4 0.8 constant_dynamic-update-slice_fusion.3
  14.3 0.0 copy-done.5
  14.3 0.0 copy-done.6
  14.3 0.9 constant_dynamic-update-slice_fusion
  15.3 6.4 %collective-permute-start.4 = (f32[7,16,512]{2,1,0:T(8,128)S(1)}, f32[7,16,512]{2,1,0:T(8,128)S(1)}, u32[]{:S(2)}, u32[]{:S(2)}) collective-permute-start(f32[7,16,512]{2,1,0:T(8,128)S(1)} %get-tuple-element.23), channel_id=1, source_target_pairs={{1,0},{2,1},{3,2},{4,3},{5,4},{6,5},{7,6},{8,7},{9,8},{10,9},{11,1... | collective-permute-start | bytes 688136 | tf_op jit(solution)/shard_map/ppermute | solution.py:478
  21.7 1.9 %collective-permute-start.3 = (f32[7,16,512]{2,1,0:T(8,128)S(1)}, f32[7,16,512]{2,1,0:T(8,128)S(1)}, u32[]{:S(2)}, u32[]{:S(2)}) collective-permute-start(f32[7,16,512]{2,1,0:T(8,128)S(1)} %get-tuple-element.24), channel_id=1, source_target_pairs={{0,1},{1,2},{2,3},{3,4},{4,5},{5,6},{6,7},{7,8},{8,9},{9,10},{10,1... | collective-permute-start | bytes 688136 | tf_op jit(solution)/shard_map/ppermute | solution.py:478
  23.6 0.6 pad_add_fusion.where_ref
  24.2 0.0 copy-done.3
  24.2 0.0 copy-done.4
  24.2 0.7 pad_maximum_fusion.coef_ref
  24.9 0.0 collective-permute-done.2.dhi_ref
  24.9 0.0 copy-start.10
  24.9 0.0 collective-permute-done.1.dlo_ref
  24.9 0.0 copy-start.11
  25.0 0.0 collective-permute-done.4.nhi_ref
  25.0 0.0 copy-start.8
  25.0 6.0 %collective-permute-done.3.nlo_ref = f32[7,16,512]{2,1,0:T(8,128)S(1)} collective-permute-done((f32[7,16,512]{2,1,0:T(8,128)S(1)}, f32[7,16,512]{2,1,0:T(8,128)S(1)}, u32[]{:S(2)}, u32[]{:S(2)}) %collective-permute-start.3) | collective-permute-done | bytes 229408 | tf_op jit(solution)/shard_map/ppermute | solution.py:478
  31.0 0.0 copy-start.9
  31.0 0.0 collective-permute-done.shift_ref
  31.0 0.0 copy-done
  31.0 0.0 copy-done.10
  31.0 0.0 copy-done.11
  31.1 0.0 copy-done.8
  31.1 0.7 copy-done.9
  31.7 0.0 copy-start.7
  31.7 0.7 copy-done.7
  32.4 8.5 %shard_map.64 = (f32[2,2,48,512]{3,2,1,0:T(8,128)}, f32[2,32,512]{2,1,0:T(8,128)}, f32[2,2,24,256]{3,2,1,0:T(8,128)}, f32[2,16,256]{2,1,0:T(8,128)}, f32[11,16,256]{2,1,0:T(8,128)}, /*index=5*/f32[6,48,512]{2,1,0:T(8,128)}) custom-call(s32[3]{0:T(128)} %pad_add_fusion.where_ref, f32[4,32,512]{2,1,0:T(8,128)} %copy-done.7, f32[4,16,512]{2,1,0:T(8,128)} %copy-done.11, ...), custom_call_target="tpu_custom_call" | custom-call | tf_op jit(solution)/shard_map/pallas_call | solution.py:505
  40.9 1.9 %collective-permute-start.6 = (f32[11,16,256]{2,1,0:T(8,128)}, f32[11,16,256]{2,1,0:T(8,128)S(1)}, u32[]{:S(2)}, u32[]{:S(2)}) collective-permute-start(f32[11,16,256]{2,1,0:T(8,128)} %get-tuple-element.13.own_ref), channel_id=1, source_target_pairs={{1,0},{2,1},{3,2},{4,3},{5,4},{6,5},{7,6},{8,7},{9,8},{10,9},{11,1... | collective-permute-start | bytes 540680 | tf_op jit(solution)/shard_map/ppermute | solution.py:478
  42.8 3.4 %collective-permute-start.5 = (f32[11,16,256]{2,1,0:T(8,128)}, f32[11,16,256]{2,1,0:T(8,128)S(1)}, u32[]{:S(2)}, u32[]{:S(2)}) collective-permute-start(f32[11,16,256]{2,1,0:T(8,128)} %get-tuple-element.13.own_ref), channel_id=1, source_target_pairs={{0,1},{1,2},{2,3},{3,4},{4,5},{5,6},{6,7},{7,8},{8,9},{9,10},{10,1... | collective-permute-start | bytes 540680 | tf_op jit(solution)/shard_map/ppermute | solution.py:478
  46.2 0.9 slice.34
  47.1 1.3 %collective-permute-done.6.hi_ref = f32[11,16,256]{2,1,0:T(8,128)S(1)} collective-permute-done((f32[11,16,256]{2,1,0:T(8,128)}, f32[11,16,256]{2,1,0:T(8,128)S(1)}, u32[]{:S(2)}, u32[]{:S(2)}) %collective-permute-start.6) | collective-permute-done | bytes 180256 | tf_op jit(solution)/shard_map/ppermute | solution.py:478
  48.4 0.0 copy-start.1
  48.4 4.0 %collective-permute-done.5.lo_ref = f32[11,16,256]{2,1,0:T(8,128)S(1)} collective-permute-done((f32[11,16,256]{2,1,0:T(8,128)}, f32[11,16,256]{2,1,0:T(8,128)S(1)}, u32[]{:S(2)}, u32[]{:S(2)}) %collective-permute-start.5) | collective-permute-done | bytes 180256 | tf_op jit(solution)/shard_map/ppermute | solution.py:478
  52.5 0.0 copy-start.2
  52.5 13.1 %all-gather = f32[24,40,256]{2,1,0:T(8,128)} all-gather(f32[6,40,256]{2,1,0:T(8,128)S(1)} %pad_maximum_fusion.1), channel_id=2, replica_groups=mesh['k'=4,'m'=4,'space'=16] {'m'}, dimensions={0}, use_global_device_ids=true | all-gather | bytes 1228800 | tf_op jit(solution)/shard_map/all_gather | solution.py:521
  65.7 0.0 copy-done.1
  65.7 0.0 copy-done.2
  65.7 2.8 %shard_map.65 = (f32[4,8,128]{2,1,0:T(8,128)}, f32[6,40,256]{2,1,0:T(8,128)}) custom-call(f32[4,6,40,256]{3,2,1,0:T(8,128)} %bitcast.20, f32[11,16,256]{2,1,0:T(8,128)} %get-tuple-element.13.own_ref, f32[11,16,256]{2,1,0:T(8,128)} %copy-done.2, f32[11,16,256]{2,1,0:T(8,128)} %copy-done.1), custom_call_target="tpu_custom_call" | custom-call | tf_op jit(solution)/shard_map/pallas_call | solution.py:522
  68.4 1.3 %collective-permute-start.9 = (f32[4,8,128]{2,1,0:T(8,128)}, f32[4,8,128]{2,1,0:T(8,128)S(1)}, u32[]{:S(2)}, u32[]{:S(2)}) collective-permute-start(f32[4,8,128]{2,1,0:T(8,128)} %get-tuple-element.14.pred_ref), channel_id=1, source_target_pairs={{1,64},{2,65},{3,66},{4,67},{5,68},{6,69},{7,70},{8,71},{9,72},{10... | collective-permute-start | bytes 49160 | tf_op jit(solution)/shard_map/ppermute | solution.py:488
  69.7 1.3 %collective-permute-start.8 = (f32[4,8,128]{2,1,0:T(8,128)}, f32[4,8,128]{2,1,0:T(8,128)S(1)}, u32[]{:S(2)}, u32[]{:S(2)}) collective-permute-start(f32[4,8,128]{2,1,0:T(8,128)} %get-tuple-element.14.pred_ref), channel_id=1, source_target_pairs={{0,64},{1,65},{2,66},{3,67},{4,68},{5,69},{6,70},{7,71},{8,72},{9,... | collective-permute-start | bytes 49160 | tf_op jit(solution)/shard_map/ppermute | solution.py:488
  71.0 1.3 %collective-permute-start.7 = (f32[4,8,128]{2,1,0:T(8,128)}, f32[4,8,128]{2,1,0:T(8,128)S(1)}, u32[]{:S(2)}, u32[]{:S(2)}) collective-permute-start(f32[4,8,128]{2,1,0:T(8,128)} %get-tuple-element.14.pred_ref), channel_id=1, source_target_pairs={{0,65},{1,66},{2,67},{3,68},{4,69},{5,70},{6,71},{7,72},{8,73},{9,... | collective-permute-start | bytes 49160 | tf_op jit(solution)/shard_map/ppermute | solution.py:488
  72.3 0.0 collective-permute-done.9
  72.3 0.0 collective-permute-done.8
  72.3 1.0 %collective-permute-done.7 = f32[4,8,128]{2,1,0:T(8,128)S(1)} collective-permute-done((f32[4,8,128]{2,1,0:T(8,128)}, f32[4,8,128]{2,1,0:T(8,128)S(1)}, u32[]{:S(2)}, u32[]{:S(2)}) %collective-permute-start.7) | collective-permute-done | bytes 16416 | tf_op jit(solution)/shard_map/ppermute | solution.py:488
  73.4 16.1 %all-gather.1 = f32[12,4,8,128]{3,2,1,0:T(8,128)} all-gather(f32[3,4,8,128]{3,2,1,0:T(8,128)S(1)} %pad_maximum_fusion.2), channel_id=3, replica_groups=mesh['k'=4,'m'=4,'space'=16] {'m'}, dimensions={0}, use_global_device_ids=true | all-gather | bytes 245760 | tf_op jit(solution)/shard_map/all_gather | solution.py:530
  89.5 6.8 %shard_map.66 = f32[16,2,32,512]{3,2,1,0:T(8,128)} custom-call(s32[3]{0:T(128)} %pad_add_fusion.where_ref, f32[4,6,40,256]{3,2,1,0:T(8,128)} %bitcast.21, f32[4,3,4,8,128]{4,3,2,1,0:T(8,128)} %bitcast.22, f32[4,8,128]{2,1,0:T(8,128)} %get-tuple-element.14.pred_ref, f32[6,40,256]{2,1,0:T(8,128)} %get-tuple-element.15.mid_coef, ...), custom_call_target="tpu_custom_call" | custom-call | tf_op jit(solution)/shard_map/pallas_call | solution.py:531
  (8 shorter events, 0.1 us)
Async XLA Ops:
  0.0 24.2 %copy-start.3 = (f32[2,32,512]{2,1,0:T(8,128)S(1)}, f32[2,32,512]{2,1,0:T(8,128)}, u32[]{:S(2)}) copy-start(f32[2,32,512]{2,1,0:T(8,128)} %param.8) | copy-start | bytes 393220
  0.0 24.2 %copy-start.4 = (f32[32,512]{1,0:T(8,128)S(1)}, f32[32,512]{1,0:T(8,128)}, u32[]{:S(2)}) copy-start(f32[32,512]{1,0:T(8,128)} %param.9) | copy-start | bytes 196612
  0.0 14.3 %copy-start.5 = (f32[32,512]{1,0:T(8,128)S(1)}, f32[32,512]{1,0:T(8,128)}, u32[]{:S(2)}) copy-start(f32[32,512]{1,0:T(8,128)} %param.10) | copy-start | bytes 196612
  0.0 14.3 %copy-start.6 = (f32[32,512]{1,0:T(8,128)S(1)}, f32[32,512]{1,0:T(8,128)}, u32[]{:S(2)}) copy-start(f32[32,512]{1,0:T(8,128)} %param.11) | copy-start | bytes 196612
  1.1 30.0 %copy-start = (f32[2,32,512]{2,1,0:T(8,128)}, f32[2,32,512]{2,1,0:T(8,128)S(1)}, u32[]{:S(2)}) copy-start(f32[2,32,512]{2,1,0:T(8,128)S(1)} %get-tuple-element.21.own_ref) | copy-start | bytes 393220
  2.1 28.9 %collective-permute-start = (f32[4,32,512]{2,1,0:T(8,128)S(1)}, f32[4,32,512]{2,1,0:T(8,128)S(1)}, u32[]{:S(2)}, u32[]{:S(2)}) collective-permute-start(f32[4,32,512]{2,1,0:T(8,128)S(1)} %maximum_select_fusion), channel_id=1, source_target_pairs={{0,16},{1,17},{2,18},{3,19},{4,20},{5,21},{6,22},{7,23},{8,24},{9,... | collective-permute-start | bytes 786440 | tf_op jit(solution)/shard_map/ppermute | solution.py:478
  4.4 20.6 %collective-permute-start.2 = (f32[4,16,512]{2,1,0:T(8,128)S(1)}, f32[4,16,512]{2,1,0:T(8,128)S(1)}, u32[]{:S(2)}, u32[]{:S(2)}) collective-permute-start(f32[4,16,512]{2,1,0:T(8,128)S(1)} %get-tuple-element.25), channel_id=1, source_target_pairs={{1,16},{2,17},{3,18},{4,19},{5,20},{6,21},{7,22},{8,23},{9,24},{10... | collective-permute-start | bytes 393224 | tf_op jit(solution)/shard_map/ppermute | solution.py:478
  8.4 16.6 %collective-permute-start.1 = (f32[4,16,512]{2,1,0:T(8,128)S(1)}, f32[4,16,512]{2,1,0:T(8,128)S(1)}, u32[]{:S(2)}, u32[]{:S(2)}) collective-permute-start(f32[4,16,512]{2,1,0:T(8,128)S(1)} %get-tuple-element.26), channel_id=1, source_target_pairs={{0,17},{1,18},{2,19},{3,20},{4,21},{5,22},{6,23},{7,24},{8,25},{9,... | collective-permute-start | bytes 393224 | tf_op jit(solution)/shard_map/ppermute | solution.py:478
  15.3 9.7 %collective-permute-start.4 = (f32[7,16,512]{2,1,0:T(8,128)S(1)}, f32[7,16,512]{2,1,0:T(8,128)S(1)}, u32[]{:S(2)}, u32[]{:S(2)}) collective-permute-start(f32[7,16,512]{2,1,0:T(8,128)S(1)} %get-tuple-element.23), channel_id=1, source_target_pairs={{1,0},{2,1},{3,2},{4,3},{5,4},{6,5},{7,6},{8,7},{9,8},{10,9},{11,1... | collective-permute-start | bytes 688136 | tf_op jit(solution)/shard_map/ppermute | solution.py:478
  21.7 9.4 %collective-permute-start.3 = (f32[7,16,512]{2,1,0:T(8,128)S(1)}, f32[7,16,512]{2,1,0:T(8,128)S(1)}, u32[]{:S(2)}, u32[]{:S(2)}) collective-permute-start(f32[7,16,512]{2,1,0:T(8,128)S(1)} %get-tuple-element.24), channel_id=1, source_target_pairs={{0,1},{1,2},{2,3},{3,4},{4,5},{5,6},{6,7},{7,8},{8,9},{9,10},{10,1... | collective-permute-start | bytes 688136 | tf_op jit(solution)/shard_map/ppermute | solution.py:478
  24.9 6.1 %copy-start.10 = (f32[4,16,512]{2,1,0:T(8,128)}, f32[4,16,512]{2,1,0:T(8,128)S(1)}, u32[]{:S(2)}) copy-start(f32[4,16,512]{2,1,0:T(8,128)S(1)} %collective-permute-done.2.dhi_ref) | copy-start | bytes 393220
  24.9 6.1 %copy-start.11 = (f32[4,16,512]{2,1,0:T(8,128)}, f32[4,16,512]{2,1,0:T(8,128)S(1)}, u32[]{:S(2)}) copy-start(f32[4,16,512]{2,1,0:T(8,128)S(1)} %collective-permute-done.1.dlo_ref) | copy-start | bytes 393220
  25.0 6.1 %copy-start.8 = (f32[7,16,512]{2,1,0:T(8,128)}, f32[7,16,512]{2,1,0:T(8,128)S(1)}, u32[]{:S(2)}) copy-start(f32[7,16,512]{2,1,0:T(8,128)S(1)} %collective-permute-done.4.nhi_ref) | copy-start | bytes 688132
  31.0 0.7 copy-start.9
  31.7 0.7 copy-start.7
  40.9 7.5 %collective-permute-start.6 = (f32[11,16,256]{2,1,0:T(8,128)}, f32[11,16,256]{2,1,0:T(8,128)S(1)}, u32[]{:S(2)}, u32[]{:S(2)}) collective-permute-start(f32[11,16,256]{2,1,0:T(8,128)} %get-tuple-element.13.own_ref), channel_id=1, source_target_pairs={{1,0},{2,1},{3,2},{4,3},{5,4},{6,5},{7,6},{8,7},{9,8},{10,9},{11,1... | collective-permute-start | bytes 540680 | tf_op jit(solution)/shard_map/ppermute | solution.py:478
  42.8 9.7 %collective-permute-start.5 = (f32[11,16,256]{2,1,0:T(8,128)}, f32[11,16,256]{2,1,0:T(8,128)S(1)}, u32[]{:S(2)}, u32[]{:S(2)}) collective-permute-start(f32[11,16,256]{2,1,0:T(8,128)} %get-tuple-element.13.own_ref), channel_id=1, source_target_pairs={{0,1},{1,2},{2,3},{3,4},{4,5},{5,6},{6,7},{7,8},{8,9},{9,10},{10,1... | collective-permute-start | bytes 540680 | tf_op jit(solution)/shard_map/ppermute | solution.py:478
  48.4 17.2 %copy-start.1 = (f32[11,16,256]{2,1,0:T(8,128)}, f32[11,16,256]{2,1,0:T(8,128)S(1)}, u32[]{:S(2)}) copy-start(f32[11,16,256]{2,1,0:T(8,128)S(1)} %collective-permute-done.6.hi_ref) | copy-start | bytes 540676
  52.5 13.2 %copy-start.2 = (f32[11,16,256]{2,1,0:T(8,128)}, f32[11,16,256]{2,1,0:T(8,128)S(1)}, u32[]{:S(2)}) copy-start(f32[11,16,256]{2,1,0:T(8,128)S(1)} %collective-permute-done.5.lo_ref) | copy-start | bytes 540676
  68.4 3.9 %collective-permute-start.9 = (f32[4,8,128]{2,1,0:T(8,128)}, f32[4,8,128]{2,1,0:T(8,128)S(1)}, u32[]{:S(2)}, u32[]{:S(2)}) collective-permute-start(f32[4,8,128]{2,1,0:T(8,128)} %get-tuple-element.14.pred_ref), channel_id=1, source_target_pairs={{1,64},{2,65},{3,66},{4,67},{5,68},{6,69},{7,70},{8,71},{9,72},{10... | collective-permute-start | bytes 49160 | tf_op jit(solution)/shard_map/ppermute | solution.py:488
  69.7 2.6 %collective-permute-start.8 = (f32[4,8,128]{2,1,0:T(8,128)}, f32[4,8,128]{2,1,0:T(8,128)S(1)}, u32[]{:S(2)}, u32[]{:S(2)}) collective-permute-start(f32[4,8,128]{2,1,0:T(8,128)} %get-tuple-element.14.pred_ref), channel_id=1, source_target_pairs={{0,64},{1,65},{2,66},{3,67},{4,68},{5,69},{6,70},{7,71},{8,72},{9,... | collective-permute-start | bytes 49160 | tf_op jit(solution)/shard_map/ppermute | solution.py:488
  71.0 2.4 %collective-permute-start.7 = (f32[4,8,128]{2,1,0:T(8,128)}, f32[4,8,128]{2,1,0:T(8,128)S(1)}, u32[]{:S(2)}, u32[]{:S(2)}) collective-permute-start(f32[4,8,128]{2,1,0:T(8,128)} %get-tuple-element.14.pred_ref), channel_id=1, source_target_pairs={{0,65},{1,66},{2,67},{3,68},{4,69},{5,70},{6,71},{7,72},{8,73},{9,... | collective-permute-start | bytes 49160 | tf_op jit(solution)/shard_map/ppermute | solution.py:488

commit v2 on v1

--- a/solution.py
+++ b/solution.py
@@ -9,6 +9,7 @@
 F32 = jnp.float32
 AXES = ("k", "m", "space")
 VMEM = pl.BlockSpec(memory_space=pltpu.VMEM)
+ANY = pl.BlockSpec(memory_space=pl.ANY)
 SMEM = pl.BlockSpec(memory_space=pltpu.SMEM)
 N_TM = 16
 N_SPACE = 16
@@ -160,26 +161,69 @@
         return jnp.concatenate(parts, axis=1)
 
 
+def pack_kernel(
+    where_ref, initial_ref, guess_ref, kappa_ref, feed_ref, kill_ref, react_ref,
+    own_ref, low_ref, high_ref, sems,
+):
+    last = where_ref[0] == N_TM - 1
+    count = [0]
+
+    def copy(source, target):
+        n = count[0]
+        count[0] += 1
+        return pltpu.make_async_copy(source, target, sems.at[n])
+
+    def copies(pick, place, many):
+        out = []
+        at = pl.ds(place, many) if many > 1 else place
+        for target, low, size in ((own_ref, 0, 32), (low_ref, 16, 16), (high_ref, 0, 16)):
+            out.append(copy(pick(pl.ds(low, size)), target.at[at]))
+        return out
+
+    plain = []
+    plain += copies(lambda r: guess_ref.at[7, :, r], 5, 2)
+    plain += copies(lambda r: kappa_ref.at[:, r], 0, 2)
+    plain += copies(lambda r: feed_ref.at[r], 2, 1)
+    plain += copies(lambda r: kill_ref.at[r], 3, 1)
+    plain += copies(lambda r: react_ref.at[r], 4, 1)
+    for c in plain:
+        c.start()
+    mark = count[0]
+    ends = copies(lambda r: guess_ref.at[15, :, r], 7, 2)
+    count[0] = mark
+    starts = copies(lambda r: initial_ref.at[:, r], 7, 2)
+
+    @pl.when(last)
+    def _():
+        for c in starts:
+            c.start()
+
+    @pl.when(jnp.logical_not(last))
+    def _():
+        for c in ends:
+            c.start()
+
+    for c in plain + ends:
+        c.wait()
+
+
 def fine_kernel(
-    where_ref, shift_ref, dlo_ref, dhi_ref, nlo_ref, nhi_ref, own_ref, coef_ref,
-    a01_ref, a2_ref, w01_ref, w2_ref, send_ref, fine_ref,
+    where_ref, own_ref, lo_ref, hi_ref,
+    a01_ref, a2_ref, w2_ref, packed_ref, send_ref, fine_ref,
     s0, s1, raw, tall, mid_state, mid_coef, cells,
 ):
     rows = Rows(cells)
-    opening = where_ref[0] == 0
+    last = where_ref[0] == N_TM - 1
     for c in range(2):
         for q in range(2):
-            s0[c, q, 0:16] = dlo_ref[2 * c + q]
-            s0[c, q, 16:48] = shift_ref[2 * c + q]
-            s0[c, q, 48:64] = dhi_ref[2 * c + q]
-    for q in range(2):
-        s0[2, q, 0:16] = nlo_ref[5 + q]
-        s0[2, q, 16:48] = own_ref[q]
-        s0[2, q, 48:64] = nhi_ref[5 + q]
+            f = 5 + 2 * c + q
+            s0[c, q, 0:16] = lo_ref[f]
+            s0[c, q, 16:48] = own_ref[f]
+            s0[c, q, 48:64] = hi_ref[f]
     for f in range(5):
-        raw[f, 0:16] = nlo_ref[f]
-        raw[f, 16:48] = coef_ref[f]
-        raw[f, 48:64] = nhi_ref[f]
+        raw[f, 0:16] = lo_ref[f]
+        raw[f, 16:48] = own_ref[f]
+        raw[f, 48:64] = hi_ref[f]
     for i in range(8):
         r = block(i)
         parts = derived(*[raw[f, r] for f in range(5)])
@@ -206,46 +250,45 @@
         for source, target in ((s0, s1), (s1, s0)):
             run(source, target, 0, (0, 8))
             run(source, target, 1, (0, 8))
-            run(source, target, 2, (1, 7))
         return carry
 
     lax.fori_loop(0, 4, first_pair, 0)
 
     for q in range(2):
-        s0[0, q, 0:16] = jnp.where(opening, dlo_ref[q], s0[0, q, 0:16])
-        s0[0, q, 16:48] = jnp.where(opening, shift_ref[q], s0[0, q, 16:48])
-        s0[0, q, 48:64] = jnp.where(opening, dhi_ref[q], s0[0, q, 48:64])
+        a2_ref[q] = s0[0, q, 16:48]
+    stacked = [rows.coarsen(s0[0, q, 16:48]) for q in range(2)]
+    for q in range(2):
+        s0[0, q, 0:16] = jnp.where(last, lo_ref[7 + q], s0[0, q, 0:16])
+        s0[0, q, 16:48] = jnp.where(last, own_ref[7 + q], s0[0, q, 16:48])
+        s0[0, q, 48:64] = jnp.where(last, hi_ref[7 + q], s0[0, q, 48:64])
     for q in range(2):
         for c in range(2):
-            a01_ref[c, q] = s0[c, q, 8:56]
-        a2_ref[q] = s0[2, q, 16:48]
-
+            a01_ref[c, q, 0:48] = s0[c, q, 8:56]
+
+    stacked += [rows.coarsen(raw[f]) for f in range(5)]
+    stacked += [rows.coarsen(s0[c, q]) for c in range(2) for q in range(2)]
     down = down_matrix(512)
-    stacked = jnp.concatenate([rows.coarsen(raw[f]) for f in range(5)], axis=0)
-    coarse = exact_dot(stacked, down)
+    coarse = exact_dot(jnp.concatenate(stacked, axis=0), down)
+    for q in range(2):
+        w2_ref[q] = coarse[16 * q : 16 * q + 16]
+    base = 32
     for f in range(5):
-        send_ref[6 + f] = coarse[32 * f + 8 : 32 * f + 24]
+        send_ref[6 + f] = coarse[base + 32 * f + 8 : base + 32 * f + 24]
     for i in range(4):
-        at = [coarse[32 * f + 8 * i : 32 * f + 8 * i + 8] for f in range(5)]
+        at = [coarse[base + 32 * f + 8 * i : base + 32 * f + 8 * i + 8] for f in range(5)]
         parts = derived(2.0 * at[0], 2.0 * at[1], 8.0 * at[2], 8.0 * at[3], 8.0 * at[4])
         for n in range(6):
             mid_coef[n, block(i)] = parts[n]
-    stacked = jnp.concatenate(
-        [rows.coarsen(s0[c, q]) for c in range(2) for q in range(2)]
-        + [rows.coarsen(s0[2, q, 16:48]) for q in range(2)],
-        axis=0,
-    )
-    coarse = exact_dot(stacked, down)
+    base = 192
     for c in range(2):
         for q in range(2):
-            mid_state[c, q] = coarse[32 * (2 * c + q) : 32 * (2 * c + q) + 32]
-    for q in range(2):
-        w2_ref[q] = coarse[128 + 16 * q : 144 + 16 * q]
-    for c in range(2):
-        for q in range(2):
-            w01_ref[c, q] = mid_state[c, q, 4:28]
+            n = base + 32 * (2 * c + q)
+            mid_state[c, q] = coarse[n : n + 32]
+            a01_ref[c, q, 48:60, 0:256] = coarse[n + 4 : n + 16]
+            a01_ref[c, q, 48:60, 256:512] = coarse[n + 16 : n + 28]
     for q in range(2):
         send_ref[4 + q] = mid_state[0, q, 8:24]
+        packed_ref[4 + q] = mid_state[0, q, 8:24]
 
     def second_pair(n, carry):
         for source, target in ((s0, s1), (s1, s0)):
@@ -255,20 +298,11 @@
 
     lax.fori_loop(0, 4, second_pair, 0)
 
-    for q in range(2):
-        s0[0, q, 16:48] = s0[0, q, 16:48] - a01_ref[1, q, 8:40]
-        s0[1, q, 16:48] = s0[1, q, 16:48] - a2_ref[q]
     stacked = jnp.concatenate(
         [rows.coarsen(s0[c, q, 16:48]) for c in range(2) for q in range(2)], axis=0
     )
     coarse = exact_dot(stacked, down)
     for c in range(2):
-        for q in range(2):
-            at = coarse[16 * (2 * c + q) : 16 * (2 * c + q) + 16]
-            end = mid_state[1, q, 8:24] if c == 0 else w2_ref[q]
-            send_ref[2 * c + q] = at + end
-
-    for c in range(2):
 
         def load(i):
             return [mid_state[c, q, block(i)] for q in range(2)]
@@ -276,9 +310,10 @@
         def store(i, values):
             if 1 <= i < 3:
                 for q in range(2):
-                    send_ref[2 * c + q, block(i - 1)] = (
-                        send_ref[2 * c + q, block(i - 1)] - values[q]
-                    )
+                    n = 16 * (2 * c + q) + 8 * (i - 1)
+                    forcing = coarse[n : n + 8] - values[q]
+                    send_ref[2 * c + q, block(i - 1)] = forcing
+                    packed_ref[2 * c + q, block(i - 1)] = forcing
 
         advance(load, store, lambda i: [mid_coef[n, block(i)] for n in range(6)], (0, 4))
 
@@ -331,9 +366,9 @@
 
 def final_kernel(
     where_ref, gathered_ref, top_ref, pred_ref, mid_coef, own_ref, lo_ref, hi_ref,
-    a01_ref, a2_ref, w01_ref, w2_ref, fine_ref,
-    out_ref,
-    raw, low_coef, yz, series, cells, fine,
+    a01_ref, a2_ref, w2_ref, fine_ref,
+    result_ref,
+    raw, low_coef, yz, series, cells, fine, w01, out_ref, sems,
 ):
     rows = Rows(cells)
     k, m = where_ref[1], where_ref[2]
@@ -421,17 +456,25 @@
     changes = []
     for c in range(2):
         for q in range(2):
-            changes.append(series[2 * m + c, q, 8:32] - w01_ref[c, q])
+            w01[c, q, 0:12] = a01_ref[c, q, 48:60, 0:256]
+            w01[c, q, 12:24] = a01_ref[c, q, 48:60, 256:512]
+            changes.append(series[2 * m + c, q, 8:32] - w01[c, q])
     for q in range(2):
         changes.append(series[2 * m + 2, q, 12:28] - w2_ref[q])
     refined = exact_dot(jnp.concatenate(changes, axis=0), up_matrix(512))
     for c in range(2):
         for q in range(2):
             n = 2 * c + q
-            fine[0, c, q] = a01_ref[c, q] + rows.repeat(refined[24 * n : 24 * n + 24])
+            fine[0, c, q] = a01_ref[c, q, 0:48] + rows.repeat(refined[24 * n : 24 * n + 24])
     for q in range(2):
         out_ref[15, q] = a2_ref[q] + rows.repeat(refined[96 + 16 * q : 112 + 16 * q])
         out_ref[7, q] = fine[0, 1, q, 8:40]
+
+    def leave(n):
+        return pltpu.make_async_copy(out_ref.at[n], result_ref.at[n], sems.at[n])
+
+    leave(15).start()
+    leave(7).start()
 
     def fine_step(source, target, position):
         for c in range(2):
@@ -446,6 +489,7 @@
                         out_ref[8 * c + position, q, block(i - 1)] = values[q]
 
             advance(load, store, lambda i: [fine_ref[n, block(i)] for n in range(6)], (0, 6))
+            leave(8 * c + position).start()
 
     def pair(n, carry):
         fine_step(0, 1, 2 * n)
@@ -454,6 +498,8 @@
 
     lax.fori_loop(0, 3, pair, 0)
     fine_step(0, 1, 6)
+    for n in range(16):
+        leave(n).wait()
 
 
 def struct(*shape):
@@ -490,35 +536,37 @@
 
 def local(initial, guess, kappa, feed, kill, react):
     k, m = lax.axis_index("k"), lax.axis_index("m")
-    t = GROUP * k + m
-    where = jnp.stack([t, k, m]).astype(jnp.int32)
-    coef = jnp.concatenate([kappa, feed[None], kill[None], react[None]])
-    first_end = guess[7]
-    ends = jnp.concatenate([first_end, guess[15]])
-    sent = jnp.where(t == N_TM - 1, jnp.concatenate([initial, initial]), ends)
-    beside = jnp.concatenate([coef, first_end])
-    nlo = send(beside[:, 16:], 0, 1)
-    nhi = send(beside[:, :16], 0, -1)
-    dlo = send(sent[:, 16:], 1, 1)
-    dhi = send(sent[:, :16], 1, -1)
-    shift = send(sent, 1, 0)
-    a01, a2, w01, w2, packed, fine = pl.pallas_call(
+    where = jnp.stack([GROUP * k + m, k, m]).astype(jnp.int32)
+    own, low_edge, high_edge = pl.pallas_call(
+        pack_kernel,
+        out_shape=(struct(9, 32, 512), struct(9, 16, 512), struct(9, 16, 512)),
+        in_specs=[SMEM] + [ANY] * 6,
+        out_specs=(VMEM,) * 3,
+        scratch_shapes=[pltpu.SemaphoreType.DMA((18,))],
+    )(where, initial, guess, kappa, feed, kill, react)
+    lo = send(low_edge, 0, 1)
+    hi = send(high_edge, 0, -1)
+    a01, a2, w2, held, packed, fine = pl.pallas_call(
         fine_kernel,
         out_shape=(
-            struct(2, 2, 48, 512), struct(2, 32, 512), struct(2, 2, 24, 256),
-            struct(2, 16, 256), struct(11, 16, 256), struct(6, 48, 512),
+            struct(2, 2, 60, 512), struct(2, 32, 512), struct(2, 16, 256),
+            struct(6, 16, 256), struct(11, 16, 256), struct(6, 48, 512),
         ),
-        in_specs=[SMEM] + [VMEM] * 7,
+        in_specs=[SMEM] + [VMEM] * 3,
         out_specs=(VMEM,) * 6,
         scratch_shapes=[
-            scratch(3, 2, 64, 512), scratch(3, 2, 64, 512), scratch(5, 64, 512),
-            scratch(6, 64, 512), scratch(2, 2, 32, 256), scratch(6, 32, 256), scratch(60, 64, 128),
+            scratch(2, 2, 64, 512), scratch(2, 2, 64, 512), scratch(5, 64, 512),
+            scratch(6, 64, 512), scratch(2, 2, 32, 256), scratch(6, 32, 256),
+            scratch(60, 64, 128),
         ],
-    )(where, shift, dlo, dhi, nlo, nhi, first_end, coef)
-    lo = send(packed, 0, 1)
-    hi = send(packed, 0, -1)
-    window = jnp.concatenate([lo[:6, 4:], packed[:6], hi[:6, :12]], axis=1)
+    )(where, own, lo, hi)
+    lo = send(packed, 1, 1)
+    hi = send(packed, 1, -1)
+    middle = send(held, 1, 0)
+    window = jnp.concatenate([lo[:6, 4:], middle, hi[:6, :12]], axis=1)
     gathered = lax.all_gather(window, "m", axis=0, tiled=False)
+    gathered, a01 = lax.optimization_barrier((gathered, a01))
+    a01 = send(a01, 1, 0)
     pred, mid_coef = pl.pallas_call(
         mid_kernel,
         out_shape=(struct(4, 8, 128), struct(6, 40, 256)),
@@ -531,13 +579,14 @@
     return pl.pallas_call(
         final_kernel,
         out_shape=struct(16, 2, 32, 512),
-        in_specs=[SMEM] + [VMEM] * 12,
-        out_specs=VMEM,
+        in_specs=[SMEM] + [VMEM] * 11,
+        out_specs=ANY,
         scratch_shapes=[
             scratch(5, 48, 256), scratch(6, 24, 128), scratch(4, 2, 24, 128),
             scratch(9, 2, 40, 256), scratch(50, 48, 128), scratch(2, 2, 2, 48, 512),
+            scratch(2, 2, 24, 256), scratch(16, 2, 32, 512), pltpu.SemaphoreType.DMA((16,)),
         ],
-    )(where, gathered, top, pred, mid_coef, packed, lo, hi, a01, a2, w01, w2, fine)
+    )(where, gathered, top, pred, mid_coef, packed, lo, hi, a01, a2, w2, fine)
 
 
 def solution(mesh):

time: 97.2 us -> 88.6 us (0.912)
  local copies, waits for them, and re-layouts: 6.1 us -> 1.56 us
  blocking collectives: 29.3 us -> 25.7 us
  other arithmetic: 2.42 us -> 0.59 us
  Pallas kernels: 18 us -> 19.6 us
  waiting for transfers between devices: 12.5 us -> 13.6 us
    ppermute x7 -> x6, starting transfers between devices: 23.9 us -> 19 us  [send(): return lax.ppermute(x, AXES, pairs)]
    ppermute x3, starting transfers between devices: 3.86 us -> 8.12 us  [from_group_behind(): return lax.ppermute(x, AXES, pairs)]
    pallas_call x1 -> x2, Pallas kernels: 8.47 us -> 10.6 us  [the longest x1 7.46 us: local(): pl.pallas_call(fine_kernel, out_shape=(struct(2, 2, 60, 512), struct(2, 3...]
    all_gather x1, blocking collectives: 16.1 us -> 14 us  [local(): top = lax.all_gather(jnp.stack(pieces), 'm', axis=0, tiled=False)]
    unnamed x28 -> x12, local copies, waits for them, and re-layouts: 3.17 us -> 1.54 us
    all_gather x1, blocking collectives: 13.1 us -> 11.6 us  [local(): gathered = lax.all_gather(window, 'm', axis=0, tiled=False)]
    ppermute x7 -> x6, waiting for transfers between devices: 11.4 us -> 12.5 us  [send(): return lax.ppermute(x, AXES, pairs)]
    select_n x1 -> x0, other arithmetic: 1.05 us -> none  [local(): sent = jnp.where(t == N_TM - 1, jnp.concatenate([initial, initial]), ends)]
  transfers between devices with their start and end apart: 10 -> 9, of which waited for: 4 -> 5; matrix products, arithmetic and copies ran while one was open for 5% -> 0% of each run, Pallas kernels for 0% -> 3%
where the time goes in v2:
time: 88.6 us; the launch traced here: 88.2 us
  starting transfers between devices  27.1 us (31%)
  blocking collectives  25.7 us (29%)
  Pallas kernels  19.6 us (22%)
  waiting for transfers between devices  13.6 us (15%)
  local copies, waits for them, and re-layouts  1.56 us (2%)
    ppermute x6, starting transfers between devices, send(): return lax.ppermute(x, AXES, pairs)  19 us
    all_gather x1, blocking collectives, local(): top = lax.all_gather(jnp.stack(pieces), 'm', axis=0, tiled=False)  14 us
    ppermute x6, waiting for transfers between devices, send(): return lax.ppermute(x, AXES, pairs)  12.5 us
    all_gather x1, blocking collectives, local(): gathered = lax.all_gather(window, 'm', axis=0, tiled=False)  11.6 us
    ppermute x3, starting transfers between devices, from_group_behind(): return lax.ppermute(x, AXES, pairs)  8.12 us
    pallas_call x1, Pallas kernels, local(): pl.pallas_call(fine_kernel, out_shape=(struct(2, 2, 60, 512), struct(2, 3...  7.46 us
    pallas_call x1, Pallas kernels, local(): pl.pallas_call(final_kernel, out_shape=struct(16, 2, 32, 512), in_specs=[...  6.26 us
    pallas_call x1, Pallas kernels, local(): pl.pallas_call(pack_kernel, out_shape=(struct(9, 32, 512), struct(9, 16,...  3.11 us
  transfers between devices with their start and end apart: 9, of which 5 were waited for; matrix products, arithmetic and copies ran while one was open for 0% of the time, Pallas kernels for 3%

profile of v2, /device:TPU:81, one launch (start us, length us, event | category | flops | bytes accessed | tf_op | source)
XLA Modules:
  0.0 88.2 jit_solution(9714000346872062449)
XLA Ops:
  0.0 0.6 pad_add_fusion.where_ref
  0.6 3.1 %shard_map.64 = (f32[9,32,512]{2,1,0:T(8,128)}, f32[9,16,512]{2,1,0:T(8,128)}, f32[9,16,512]{2,1,0:T(8,128)}) custom-call(s32[3]{0:T(128)} %pad_add_fusion.where_ref, f32[2,32,512]{2,1,0:T(8,128)} %initial_ref.1, f32[16,2,32,512]{3,2,1,0:T(8,128)} %guess_ref.1, f32[2,32,512]{2,1,0:T(8,128)} %kappa_ref.1, f32[32,512]{1,0:T(8,128)} %feed_ref.1, ...), custom_call_target="tpu_custom_call" | custom-call | tf_op jit(solution)/shard_map/pallas_call | solution.py:540
  3.7 3.1 %collective-permute-start = (f32[9,16,512]{2,1,0:T(8,128)}, f32[9,16,512]{2,1,0:T(8,128)S(1)}, u32[]{:S(2)}, u32[]{:S(2)}) collective-permute-start(f32[9,16,512]{2,1,0:T(8,128)} %get-tuple-element.19), channel_id=1, source_target_pairs={{0,1},{1,2},{2,3},{3,4},{4,5},{5,6},{6,7},{7,8},{8,9},{9,10},{10,1... | collective-permute-start | bytes 884744 | tf_op jit(solution)/shard_map/ppermute | solution.py:524
  6.8 4.3 %collective-permute-start.1 = (f32[9,16,512]{2,1,0:T(8,128)}, f32[9,16,512]{2,1,0:T(8,128)S(1)}, u32[]{:S(2)}, u32[]{:S(2)}) collective-permute-start(f32[9,16,512]{2,1,0:T(8,128)} %get-tuple-element.20), channel_id=1, source_target_pairs={{1,0},{2,1},{3,2},{4,3},{5,4},{6,5},{7,6},{8,7},{9,8},{10,9},{11,1... | collective-permute-start | bytes 884744 | tf_op jit(solution)/shard_map/ppermute | solution.py:524
  11.1 4.7 %collective-permute-done.lo_ref = f32[9,16,512]{2,1,0:T(8,128)S(1)} collective-permute-done((f32[9,16,512]{2,1,0:T(8,128)}, f32[9,16,512]{2,1,0:T(8,128)S(1)}, u32[]{:S(2)}, u32[]{:S(2)}) %collective-permute-start) | collective-permute-done | bytes 294944 | tf_op jit(solution)/shard_map/ppermute | solution.py:524
  15.8 0.0 copy-start.3
  15.8 1.0 %collective-permute-done.1.hi_ref = f32[9,16,512]{2,1,0:T(8,128)S(1)} collective-permute-done((f32[9,16,512]{2,1,0:T(8,128)}, f32[9,16,512]{2,1,0:T(8,128)S(1)}, u32[]{:S(2)}, u32[]{:S(2)}) %collective-permute-start.1) | collective-permute-done | bytes 294944 | tf_op jit(solution)/shard_map/ppermute | solution.py:524
  16.8 0.0 copy-start.4
  16.8 0.0 copy-done.3
  16.8 0.7 copy-done.4
  17.5 7.5 %shard_map.65 = (f32[2,2,60,512]{3,2,1,0:T(8,128)}, f32[2,32,512]{2,1,0:T(8,128)}, f32[2,16,256]{2,1,0:T(8,128)}, f32[6,16,256]{2,1,0:T(8,128)}, f32[11,16,256]{2,1,0:T(8,128)}, /*index=5*/f32[6,48,512]{2,1,0:T(8,128)}) custom-call(s32[3]{0:T(128)} %pad_add_fusion.where_ref, f32[9,32,512]{2,1,0:T(8,128)} %get-tuple-element.18.own_ref, ...), custom_call_target="tpu_custom_call" | custom-call | tf_op jit(solution)/shard_map/pallas_call | solution.py:549
  25.0 0.0 copy-start.5
  25.0 9.3 %collective-permute-start.4 = (f32[11,16,256]{2,1,0:T(8,128)}, f32[11,16,256]{2,1,0:T(8,128)S(1)}, u32[]{:S(2)}, u32[]{:S(2)}) collective-permute-start(f32[11,16,256]{2,1,0:T(8,128)} %get-tuple-element.21.own_ref), channel_id=1, source_target_pairs={{1,16},{2,17},{3,18},{4,19},{5,20},{6,21},{7,22},{8,23},{9,24},{10... | collective-permute-start | bytes 540680 | tf_op jit(solution)/shard_map/ppermute | solution.py:524
  34.3 1.9 %collective-permute-start.2 = (f32[11,16,256]{2,1,0:T(8,128)}, f32[11,16,256]{2,1,0:T(8,128)S(1)}, u32[]{:S(2)}, u32[]{:S(2)}) collective-permute-start(f32[11,16,256]{2,1,0:T(8,128)} %get-tuple-element.21.own_ref), channel_id=1, source_target_pairs={{0,17},{1,18},{2,19},{3,20},{4,21},{5,22},{6,23},{7,24},{8,25},{9,... | collective-permute-start | bytes 540680 | tf_op jit(solution)/shard_map/ppermute | solution.py:524
  36.2 0.4 collective-permute-start.3
  36.6 0.4 collective-permute-done.4.hi_ref
  37.0 0.0 copy-start
  37.0 6.4 %collective-permute-done.2.lo_ref = f32[11,16,256]{2,1,0:T(8,128)S(1)} collective-permute-done((f32[11,16,256]{2,1,0:T(8,128)}, f32[11,16,256]{2,1,0:T(8,128)S(1)}, u32[]{:S(2)}, u32[]{:S(2)}) %collective-permute-start.2) | collective-permute-done | bytes 180256 | tf_op jit(solution)/shard_map/ppermute | solution.py:524
  43.4 0.0 copy-start.1
  43.4 0.0 collective-permute-done.3
  43.5 11.6 %all-gather = f32[24,40,256]{2,1,0:T(8,128)} all-gather(f32[6,40,256]{2,1,0:T(8,128)S(1)} %pad_maximum_fusion), channel_id=2, replica_groups=mesh['k'=4,'m'=4,'space'=16] {'m'}, dimensions={0}, use_global_device_ids=true | all-gather | bytes 1228800 | tf_op jit(solution)/shard_map/all_gather | solution.py:567
  55.1 0.0 copy-done.5
  55.1 0.0 collective-permute-start.8
  55.1 0.0 copy-done
  55.1 0.0 copy-done.1
  55.1 2.8 %shard_map.66 = (f32[4,8,128]{2,1,0:T(8,128)}, f32[6,40,256]{2,1,0:T(8,128)}) custom-call(f32[4,6,40,256]{3,2,1,0:T(8,128)} %bitcast.8, f32[11,16,256]{2,1,0:T(8,128)} %get-tuple-element.21.own_ref, f32[11,16,256]{2,1,0:T(8,128)} %copy-done.1, f32[11,16,256]{2,1,0:T(8,128)} %copy-done), custom_call_target="tpu_custom_call" | custom-call | tf_op jit(solution)/shard_map/pallas_call | solution.py:570
  57.9 5.5 %collective-permute-start.7 = (f32[4,8,128]{2,1,0:T(8,128)}, f32[4,8,128]{2,1,0:T(8,128)S(1)}, u32[]{:S(2)}, u32[]{:S(2)}) collective-permute-start(f32[4,8,128]{2,1,0:T(8,128)} %get-tuple-element.25.pred_ref), channel_id=1, source_target_pairs={{1,64},{2,65},{3,66},{4,67},{5,68},{6,69},{7,70},{8,71},{9,72},{10... | collective-permute-start | bytes 49160 | tf_op jit(solution)/shard_map/ppermute | solution.py:534
  63.4 1.3 %collective-permute-start.6 = (f32[4,8,128]{2,1,0:T(8,128)}, f32[4,8,128]{2,1,0:T(8,128)S(1)}, u32[]{:S(2)}, u32[]{:S(2)}) collective-permute-start(f32[4,8,128]{2,1,0:T(8,128)} %get-tuple-element.25.pred_ref), channel_id=1, source_target_pairs={{0,64},{1,65},{2,66},{3,67},{4,68},{5,69},{6,70},{7,71},{8,72},{9,... | collective-permute-start | bytes 49160 | tf_op jit(solution)/shard_map/ppermute | solution.py:534
  64.7 1.3 %collective-permute-start.5 = (f32[4,8,128]{2,1,0:T(8,128)}, f32[4,8,128]{2,1,0:T(8,128)S(1)}, u32[]{:S(2)}, u32[]{:S(2)}) collective-permute-start(f32[4,8,128]{2,1,0:T(8,128)} %get-tuple-element.25.pred_ref), channel_id=1, source_target_pairs={{0,65},{1,66},{2,67},{3,68},{4,69},{5,70},{6,71},{7,72},{8,73},{9,... | collective-permute-start | bytes 49160 | tf_op jit(solution)/shard_map/ppermute | solution.py:534
  66.0 0.0 collective-permute-done.7
  66.0 0.0 collective-permute-done.6
  66.0 1.0 %collective-permute-done.5 = f32[4,8,128]{2,1,0:T(8,128)S(1)} collective-permute-done((f32[4,8,128]{2,1,0:T(8,128)}, f32[4,8,128]{2,1,0:T(8,128)S(1)}, u32[]{:S(2)}, u32[]{:S(2)}) %collective-permute-start.5) | collective-permute-done | bytes 16416 | tf_op jit(solution)/shard_map/ppermute | solution.py:534
  67.1 14.0 %all-gather.1 = f32[12,4,8,128]{3,2,1,0:T(8,128)} all-gather(f32[3,4,8,128]{3,2,1,0:T(8,128)S(1)} %pad_maximum_fusion.1), channel_id=3, replica_groups=mesh['k'=4,'m'=4,'space'=16] {'m'}, dimensions={0}, use_global_device_ids=true | all-gather | bytes 245760 | tf_op jit(solution)/shard_map/all_gather | solution.py:578
  81.1 0.0 collective-permute-done.8.a01_ref
  81.1 0.0 copy-start.2
  81.1 0.8 copy-done.2
  82.0 6.3 %shard_map.67 = f32[16,2,32,512]{3,2,1,0:T(8,128)} custom-call(s32[3]{0:T(128)} %pad_add_fusion.where_ref, f32[4,6,40,256]{3,2,1,0:T(8,128)} %bitcast.9, f32[4,3,4,8,128]{4,3,2,1,0:T(8,128)} %bitcast.10, f32[4,8,128]{2,1,0:T(8,128)} %get-tuple-element.25.pred_ref, f32[6,40,256]{2,1,0:T(8,128)} %get-tuple-element.26.mid_coef, ...), custom_call_target="tpu_custom_call" | custom-call | tf_op jit(solution)/shard_map/pallas_call | solution.py:579
  (4 shorter events, 0.1 us)
Async XLA Ops:
  3.7 12.1 %collective-permute-start = (f32[9,16,512]{2,1,0:T(8,128)}, f32[9,16,512]{2,1,0:T(8,128)S(1)}, u32[]{:S(2)}, u32[]{:S(2)}) collective-permute-start(f32[9,16,512]{2,1,0:T(8,128)} %get-tuple-element.19), channel_id=1, source_target_pairs={{0,1},{1,2},{2,3},{3,4},{4,5},{5,6},{6,7},{7,8},{8,9},{9,10},{10,1... | collective-permute-start | bytes 884744 | tf_op jit(solution)/shard_map/ppermute | solution.py:524
  6.8 10.0 %collective-permute-start.1 = (f32[9,16,512]{2,1,0:T(8,128)}, f32[9,16,512]{2,1,0:T(8,128)S(1)}, u32[]{:S(2)}, u32[]{:S(2)}) collective-permute-start(f32[9,16,512]{2,1,0:T(8,128)} %get-tuple-element.20), channel_id=1, source_target_pairs={{1,0},{2,1},{3,2},{4,3},{5,4},{6,5},{7,6},{8,7},{9,8},{10,9},{11,1... | collective-permute-start | bytes 884744 | tf_op jit(solution)/shard_map/ppermute | solution.py:524
  15.8 1.0 %copy-start.3 = (f32[9,16,512]{2,1,0:T(8,128)}, f32[9,16,512]{2,1,0:T(8,128)S(1)}, u32[]{:S(2)}) copy-start(f32[9,16,512]{2,1,0:T(8,128)S(1)} %collective-permute-done.lo_ref) | copy-start | bytes 884740
  16.8 0.7 copy-start.4
  25.0 30.1 %copy-start.5 = (f32[2,2,60,512]{3,2,1,0:T(8,128)S(1)}, f32[2,2,60,512]{3,2,1,0:T(8,128)}, u32[]{:S(2)}) copy-start(f32[2,2,60,512]{3,2,1,0:T(8,128)} %get-tuple-element.27) | copy-start | bytes 1474564
  25.0 12.0 %collective-permute-start.4 = (f32[11,16,256]{2,1,0:T(8,128)}, f32[11,16,256]{2,1,0:T(8,128)S(1)}, u32[]{:S(2)}, u32[]{:S(2)}) collective-permute-start(f32[11,16,256]{2,1,0:T(8,128)} %get-tuple-element.21.own_ref), channel_id=1, source_target_pairs={{1,16},{2,17},{3,18},{4,19},{5,20},{6,21},{7,22},{8,23},{9,24},{10... | collective-permute-start | bytes 540680 | tf_op jit(solution)/shard_map/ppermute | solution.py:524
  34.3 9.1 %collective-permute-start.2 = (f32[11,16,256]{2,1,0:T(8,128)}, f32[11,16,256]{2,1,0:T(8,128)S(1)}, u32[]{:S(2)}, u32[]{:S(2)}) collective-permute-start(f32[11,16,256]{2,1,0:T(8,128)} %get-tuple-element.21.own_ref), channel_id=1, source_target_pairs={{0,17},{1,18},{2,19},{3,20},{4,21},{5,22},{6,23},{7,24},{8,25},{9,... | collective-permute-start | bytes 540680 | tf_op jit(solution)/shard_map/ppermute | solution.py:524
  36.2 7.2 %collective-permute-start.3 = (f32[6,16,256]{2,1,0:T(8,128)}, f32[6,16,256]{2,1,0:T(8,128)S(1)}, u32[]{:S(2)}, u32[]{:S(2)}) collective-permute-start(f32[6,16,256]{2,1,0:T(8,128)} %get-tuple-element.22), channel_id=1, source_target_pairs={{0,16},{1,17},{2,18},{3,19},{4,20},{5,21},{6,22},{7,23},{8,24},{9,... | collective-permute-start | bytes 294920 | tf_op jit(solution)/shard_map/ppermute | solution.py:524
  37.0 18.1 %copy-start = (f32[11,16,256]{2,1,0:T(8,128)}, f32[11,16,256]{2,1,0:T(8,128)S(1)}, u32[]{:S(2)}) copy-start(f32[11,16,256]{2,1,0:T(8,128)S(1)} %collective-permute-done.4.hi_ref) | copy-start | bytes 540676
  43.4 11.7 %copy-start.1 = (f32[11,16,256]{2,1,0:T(8,128)}, f32[11,16,256]{2,1,0:T(8,128)S(1)}, u32[]{:S(2)}) copy-start(f32[11,16,256]{2,1,0:T(8,128)S(1)} %collective-permute-done.2.lo_ref) | copy-start | bytes 540676
  55.1 26.1 %collective-permute-start.8 = (f32[2,2,60,512]{3,2,1,0:T(8,128)S(1)}, f32[2,2,60,512]{3,2,1,0:T(8,128)S(1)}, u32[]{:S(2)}, u32[]{:S(2)}) collective-permute-start(f32[2,2,60,512]{3,2,1,0:T(8,128)S(1)} %copy-done.5), channel_id=1, source_target_pairs={{0,16},{1,17},{2,18},{3,19},{4,20},{5,21},{6,22},{7,23},{8,24},{9,... | collective-permute-start | bytes 1474568 | tf_op jit(solution)/shard_map/ppermute | solution.py:524
  57.9 8.1 %collective-permute-start.7 = (f32[4,8,128]{2,1,0:T(8,128)}, f32[4,8,128]{2,1,0:T(8,128)S(1)}, u32[]{:S(2)}, u32[]{:S(2)}) collective-permute-start(f32[4,8,128]{2,1,0:T(8,128)} %get-tuple-element.25.pred_ref), channel_id=1, source_target_pairs={{1,64},{2,65},{3,66},{4,67},{5,68},{6,69},{7,70},{8,71},{9,72},{10... | collective-permute-start | bytes 49160 | tf_op jit(solution)/shard_map/ppermute | solution.py:534
  63.4 2.6 %collective-permute-start.6 = (f32[4,8,128]{2,1,0:T(8,128)}, f32[4,8,128]{2,1,0:T(8,128)S(1)}, u32[]{:S(2)}, u32[]{:S(2)}) collective-permute-start(f32[4,8,128]{2,1,0:T(8,128)} %get-tuple-element.25.pred_ref), channel_id=1, source_target_pairs={{0,64},{1,65},{2,66},{3,67},{4,68},{5,69},{6,70},{7,71},{8,72},{9,... | collective-permute-start | bytes 49160 | tf_op jit(solution)/shard_map/ppermute | solution.py:534
  64.7 2.4 %collective-permute-start.5 = (f32[4,8,128]{2,1,0:T(8,128)}, f32[4,8,128]{2,1,0:T(8,128)S(1)}, u32[]{:S(2)}, u32[]{:S(2)}) collective-permute-start(f32[4,8,128]{2,1,0:T(8,128)} %get-tuple-element.25.pred_ref), channel_id=1, source_target_pairs={{0,65},{1,66},{2,67},{3,68},{4,69},{5,70},{6,71},{7,72},{8,73},{9,... | collective-permute-start | bytes 49160 | tf_op jit(solution)/shard_map/ppermute | solution.py:534
  81.1 0.8 copy-start.2

commit v3 on v2

--- a/solution.py
+++ b/solution.py
@@ -9,8 +9,7 @@
 F32 = jnp.float32
 AXES = ("k", "m", "space")
 VMEM = pl.BlockSpec(memory_space=pltpu.VMEM)
-ANY = pl.BlockSpec(memory_space=pl.ANY)
-SMEM = pl.BlockSpec(memory_space=pltpu.SMEM)
+HBM = pl.BlockSpec(memory_space=pltpu.HBM)
 N_TM = 16
 N_SPACE = 16
 GROUP = 4
@@ -119,6 +118,16 @@
         store(i, out)
 
 
+def advanced(values, coeffs, force=None):
+    out = [None] * len(values)
+
+    def store(i, new):
+        out[i] = new
+
+    advance(lambda i: values[i], store, coeffs, (0, len(values)), force)
+    return out
+
+
 def derived(spread_a, spread_b, supply, removal, coupling):
     return (
         spread_a,
@@ -162,10 +171,10 @@
 
 
 def pack_kernel(
-    where_ref, initial_ref, guess_ref, kappa_ref, feed_ref, kill_ref, react_ref,
+    initial_ref, guess_ref, kappa_ref, feed_ref, kill_ref, react_ref,
     own_ref, low_ref, high_ref, sems,
 ):
-    last = where_ref[0] == N_TM - 1
+    last = GROUP * lax.axis_index("k") + lax.axis_index("m") == N_TM - 1
     count = [0]
 
     def copy(source, target):
@@ -208,12 +217,12 @@
 
 
 def fine_kernel(
-    where_ref, own_ref, lo_ref, hi_ref,
+    own_ref, lo_ref, hi_ref,
     a01_ref, a2_ref, w2_ref, packed_ref, send_ref, fine_ref,
     s0, s1, raw, tall, mid_state, mid_coef, cells,
 ):
     rows = Rows(cells)
-    last = where_ref[0] == N_TM - 1
+    last = GROUP * lax.axis_index("k") + lax.axis_index("m") == N_TM - 1
     for c in range(2):
         for q in range(2):
             f = 5 + 2 * c + q
@@ -338,24 +347,19 @@
     def coeffs(i):
         return [coef_out_ref[n, block(i)] for n in range(6)]
 
+    values = [[gathered_ref[0, 4 + q, block(i)] for q in range(2)] for i in range(5)]
     for step in range(8):
         holder, place = step // 2, step % 2
 
-        def load(i):
-            if step == 0:
-                return [gathered_ref[0, 4 + q, block(i)] for q in range(2)]
-            return [state[(step + 1) % 2, q, block(i)] for q in range(2)]
-
         def force(i):
             return [gathered_ref[holder, 2 * place + q, block(i)] for q in range(2)]
 
-        def store(i, values):
-            for q in range(2):
-                state[step % 2, q, block(i)] = values[q]
-
-        advance(load, store, coeffs, (0, 5), force)
+        values = advanced(values, coeffs, force)
+    for i in range(5):
+        for q in range(2):
+            state[q, block(i)] = values[i][q]
     stacked = jnp.concatenate(
-        [rows.coarsen(state[1, q, 12:28]) for q in range(2)]
+        [rows.coarsen(state[q, 12:28]) for q in range(2)]
         + [rows.coarsen(gathered_ref[0, 4 + q, 12:28]) for q in range(2)],
         axis=0,
     )
@@ -365,13 +369,13 @@
 
 
 def final_kernel(
-    where_ref, gathered_ref, top_ref, pred_ref, mid_coef, own_ref, lo_ref, hi_ref,
+    gathered_ref, top_ref, pred_ref, mid_coef, own_ref, lo_ref, hi_ref,
     a01_ref, a2_ref, w2_ref, fine_ref,
     result_ref,
     raw, low_coef, yz, series, cells, fine, w01, out_ref, sems,
 ):
     rows = Rows(cells)
-    k, m = where_ref[1], where_ref[2]
+    k, m = lax.axis_index("k"), lax.axis_index("m")
     for f in range(5):
         raw[f, 0:16] = lo_ref[6 + f]
         raw[f, 16:32] = own_ref[6 + f]
@@ -385,30 +389,24 @@
     for n in range(6):
         low_coef[n] = parts[n]
 
-    def low_step(slot, target):
-        def load(i):
-            return [yz[slot, q, block(i)] for q in range(2)]
-
-        def store(i, values):
-            for q in range(2):
-                yz[target, q, block(i)] = values[q]
-
-        advance(load, store, lambda i: [low_coef[n, block(i)] for n in range(6)], (0, 3))
-
-    for q in range(2):
-        yz[0, q] = jnp.zeros((24, 128), F32)
-    for back in (2, 1, 0):
-        behind = k - 1 - back
-        follows = jnp.where(behind > 0, F32(1.0), F32(0.0))
+    def low_step(values):
+        return advanced(values, lambda i: [low_coef[n, block(i)] for n in range(6)])
+
+    def kept(slot):
+        return [[yz[slot, q, block(i)] for q in range(2)] for i in range(3)]
+
+    values = [[top_ref[2, i, q] for q in range(2)] for i in range(3)]
+    for back in (1, 0):
+        follows = jnp.where(k - 1 - back > 0, F32(1.0), F32(0.0))
+        other = low_step([[top_ref[back, i, 2 + q] for q in range(2)] for i in range(3)])
+        values = low_step(values)
+        values = [
+            [top_ref[back, i, q] + follows * (values[i][q] - other[i][q]) for q in range(2)]
+            for i in range(3)
+        ]
+    for i in range(3):
         for q in range(2):
-            for piece in range(3):
-                yz[1, q, block(piece)] = top_ref[back, piece, 2 + q]
-        low_step(0, 2)
-        low_step(1, 3)
-        for q in range(2):
-            for piece in range(3):
-                r = block(piece)
-                yz[0, q, r] = top_ref[back, piece, q] + follows * (yz[2, q, r] - yz[3, q, r])
+            yz[0, q, block(i)] = values[i][q]
     stacked = jnp.concatenate(
         [rows.coarsen(gathered_ref[0, 4 + q]) for q in range(2)]
         + [rows.coarsen(w2_ref[q]) for q in range(2)]
@@ -423,11 +421,9 @@
         yz[1, q] = jnp.zeros((24, 128), F32)
         yz[1, q, 2:22] = z
         fixes.append(inner * (yz[0, q, 2:22] - z))
-    low_step(0, 2)
-    low_step(1, 3)
-    for q in range(2):
-        r = block(1)
-        end = pred_ref[q] + inner * (yz[2, q, r] - yz[3, q, r])
+    values, other = low_step(values), low_step(kept(1))
+    for q in range(2):
+        end = pred_ref[q] + inner * (values[1][q] - other[1][q])
         fixes.append(end - coarse[40 + 8 * q : 48 + 8 * q])
     fixes.append(jnp.zeros((8, 128), F32))
     refined = exact_dot(jnp.concatenate(fixes, axis=0), up_low)
@@ -436,22 +432,17 @@
         end = rows.repeat(refined[40 + 8 * q : 48 + 8 * q])
         series[8, q, 12:28] = w2_ref[q] + end
 
+    values = [[series[0, q, block(i)] for q in range(2)] for i in range(5)]
     for step in range(7):
         holder, place = step // 2, step % 2
 
-        def load(i):
-            return [series[step, q, block(i)] for q in range(2)]
-
         def force(i):
             return [gathered_ref[holder, 2 * place + q, block(i)] for q in range(2)]
 
-        def store(i, values):
+        values = advanced(values, lambda i: [mid_coef[n, block(i)] for n in range(6)], force)
+        for i in range(5):
             for q in range(2):
-                series[step + 1, q, block(i)] = values[q]
-
-        advance(
-            load, store, lambda i: [mid_coef[n, block(i)] for n in range(6)], (0, 5), force
-        )
+                series[step + 1, q, block(i)] = values[i][q]
 
     changes = []
     for c in range(2):
@@ -503,11 +494,23 @@
 
 
 def struct(*shape):
-    return jax.ShapeDtypeStruct(shape, F32)
+    return pltpu.VMEM(shape, F32)
 
 
 def scratch(*shape):
     return pltpu.VMEM(shape, F32)
+
+
+def limit(mib):
+    return pltpu.CompilerParams(vmem_limit_bytes=mib * 2**20)
+
+
+def near(x):
+    return pltpu.with_memory_space_constraint(x, pltpu.VMEM)
+
+
+def far(x):
+    return pltpu.with_memory_space_constraint(x, pltpu.HBM)
 
 
 def device(t, s):
@@ -535,15 +538,14 @@
 
 
 def local(initial, guess, kappa, feed, kill, react):
-    k, m = lax.axis_index("k"), lax.axis_index("m")
-    where = jnp.stack([GROUP * k + m, k, m]).astype(jnp.int32)
     own, low_edge, high_edge = pl.pallas_call(
         pack_kernel,
         out_shape=(struct(9, 32, 512), struct(9, 16, 512), struct(9, 16, 512)),
-        in_specs=[SMEM] + [ANY] * 6,
+        in_specs=[HBM] * 6,
         out_specs=(VMEM,) * 3,
         scratch_shapes=[pltpu.SemaphoreType.DMA((18,))],
-    )(where, initial, guess, kappa, feed, kill, react)
+        compiler_params=limit(4),
+    )(*[far(x) for x in (initial, guess, kappa, feed, kill, react)])
     lo = send(low_edge, 0, 1)
     hi = send(high_edge, 0, -1)
     a01, a2, w2, held, packed, fine = pl.pallas_call(
@@ -552,14 +554,15 @@
             struct(2, 2, 60, 512), struct(2, 32, 512), struct(2, 16, 256),
             struct(6, 16, 256), struct(11, 16, 256), struct(6, 48, 512),
         ),
-        in_specs=[SMEM] + [VMEM] * 3,
+        in_specs=[VMEM] * 3,
         out_specs=(VMEM,) * 6,
         scratch_shapes=[
             scratch(2, 2, 64, 512), scratch(2, 2, 64, 512), scratch(5, 64, 512),
             scratch(6, 64, 512), scratch(2, 2, 32, 256), scratch(6, 32, 256),
             scratch(60, 64, 128),
         ],
-    )(where, own, lo, hi)
+        compiler_params=limit(14),
+    )(near(own), near(lo), near(hi))
     lo = send(packed, 1, 1)
     hi = send(packed, 1, -1)
     middle = send(held, 1, 0)
@@ -572,21 +575,23 @@
         out_shape=(struct(4, 8, 128), struct(6, 40, 256)),
         in_specs=[VMEM] * 4,
         out_specs=(VMEM,) * 2,
-        scratch_shapes=[scratch(5, 48, 256), scratch(2, 2, 40, 256), scratch(8, 16, 128)],
-    )(gathered, packed, lo, hi)
+        scratch_shapes=[scratch(5, 48, 256), scratch(2, 40, 256), scratch(8, 16, 128)],
+        compiler_params=limit(8),
+    )(near(gathered), near(packed), near(lo), near(hi))
     pieces = [from_group_behind(pred, ds) for ds in (-1, 0, 1)]
     top = lax.all_gather(jnp.stack(pieces), "m", axis=0, tiled=False)
     return pl.pallas_call(
         final_kernel,
-        out_shape=struct(16, 2, 32, 512),
-        in_specs=[SMEM] + [VMEM] * 11,
-        out_specs=ANY,
+        out_shape=jax.ShapeDtypeStruct((16, 2, 32, 512), F32),
+        in_specs=[VMEM] * 11,
+        out_specs=HBM,
         scratch_shapes=[
-            scratch(5, 48, 256), scratch(6, 24, 128), scratch(4, 2, 24, 128),
+            scratch(5, 48, 256), scratch(6, 24, 128), scratch(2, 2, 24, 128),
             scratch(9, 2, 40, 256), scratch(50, 48, 128), scratch(2, 2, 2, 48, 512),
             scratch(2, 2, 24, 256), scratch(16, 2, 32, 512), pltpu.SemaphoreType.DMA((16,)),
         ],
-    )(where, gathered, top, pred, mid_coef, packed, lo, hi, a01, a2, w2, fine)
+        compiler_params=limit(18),
+    )(*[near(x) for x in (gathered, top, pred, mid_coef, packed, lo, hi, a01, a2, w2, fine)])
 
 
 def solution(mesh):

time: 88.6 us -> 76.9 us (0.87)
  Pallas kernels: 19.6 us -> 11.9 us
  local copies, waits for them, and re-layouts: 1.56 us -> 0.02 us
  blocking collectives: 25.7 us -> 24.7 us
    pallas_call x1, Pallas kernels: 6.26 us -> 4.12 us  [local(): pl.pallas_call(final_kernel, out_shape=jax.ShapeDtypeStruct((16, 2, 32, 5...]
    pallas_call x1, Pallas kernels: 2.78 us -> 0.8 us  [local(): pl.pallas_call(mid_kernel, out_shape=(struct(4, 8, 128), struct(6, 40, 25...]
    pallas_call x1, Pallas kernels: 7.46 us -> 5.53 us  [local(): pl.pallas_call(fine_kernel, out_shape=(struct(2, 2, 60, 512), struct(2, 3...]
    pallas_call x1, Pallas kernels: 3.11 us -> 1.48 us  [local(): pl.pallas_call(pack_kernel, out_shape=(struct(9, 32, 512), struct(9, 16,...]
    unnamed x12 -> x0, local copies, waits for them, and re-layouts: 1.54 us -> none
  transfers between devices with their start and end apart: 9 -> 9, of which waited for: 5 -> 5; matrix products, arithmetic and copies ran while one was open for 0% -> 0% of each run, Pallas kernels for 3% -> 1%
where the time goes in v3:
time: 76.9 us; the launch traced here: 76.6 us
  starting transfers between devices  26.9 us (35%)
  blocking collectives  24.7 us (32%)
  waiting for transfers between devices  12.9 us (17%)
  Pallas kernels  11.9 us (15%)
    ppermute x6, starting transfers between devices, send(): return lax.ppermute(x, AXES, pairs)  18.9 us
    all_gather x1, blocking collectives, local(): top = lax.all_gather(jnp.stack(pieces), 'm', axis=0, tiled=False)  13.5 us
    ppermute x6, waiting for transfers between devices, send(): return lax.ppermute(x, AXES, pairs)  12.1 us
    all_gather x1, blocking collectives, local(): gathered = lax.all_gather(window, 'm', axis=0, tiled=False)  11.2 us
    ppermute x3, starting transfers between devices, from_group_behind(): return lax.ppermute(x, AXES, pairs)  8.02 us
    pallas_call x1, Pallas kernels, local(): pl.pallas_call(fine_kernel, out_shape=(struct(2, 2, 60, 512), struct(2, 3...  5.53 us
    pallas_call x1, Pallas kernels, local(): pl.pallas_call(final_kernel, out_shape=jax.ShapeDtypeStruct((16, 2, 32, 5...  4.12 us
  transfers between devices with their start and end apart: 9, of which 5 were waited for; matrix products, arithmetic and copies ran while one was open for 0% of the time, Pallas kernels for 1%

profile of v3, /device:TPU:81, one launch (start us, length us, event | category | flops | bytes accessed | tf_op | source)
XLA Modules:
  0.0 76.6 jit_solution(16056744061781468005)
XLA Ops:
  0.0 1.5 %shard_map.64 = (f32[9,32,512]{2,1,0:T(8,128)S(1)}, f32[9,16,512]{2,1,0:T(8,128)S(1)}, f32[9,16,512]{2,1,0:T(8,128)S(1)}) custom-call(f32[2,32,512]{2,1,0:T(8,128)} %initial_ref.1, f32[16,2,32,512]{3,2,1,0:T(8,128)} %guess_ref.1, f32[2,32,512]{2,1,0:T(8,128)} %kappa_ref.1, f32[32,512]{1,0:T(8,128)} %feed_ref.1, f32[32,512]{1,0:T(8,128)} %kill_ref.1, ...), custom_call_target="tpu_custom_call" | custom-call | tf_op jit(solution)/shard_map/pallas_call | solution.py:541
  1.5 3.1 %collective-permute-start = (f32[9,16,512]{2,1,0:T(8,128)S(1)}, f32[9,16,512]{2,1,0:T(8,128)S(1)}, u32[]{:S(2)}, u32[]{:S(2)}) collective-permute-start(f32[9,16,512]{2,1,0:T(8,128)S(1)} %get-tuple-element.19), channel_id=1, source_target_pairs={{0,1},{1,2},{2,3},{3,4},{4,5},{5,6},{6,7},{7,8},{8,9},{9,10},{10,1... | collective-permute-start | bytes 884744 | tf_op jit(solution)/shard_map/ppermute | solution.py:527
  4.6 4.3 %collective-permute-start.1 = (f32[9,16,512]{2,1,0:T(8,128)S(1)}, f32[9,16,512]{2,1,0:T(8,128)S(1)}, u32[]{:S(2)}, u32[]{:S(2)}) collective-permute-start(f32[9,16,512]{2,1,0:T(8,128)S(1)} %get-tuple-element.20), channel_id=1, source_target_pairs={{1,0},{2,1},{3,2},{4,3},{5,4},{6,5},{7,6},{8,7},{9,8},{10,9},{11,1... | collective-permute-start | bytes 884744 | tf_op jit(solution)/shard_map/ppermute | solution.py:527
  8.9 4.5 %collective-permute-done.lo_ref = f32[9,16,512]{2,1,0:T(8,128)S(1)} collective-permute-done((f32[9,16,512]{2,1,0:T(8,128)S(1)}, f32[9,16,512]{2,1,0:T(8,128)S(1)}, u32[]{:S(2)}, u32[]{:S(2)}) %collective-permute-start) | collective-permute-done | bytes 294944 | tf_op jit(solution)/shard_map/ppermute | solution.py:527
  13.4 0.9 %collective-permute-done.1.hi_ref = f32[9,16,512]{2,1,0:T(8,128)S(1)} collective-permute-done((f32[9,16,512]{2,1,0:T(8,128)S(1)}, f32[9,16,512]{2,1,0:T(8,128)S(1)}, u32[]{:S(2)}, u32[]{:S(2)}) %collective-permute-start.1) | collective-permute-done | bytes 294944 | tf_op jit(solution)/shard_map/ppermute | solution.py:527
  14.3 5.5 %shard_map.65 = (f32[2,2,60,512]{3,2,1,0:T(8,128)S(1)}, f32[2,32,512]{2,1,0:T(8,128)S(1)}, f32[2,16,256]{2,1,0:T(8,128)S(1)}, f32[6,16,256]{2,1,0:T(8,128)S(1)},...) custom-call(f32[9,32,512]{2,1,0:T(8,128)S(1)} %get-tuple-element.18.own_ref, ...), custom_call_target="tpu_custom_call" | custom-call | tf_op jit(solution)/shard_map/pallas_call | solution.py:551
  19.8 9.3 %collective-permute-start.4 = (f32[11,16,256]{2,1,0:T(8,128)S(1)}, f32[11,16,256]{2,1,0:T(8,128)S(1)}, u32[]{:S(2)}, u32[]{:S(2)}) collective-permute-start(f32[11,16,256]{2,1,0:T(8,128)S(1)} %get-tuple-element.21.own_ref), channel_id=1, source_target_pairs={{1,16},{2,17},{3,18},{4,19},{5,20},{6,21},{7,22},{8,23},{9,24},{10... | collective-permute-start | bytes 540680 | tf_op jit(solution)/shard_map/ppermute | solution.py:527
  29.1 1.9 %collective-permute-start.2 = (f32[11,16,256]{2,1,0:T(8,128)S(1)}, f32[11,16,256]{2,1,0:T(8,128)S(1)}, u32[]{:S(2)}, u32[]{:S(2)}) collective-permute-start(f32[11,16,256]{2,1,0:T(8,128)S(1)} %get-tuple-element.21.own_ref), channel_id=1, source_target_pairs={{0,17},{1,18},{2,19},{3,20},{4,21},{5,22},{6,23},{7,24},{8,25},{9,... | collective-permute-start | bytes 540680 | tf_op jit(solution)/shard_map/ppermute | solution.py:527
  31.0 0.3 collective-permute-start.3
  31.3 0.2 collective-permute-done.4.hi_ref
  31.5 6.5 %collective-permute-done.2.lo_ref = f32[11,16,256]{2,1,0:T(8,128)S(1)} collective-permute-done((f32[11,16,256]{2,1,0:T(8,128)S(1)}, f32[11,16,256]{2,1,0:T(8,128)S(1)}, u32[]{:S(2)}, u32[]{:S(2)}) %collective-permute-start.2) | collective-permute-done | bytes 180256 | tf_op jit(solution)/shard_map/ppermute | solution.py:527
  38.0 0.0 collective-permute-done.3
  38.1 11.2 %all-gather = f32[24,40,256]{2,1,0:T(8,128)S(1)} all-gather(f32[6,40,256]{2,1,0:T(8,128)S(1)} %pad_maximum_fusion), channel_id=2, replica_groups=mesh['k'=4,'m'=4,'space'=16] {'m'}, dimensions={0}, use_global_device_ids=true | all-gather | bytes 1228800 | tf_op jit(solution)/shard_map/all_gather | solution.py:570
  49.3 0.0 collective-permute-start.8
  49.3 0.8 %shard_map.66 = (f32[4,8,128]{2,1,0:T(8,128)S(1)}, f32[6,40,256]{2,1,0:T(8,128)S(1)}) custom-call(f32[4,6,40,256]{3,2,1,0:T(8,128)S(1)} %bitcast.5, f32[11,16,256]{2,1,0:T(8,128)S(1)} %get-tuple-element.21.own_ref, f32[11,16,256]{2,1,0:T(8,128)S(1)} %collective-permute-done.2.lo_ref, f32[11,16,256]{2,1,0:T(8,128)S(1)} %collective-permute-done.4.hi_ref), custom_call_target="tpu_custom_call" | custom-call | tf_op jit(solution)/shard_map/pallas_call | solution.py:573
  50.1 5.4 %collective-permute-start.7 = (f32[4,8,128]{2,1,0:T(8,128)S(1)}, f32[4,8,128]{2,1,0:T(8,128)S(1)}, u32[]{:S(2)}, u32[]{:S(2)}) collective-permute-start(f32[4,8,128]{2,1,0:T(8,128)S(1)} %get-tuple-element.25.pred_ref), channel_id=1, source_target_pairs={{1,64},{2,65},{3,66},{4,67},{5,68},{6,69},{7,70},{8,71},{9,72},{10... | collective-permute-start | bytes 49160 | tf_op jit(solution)/shard_map/ppermute | solution.py:537
  55.5 1.3 %collective-permute-start.6 = (f32[4,8,128]{2,1,0:T(8,128)S(1)}, f32[4,8,128]{2,1,0:T(8,128)S(1)}, u32[]{:S(2)}, u32[]{:S(2)}) collective-permute-start(f32[4,8,128]{2,1,0:T(8,128)S(1)} %get-tuple-element.25.pred_ref), channel_id=1, source_target_pairs={{0,64},{1,65},{2,66},{3,67},{4,68},{5,69},{6,70},{7,71},{8,72},{9,... | collective-permute-start | bytes 49160 | tf_op jit(solution)/shard_map/ppermute | solution.py:537
  56.8 1.3 %collective-permute-start.5 = (f32[4,8,128]{2,1,0:T(8,128)S(1)}, f32[4,8,128]{2,1,0:T(8,128)S(1)}, u32[]{:S(2)}, u32[]{:S(2)}) collective-permute-start(f32[4,8,128]{2,1,0:T(8,128)S(1)} %get-tuple-element.25.pred_ref), channel_id=1, source_target_pairs={{0,65},{1,66},{2,67},{3,68},{4,69},{5,70},{6,71},{7,72},{8,73},{9,... | collective-permute-start | bytes 49160 | tf_op jit(solution)/shard_map/ppermute | solution.py:537
  58.1 0.0 collective-permute-done.7
  58.1 0.0 collective-permute-done.6
  58.1 0.8 %collective-permute-done.5 = f32[4,8,128]{2,1,0:T(8,128)S(1)} collective-permute-done((f32[4,8,128]{2,1,0:T(8,128)S(1)}, f32[4,8,128]{2,1,0:T(8,128)S(1)}, u32[]{:S(2)}, u32[]{:S(2)}) %collective-permute-start.5) | collective-permute-done | bytes 16416 | tf_op jit(solution)/shard_map/ppermute | solution.py:537
  59.0 13.5 %all-gather.1 = f32[12,4,8,128]{3,2,1,0:T(8,128)S(1)} all-gather(f32[3,4,8,128]{3,2,1,0:T(8,128)S(1)} %pad_maximum_fusion.1), channel_id=3, replica_groups=mesh['k'=4,'m'=4,'space'=16] {'m'}, dimensions={0}, use_global_device_ids=true | all-gather | bytes 245760 | tf_op jit(solution)/shard_map/all_gather | solution.py:582
  72.5 0.0 collective-permute-done.8.a01_ref
  72.5 4.1 %shard_map.67 = f32[16,2,32,512]{3,2,1,0:T(8,128)} custom-call(f32[4,6,40,256]{3,2,1,0:T(8,128)S(1)} %bitcast.6, f32[4,3,4,8,128]{4,3,2,1,0:T(8,128)S(1)} %bitcast.7, f32[4,8,128]{2,1,0:T(8,128)S(1)} %get-tuple-element.25.pred_ref, f32[6,40,256]{2,1,0:T(8,128)S(1)} %get-tuple-element.26.mid_coef, f32[11,16,256]{2,1,0:T(8,128)S(1)} %get-tuple-element.21.own_ref, ...), custom_call_target="tpu_custom_call" | custom-call | tf_op jit(solution)/shard_map/pallas_call | solution.py:583
  (4 shorter events, 0.1 us)
Async XLA Ops:
  1.5 11.9 %collective-permute-start = (f32[9,16,512]{2,1,0:T(8,128)S(1)}, f32[9,16,512]{2,1,0:T(8,128)S(1)}, u32[]{:S(2)}, u32[]{:S(2)}) collective-permute-start(f32[9,16,512]{2,1,0:T(8,128)S(1)} %get-tuple-element.19), channel_id=1, source_target_pairs={{0,1},{1,2},{2,3},{3,4},{4,5},{5,6},{6,7},{7,8},{8,9},{9,10},{10,1... | collective-permute-start | bytes 884744 | tf_op jit(solution)/shard_map/ppermute | solution.py:527
  4.6 9.7 %collective-permute-start.1 = (f32[9,16,512]{2,1,0:T(8,128)S(1)}, f32[9,16,512]{2,1,0:T(8,128)S(1)}, u32[]{:S(2)}, u32[]{:S(2)}) collective-permute-start(f32[9,16,512]{2,1,0:T(8,128)S(1)} %get-tuple-element.20), channel_id=1, source_target_pairs={{1,0},{2,1},{3,2},{4,3},{5,4},{6,5},{7,6},{8,7},{9,8},{10,9},{11,1... | collective-permute-start | bytes 884744 | tf_op jit(solution)/shard_map/ppermute | solution.py:527
  19.8 11.7 %collective-permute-start.4 = (f32[11,16,256]{2,1,0:T(8,128)S(1)}, f32[11,16,256]{2,1,0:T(8,128)S(1)}, u32[]{:S(2)}, u32[]{:S(2)}) collective-permute-start(f32[11,16,256]{2,1,0:T(8,128)S(1)} %get-tuple-element.21.own_ref), channel_id=1, source_target_pairs={{1,16},{2,17},{3,18},{4,19},{5,20},{6,21},{7,22},{8,23},{9,24},{10... | collective-permute-start | bytes 540680 | tf_op jit(solution)/shard_map/ppermute | solution.py:527
  29.1 8.9 %collective-permute-start.2 = (f32[11,16,256]{2,1,0:T(8,128)S(1)}, f32[11,16,256]{2,1,0:T(8,128)S(1)}, u32[]{:S(2)}, u32[]{:S(2)}) collective-permute-start(f32[11,16,256]{2,1,0:T(8,128)S(1)} %get-tuple-element.21.own_ref), channel_id=1, source_target_pairs={{0,17},{1,18},{2,19},{3,20},{4,21},{5,22},{6,23},{7,24},{8,25},{9,... | collective-permute-start | bytes 540680 | tf_op jit(solution)/shard_map/ppermute | solution.py:527
  31.0 7.0 %collective-permute-start.3 = (f32[6,16,256]{2,1,0:T(8,128)S(1)}, f32[6,16,256]{2,1,0:T(8,128)S(1)}, u32[]{:S(2)}, u32[]{:S(2)}) collective-permute-start(f32[6,16,256]{2,1,0:T(8,128)S(1)} %get-tuple-element.22), channel_id=1, source_target_pairs={{0,16},{1,17},{2,18},{3,19},{4,20},{5,21},{6,22},{7,23},{8,24},{9,... | collective-permute-start | bytes 294920 | tf_op jit(solution)/shard_map/ppermute | solution.py:527
  49.3 23.2 %collective-permute-start.8 = (f32[2,2,60,512]{3,2,1,0:T(8,128)S(1)}, f32[2,2,60,512]{3,2,1,0:T(8,128)S(1)}, u32[]{:S(2)}, u32[]{:S(2)}) collective-permute-start(f32[2,2,60,512]{3,2,1,0:T(8,128)S(1)} %get-tuple-element.27), channel_id=1, source_target_pairs={{0,16},{1,17},{2,18},{3,19},{4,20},{5,21},{6,22},{7,23},{8,24},{9,... | collective-permute-start | bytes 1474568 | tf_op jit(solution)/shard_map/ppermute | solution.py:527
  50.1 8.1 %collective-permute-start.7 = (f32[4,8,128]{2,1,0:T(8,128)S(1)}, f32[4,8,128]{2,1,0:T(8,128)S(1)}, u32[]{:S(2)}, u32[]{:S(2)}) collective-permute-start(f32[4,8,128]{2,1,0:T(8,128)S(1)} %get-tuple-element.25.pred_ref), channel_id=1, source_target_pairs={{1,64},{2,65},{3,66},{4,67},{5,68},{6,69},{7,70},{8,71},{9,72},{10... | collective-permute-start | bytes 49160 | tf_op jit(solution)/shard_map/ppermute | solution.py:537
  55.5 2.6 %collective-permute-start.6 = (f32[4,8,128]{2,1,0:T(8,128)S(1)}, f32[4,8,128]{2,1,0:T(8,128)S(1)}, u32[]{:S(2)}, u32[]{:S(2)}) collective-permute-start(f32[4,8,128]{2,1,0:T(8,128)S(1)} %get-tuple-element.25.pred_ref), channel_id=1, source_target_pairs={{0,64},{1,65},{2,66},{3,67},{4,68},{5,69},{6,70},{7,71},{8,72},{9,... | collective-permute-start | bytes 49160 | tf_op jit(solution)/shard_map/ppermute | solution.py:537
  56.8 2.1 %collective-permute-start.5 = (f32[4,8,128]{2,1,0:T(8,128)S(1)}, f32[4,8,128]{2,1,0:T(8,128)S(1)}, u32[]{:S(2)}, u32[]{:S(2)}) collective-permute-start(f32[4,8,128]{2,1,0:T(8,128)S(1)} %get-tuple-element.25.pred_ref), channel_id=1, source_target_pairs={{0,65},{1,66},{2,67},{3,68},{4,69},{5,70},{6,71},{7,72},{8,73},{9,... | collective-permute-start | bytes 49160 | tf_op jit(solution)/shard_map/ppermute | solution.py:537

commit v4 on v3

--- a/solution.py
+++ b/solution.py
@@ -395,13 +395,13 @@
     def kept(slot):
         return [[yz[slot, q, block(i)] for q in range(2)] for i in range(3)]
 
-    values = [[top_ref[2, i, q] for q in range(2)] for i in range(3)]
+    values = [[top_ref[RECEIVER[2], i, q] for q in range(2)] for i in range(3)]
     for back in (1, 0):
         follows = jnp.where(k - 1 - back > 0, F32(1.0), F32(0.0))
-        other = low_step([[top_ref[back, i, 2 + q] for q in range(2)] for i in range(3)])
+        other = low_step([[top_ref[RECEIVER[back], i, 2 + q] for q in range(2)] for i in range(3)])
         values = low_step(values)
         values = [
-            [top_ref[back, i, q] + follows * (values[i][q] - other[i][q]) for q in range(2)]
+            [top_ref[RECEIVER[back], i, q] + follows * (values[i][q] - other[i][q]) for q in range(2)]
             for i in range(3)
         ]
     for i in range(3):
@@ -527,13 +527,18 @@
     return lax.ppermute(x, AXES, pairs)
 
 
+SENDER = (3, 2, 1)
+RECEIVER = (1, 0, 3)
+
+
 def from_group_behind(x, ds):
     pairs = []
     for k in range(GROUP):
-        for m in range(k):
+        for back in range(k):
             for s in range(N_SPACE):
                 if 0 <= s + ds < N_SPACE:
-                    pairs.append((device(4 * (k - 1 - m) + m, s + ds), device(4 * k + m, s)))
+                    source = device(4 * (k - 1 - back) + SENDER[back], s + ds)
+                    pairs.append((source, device(4 * k + RECEIVER[back], s)))
     return lax.ppermute(x, AXES, pairs)
 
 

time: 76.9 us -> 72.7 us (0.945)
  the two profiles are of different devices: /device:TPU:81 before, /device:TPU:145 now
where the time goes in v4:
time: 72.7 us; the launch traced here: 72.5 us
  starting transfers between devices  22.9 us (31%)
  waiting for transfers between devices  21.4 us (29%)
  blocking collectives  16.2 us (22%)
  Pallas kernels  11.9 us (16%)
    ppermute x6, starting transfers between devices, send(): return lax.ppermute(x, AXES, pairs)  19 us
    ppermute x6, waiting for transfers between devices, send(): return lax.ppermute(x, AXES, pairs)  14 us
    all_gather x1, blocking collectives, local(): gathered = lax.all_gather(window, 'm', axis=0, tiled=False)  8.57 us
    all_gather x1, blocking collectives, local(): top = lax.all_gather(jnp.stack(pieces), 'm', axis=0, tiled=False)  7.6 us
    ppermute x3, waiting for transfers between devices, from_group_behind(): return lax.ppermute(x, AXES, pairs)  7.4 us
    pallas_call x1, Pallas kernels, local(): pl.pallas_call(fine_kernel, out_shape=(struct(2, 2, 60, 512), struct(2, 3...  5.53 us
    pallas_call x1, Pallas kernels, local(): pl.pallas_call(final_kernel, out_shape=jax.ShapeDtypeStruct((16, 2, 32, 5...  4.12 us
    ppermute x3, starting transfers between devices, from_group_behind(): return lax.ppermute(x, AXES, pairs)  3.88 us
  transfers between devices with their start and end apart: 9, of which 7 were waited for; matrix products, arithmetic and copies ran while one was open for 0% of the time, Pallas kernels for 1%

profile of v4, /device:TPU:145, one launch (start us, length us, event | category | flops | bytes accessed | tf_op | source)
XLA Modules:
  0.0 72.5 jit_solution(6368651380935053816)
XLA Ops:
  0.0 1.5 %shard_map.64 = (f32[9,32,512]{2,1,0:T(8,128)S(1)}, f32[9,16,512]{2,1,0:T(8,128)S(1)}, f32[9,16,512]{2,1,0:T(8,128)S(1)}) custom-call(f32[2,32,512]{2,1,0:T(8,128)} %initial_ref.1, f32[16,2,32,512]{3,2,1,0:T(8,128)} %guess_ref.1, f32[2,32,512]{2,1,0:T(8,128)} %kappa_ref.1, f32[32,512]{1,0:T(8,128)} %feed_ref.1, f32[32,512]{1,0:T(8,128)} %kill_ref.1, ...), custom_call_target="tpu_custom_call" | custom-call | tf_op jit(solution)/shard_map/pallas_call | solution.py:546
  1.5 3.1 %collective-permute-start = (f32[9,16,512]{2,1,0:T(8,128)S(1)}, f32[9,16,512]{2,1,0:T(8,128)S(1)}, u32[]{:S(2)}, u32[]{:S(2)}) collective-permute-start(f32[9,16,512]{2,1,0:T(8,128)S(1)} %get-tuple-element.19), channel_id=1, source_target_pairs={{0,1},{1,2},{2,3},{3,4},{4,5},{5,6},{6,7},{7,8},{8,9},{9,10},{10,1... | collective-permute-start | bytes 884744 | tf_op jit(solution)/shard_map/ppermute | solution.py:527
  4.6 4.3 %collective-permute-start.1 = (f32[9,16,512]{2,1,0:T(8,128)S(1)}, f32[9,16,512]{2,1,0:T(8,128)S(1)}, u32[]{:S(2)}, u32[]{:S(2)}) collective-permute-start(f32[9,16,512]{2,1,0:T(8,128)S(1)} %get-tuple-element.20), channel_id=1, source_target_pairs={{1,0},{2,1},{3,2},{4,3},{5,4},{6,5},{7,6},{8,7},{9,8},{10,9},{11,1... | collective-permute-start | bytes 884744 | tf_op jit(solution)/shard_map/ppermute | solution.py:527
  8.9 4.5 %collective-permute-done.lo_ref = f32[9,16,512]{2,1,0:T(8,128)S(1)} collective-permute-done((f32[9,16,512]{2,1,0:T(8,128)S(1)}, f32[9,16,512]{2,1,0:T(8,128)S(1)}, u32[]{:S(2)}, u32[]{:S(2)}) %collective-permute-start) | collective-permute-done | bytes 294944 | tf_op jit(solution)/shard_map/ppermute | solution.py:527
  13.4 0.9 %collective-permute-done.1.hi_ref = f32[9,16,512]{2,1,0:T(8,128)S(1)} collective-permute-done((f32[9,16,512]{2,1,0:T(8,128)S(1)}, f32[9,16,512]{2,1,0:T(8,128)S(1)}, u32[]{:S(2)}, u32[]{:S(2)}) %collective-permute-start.1) | collective-permute-done | bytes 294944 | tf_op jit(solution)/shard_map/ppermute | solution.py:527
  14.3 5.5 %shard_map.65 = (f32[2,2,60,512]{3,2,1,0:T(8,128)S(1)}, f32[2,32,512]{2,1,0:T(8,128)S(1)}, f32[2,16,256]{2,1,0:T(8,128)S(1)}, f32[6,16,256]{2,1,0:T(8,128)S(1)},...) custom-call(f32[9,32,512]{2,1,0:T(8,128)S(1)} %get-tuple-element.18.own_ref, ...), custom_call_target="tpu_custom_call" | custom-call | tf_op jit(solution)/shard_map/pallas_call | solution.py:556
  19.8 8.4 %collective-permute-start.4 = (f32[11,16,256]{2,1,0:T(8,128)S(1)}, f32[11,16,256]{2,1,0:T(8,128)S(1)}, u32[]{:S(2)}, u32[]{:S(2)}) collective-permute-start(f32[11,16,256]{2,1,0:T(8,128)S(1)} %get-tuple-element.21.own_ref), channel_id=1, source_target_pairs={{1,16},{2,17},{3,18},{4,19},{5,20},{6,21},{7,22},{8,23},{9,24},{10... | collective-permute-start | bytes 540680 | tf_op jit(solution)/shard_map/ppermute | solution.py:527
  28.2 1.9 %collective-permute-start.2 = (f32[11,16,256]{2,1,0:T(8,128)S(1)}, f32[11,16,256]{2,1,0:T(8,128)S(1)}, u32[]{:S(2)}, u32[]{:S(2)}) collective-permute-start(f32[11,16,256]{2,1,0:T(8,128)S(1)} %get-tuple-element.21.own_ref), channel_id=1, source_target_pairs={{0,17},{1,18},{2,19},{3,20},{4,21},{5,22},{6,23},{7,24},{8,25},{9,... | collective-permute-start | bytes 540680 | tf_op jit(solution)/shard_map/ppermute | solution.py:527
  30.1 0.0 collective-permute-start.3
  30.2 0.5 collective-permute-done.4.hi_ref
  30.6 8.1 %collective-permute-done.2.lo_ref = f32[11,16,256]{2,1,0:T(8,128)S(1)} collective-permute-done((f32[11,16,256]{2,1,0:T(8,128)S(1)}, f32[11,16,256]{2,1,0:T(8,128)S(1)}, u32[]{:S(2)}, u32[]{:S(2)}) %collective-permute-start.2) | collective-permute-done | bytes 180256 | tf_op jit(solution)/shard_map/ppermute | solution.py:527
  38.7 0.0 collective-permute-done.3
  38.8 8.6 %all-gather = f32[24,40,256]{2,1,0:T(8,128)S(1)} all-gather(f32[6,40,256]{2,1,0:T(8,128)S(1)} %pad_maximum_fusion), channel_id=2, replica_groups=mesh['k'=4,'m'=4,'space'=16] {'m'}, dimensions={0}, use_global_device_ids=true | all-gather | bytes 1228800 | tf_op jit(solution)/shard_map/all_gather | solution.py:575
  47.3 1.3 %collective-permute-start.8 = (f32[2,2,60,512]{3,2,1,0:T(8,128)S(1)}, f32[2,2,60,512]{3,2,1,0:T(8,128)S(1)}, u32[]{:S(2)}, u32[]{:S(2)}) collective-permute-start(f32[2,2,60,512]{3,2,1,0:T(8,128)S(1)} %get-tuple-element.27), channel_id=1, source_target_pairs={{0,16},{1,17},{2,18},{3,19},{4,20},{5,21},{6,22},{7,23},{8,24},{9,... | collective-permute-start | bytes 1474568 | tf_op jit(solution)/shard_map/ppermute | solution.py:527
  48.6 0.8 %shard_map.66 = (f32[4,8,128]{2,1,0:T(8,128)S(1)}, f32[6,40,256]{2,1,0:T(8,128)S(1)}) custom-call(f32[4,6,40,256]{3,2,1,0:T(8,128)S(1)} %bitcast.5, f32[11,16,256]{2,1,0:T(8,128)S(1)} %get-tuple-element.21.own_ref, f32[11,16,256]{2,1,0:T(8,128)S(1)} %collective-permute-done.2.lo_ref, f32[11,16,256]{2,1,0:T(8,128)S(1)} %collective-permute-done.4.hi_ref), custom_call_target="tpu_custom_call" | custom-call | tf_op jit(solution)/shard_map/pallas_call | solution.py:578
  49.4 1.3 %collective-permute-start.7 = (f32[4,8,128]{2,1,0:T(8,128)S(1)}, f32[4,8,128]{2,1,0:T(8,128)S(1)}, u32[]{:S(2)}, u32[]{:S(2)}) collective-permute-start(f32[4,8,128]{2,1,0:T(8,128)S(1)} %get-tuple-element.25.pred_ref), channel_id=1, source_target_pairs={{49,80},{50,81},{51,82},{52,83},{53,84},{54,85},{55,86},{56,87},{5... | collective-permute-start | bytes 49160 | tf_op jit(solution)/shard_map/ppermute | solution.py:542
  50.7 1.3 %collective-permute-start.6 = (f32[4,8,128]{2,1,0:T(8,128)S(1)}, f32[4,8,128]{2,1,0:T(8,128)S(1)}, u32[]{:S(2)}, u32[]{:S(2)}) collective-permute-start(f32[4,8,128]{2,1,0:T(8,128)S(1)} %get-tuple-element.25.pred_ref), channel_id=1, source_target_pairs={{48,80},{49,81},{50,82},{51,83},{52,84},{53,85},{54,86},{55,87},{5... | collective-permute-start | bytes 49160 | tf_op jit(solution)/shard_map/ppermute | solution.py:542
  52.0 1.3 %collective-permute-start.5 = (f32[4,8,128]{2,1,0:T(8,128)S(1)}, f32[4,8,128]{2,1,0:T(8,128)S(1)}, u32[]{:S(2)}, u32[]{:S(2)}) collective-permute-start(f32[4,8,128]{2,1,0:T(8,128)S(1)} %get-tuple-element.25.pred_ref), channel_id=1, source_target_pairs={{48,81},{49,82},{50,83},{51,84},{52,85},{53,86},{54,87},{55,88},{5... | collective-permute-start | bytes 49160 | tf_op jit(solution)/shard_map/ppermute | solution.py:542
  53.3 2.7 %collective-permute-done.7 = f32[4,8,128]{2,1,0:T(8,128)S(1)} collective-permute-done((f32[4,8,128]{2,1,0:T(8,128)S(1)}, f32[4,8,128]{2,1,0:T(8,128)S(1)}, u32[]{:S(2)}, u32[]{:S(2)}) %collective-permute-start.7) | collective-permute-done | bytes 16416 | tf_op jit(solution)/shard_map/ppermute | solution.py:542
  56.0 2.2 %collective-permute-done.6 = f32[4,8,128]{2,1,0:T(8,128)S(1)} collective-permute-done((f32[4,8,128]{2,1,0:T(8,128)S(1)}, f32[4,8,128]{2,1,0:T(8,128)S(1)}, u32[]{:S(2)}, u32[]{:S(2)}) %collective-permute-start.6) | collective-permute-done | bytes 16416 | tf_op jit(solution)/shard_map/ppermute | solution.py:542
  58.2 2.5 %collective-permute-done.5 = f32[4,8,128]{2,1,0:T(8,128)S(1)} collective-permute-done((f32[4,8,128]{2,1,0:T(8,128)S(1)}, f32[4,8,128]{2,1,0:T(8,128)S(1)}, u32[]{:S(2)}, u32[]{:S(2)}) %collective-permute-start.5) | collective-permute-done | bytes 16416 | tf_op jit(solution)/shard_map/ppermute | solution.py:542
  60.7 7.6 %all-gather.1 = f32[12,4,8,128]{3,2,1,0:T(8,128)S(1)} all-gather(f32[3,4,8,128]{3,2,1,0:T(8,128)S(1)} %pad_maximum_fusion.1), channel_id=3, replica_groups=mesh['k'=4,'m'=4,'space'=16] {'m'}, dimensions={0}, use_global_device_ids=true | all-gather | bytes 245760 | tf_op jit(solution)/shard_map/all_gather | solution.py:587
  68.3 0.0 collective-permute-done.8.a01_ref
  68.3 4.1 %shard_map.67 = f32[16,2,32,512]{3,2,1,0:T(8,128)} custom-call(f32[4,6,40,256]{3,2,1,0:T(8,128)S(1)} %bitcast.6, f32[4,3,4,8,128]{4,3,2,1,0:T(8,128)S(1)} %bitcast.7, f32[4,8,128]{2,1,0:T(8,128)S(1)} %get-tuple-element.25.pred_ref, f32[6,40,256]{2,1,0:T(8,128)S(1)} %get-tuple-element.26.mid_coef, f32[11,16,256]{2,1,0:T(8,128)S(1)} %get-tuple-element.21.own_ref, ...), custom_call_target="tpu_custom_call" | custom-call | tf_op jit(solution)/shard_map/pallas_call | solution.py:588
  (4 shorter events, 0.1 us)
Async XLA Ops:
  1.5 11.9 %collective-permute-start = (f32[9,16,512]{2,1,0:T(8,128)S(1)}, f32[9,16,512]{2,1,0:T(8,128)S(1)}, u32[]{:S(2)}, u32[]{:S(2)}) collective-permute-start(f32[9,16,512]{2,1,0:T(8,128)S(1)} %get-tuple-element.19), channel_id=1, source_target_pairs={{0,1},{1,2},{2,3},{3,4},{4,5},{5,6},{6,7},{7,8},{8,9},{9,10},{10,1... | collective-permute-start | bytes 884744 | tf_op jit(solution)/shard_map/ppermute | solution.py:527
  4.6 9.7 %collective-permute-start.1 = (f32[9,16,512]{2,1,0:T(8,128)S(1)}, f32[9,16,512]{2,1,0:T(8,128)S(1)}, u32[]{:S(2)}, u32[]{:S(2)}) collective-permute-start(f32[9,16,512]{2,1,0:T(8,128)S(1)} %get-tuple-element.20), channel_id=1, source_target_pairs={{1,0},{2,1},{3,2},{4,3},{5,4},{6,5},{7,6},{8,7},{9,8},{10,9},{11,1... | collective-permute-start | bytes 884744 | tf_op jit(solution)/shard_map/ppermute | solution.py:527
  19.8 10.8 %collective-permute-start.4 = (f32[11,16,256]{2,1,0:T(8,128)S(1)}, f32[11,16,256]{2,1,0:T(8,128)S(1)}, u32[]{:S(2)}, u32[]{:S(2)}) collective-permute-start(f32[11,16,256]{2,1,0:T(8,128)S(1)} %get-tuple-element.21.own_ref), channel_id=1, source_target_pairs={{1,16},{2,17},{3,18},{4,19},{5,20},{6,21},{7,22},{8,23},{9,24},{10... | collective-permute-start | bytes 540680 | tf_op jit(solution)/shard_map/ppermute | solution.py:527
  28.2 10.5 %collective-permute-start.2 = (f32[11,16,256]{2,1,0:T(8,128)S(1)}, f32[11,16,256]{2,1,0:T(8,128)S(1)}, u32[]{:S(2)}, u32[]{:S(2)}) collective-permute-start(f32[11,16,256]{2,1,0:T(8,128)S(1)} %get-tuple-element.21.own_ref), channel_id=1, source_target_pairs={{0,17},{1,18},{2,19},{3,20},{4,21},{5,22},{6,23},{7,24},{8,25},{9,... | collective-permute-start | bytes 540680 | tf_op jit(solution)/shard_map/ppermute | solution.py:527
  30.1 8.6 %collective-permute-start.3 = (f32[6,16,256]{2,1,0:T(8,128)S(1)}, f32[6,16,256]{2,1,0:T(8,128)S(1)}, u32[]{:S(2)}, u32[]{:S(2)}) collective-permute-start(f32[6,16,256]{2,1,0:T(8,128)S(1)} %get-tuple-element.22), channel_id=1, source_target_pairs={{0,16},{1,17},{2,18},{3,19},{4,20},{5,21},{6,22},{7,23},{8,24},{9,... | collective-permute-start | bytes 294920 | tf_op jit(solution)/shard_map/ppermute | solution.py:527
  47.3 21.0 %collective-permute-start.8 = (f32[2,2,60,512]{3,2,1,0:T(8,128)S(1)}, f32[2,2,60,512]{3,2,1,0:T(8,128)S(1)}, u32[]{:S(2)}, u32[]{:S(2)}) collective-permute-start(f32[2,2,60,512]{3,2,1,0:T(8,128)S(1)} %get-tuple-element.27), channel_id=1, source_target_pairs={{0,16},{1,17},{2,18},{3,19},{4,20},{5,21},{6,22},{7,23},{8,24},{9,... | collective-permute-start | bytes 1474568 | tf_op jit(solution)/shard_map/ppermute | solution.py:527
  49.4 6.6 %collective-permute-start.7 = (f32[4,8,128]{2,1,0:T(8,128)S(1)}, f32[4,8,128]{2,1,0:T(8,128)S(1)}, u32[]{:S(2)}, u32[]{:S(2)}) collective-permute-start(f32[4,8,128]{2,1,0:T(8,128)S(1)} %get-tuple-element.25.pred_ref), channel_id=1, source_target_pairs={{49,80},{50,81},{51,82},{52,83},{53,84},{54,85},{55,86},{56,87},{5... | collective-permute-start | bytes 49160 | tf_op jit(solution)/shard_map/ppermute | solution.py:542
  50.7 7.5 %collective-permute-start.6 = (f32[4,8,128]{2,1,0:T(8,128)S(1)}, f32[4,8,128]{2,1,0:T(8,128)S(1)}, u32[]{:S(2)}, u32[]{:S(2)}) collective-permute-start(f32[4,8,128]{2,1,0:T(8,128)S(1)} %get-tuple-element.25.pred_ref), channel_id=1, source_target_pairs={{48,80},{49,81},{50,82},{51,83},{52,84},{53,85},{54,86},{55,87},{5... | collective-permute-start | bytes 49160 | tf_op jit(solution)/shard_map/ppermute | solution.py:542
  52.0 8.7 %collective-permute-start.5 = (f32[4,8,128]{2,1,0:T(8,128)S(1)}, f32[4,8,128]{2,1,0:T(8,128)S(1)}, u32[]{:S(2)}, u32[]{:S(2)}) collective-permute-start(f32[4,8,128]{2,1,0:T(8,128)S(1)} %get-tuple-element.25.pred_ref), channel_id=1, source_target_pairs={{48,81},{49,82},{50,83},{51,84},{52,85},{53,86},{54,87},{55,88},{5... | collective-permute-start | bytes 49160 | tf_op jit(solution)/shard_map/ppermute | solution.py:542

commit v5 on v4

--- a/solution.py
+++ b/solution.py
@@ -172,7 +172,7 @@
 
 def pack_kernel(
     initial_ref, guess_ref, kappa_ref, feed_ref, kill_ref, react_ref,
-    own_ref, low_ref, high_ref, sems,
+    own_ref, first_ref, second_ref, sems,
 ):
     last = GROUP * lax.axis_index("k") + lax.axis_index("m") == N_TM - 1
     count = [0]
@@ -182,57 +182,63 @@
         count[0] += 1
         return pltpu.make_async_copy(source, target, sems.at[n])
 
-    def copies(pick, place, many):
+    def copies(pick, place, many, top, bottom):
         out = []
         at = pl.ds(place, many) if many > 1 else place
-        for target, low, size in ((own_ref, 0, 32), (low_ref, 16, 16), (high_ref, 0, 16)):
+        for target, low, size in ((own_ref, 0, 32), (first_ref, top, 16), (second_ref, bottom, 16)):
             out.append(copy(pick(pl.ds(low, size)), target.at[at]))
         return out
 
-    plain = []
-    plain += copies(lambda r: guess_ref.at[7, :, r], 5, 2)
-    plain += copies(lambda r: kappa_ref.at[:, r], 0, 2)
-    plain += copies(lambda r: feed_ref.at[r], 2, 1)
-    plain += copies(lambda r: kill_ref.at[r], 3, 1)
-    plain += copies(lambda r: react_ref.at[r], 4, 1)
-    for c in plain:
-        c.start()
-    mark = count[0]
-    ends = copies(lambda r: guess_ref.at[15, :, r], 7, 2)
-    count[0] = mark
-    starts = copies(lambda r: initial_ref.at[:, r], 7, 2)
-
-    @pl.when(last)
-    def _():
-        for c in starts:
-            c.start()
-
-    @pl.when(jnp.logical_not(last))
-    def _():
-        for c in ends:
-            c.start()
-
-    for c in plain + ends:
+    def all_copies(top, bottom, pick_end):
+        count[0] = 0
+        out = copies(lambda r: guess_ref.at[7, :, r], 5, 2, top, bottom)
+        out += copies(lambda r: kappa_ref.at[:, r], 0, 2, top, bottom)
+        out += copies(lambda r: feed_ref.at[r], 2, 1, top, bottom)
+        out += copies(lambda r: kill_ref.at[r], 3, 1, top, bottom)
+        out += copies(lambda r: react_ref.at[r], 4, 1, top, bottom)
+        return out + copies(pick_end, 7, 2, top, bottom)
+
+    odd = is_odd()
+    for parity, top, bottom in ((odd, 16, 0), (jnp.logical_not(odd), 0, 16)):
+        for at_end, pick in (
+            (last, lambda r: initial_ref.at[:, r]),
+            (jnp.logical_not(last), lambda r: guess_ref.at[15, :, r]),
+        ):
+
+            @pl.when(jnp.logical_and(parity, at_end))
+            def _():
+                for c in all_copies(top, bottom, pick):
+                    c.start()
+
+    for c in all_copies(16, 0, lambda r: guess_ref.at[15, :, r]):
         c.wait()
 
 
 def fine_kernel(
-    own_ref, lo_ref, hi_ref,
+    own_ref, first_ref, second_ref,
     a01_ref, a2_ref, w2_ref, packed_ref, send_ref, fine_ref,
     s0, s1, raw, tall, mid_state, mid_coef, cells,
 ):
     rows = Rows(cells)
+    odd = is_odd()
+
+    def lo(f):
+        return jnp.where(odd, second_ref[f], first_ref[f])
+
+    def hi(f):
+        return jnp.where(odd, first_ref[f], second_ref[f])
+
     last = GROUP * lax.axis_index("k") + lax.axis_index("m") == N_TM - 1
     for c in range(2):
         for q in range(2):
             f = 5 + 2 * c + q
-            s0[c, q, 0:16] = lo_ref[f]
+            s0[c, q, 0:16] = lo(f)
             s0[c, q, 16:48] = own_ref[f]
-            s0[c, q, 48:64] = hi_ref[f]
+            s0[c, q, 48:64] = hi(f)
     for f in range(5):
-        raw[f, 0:16] = lo_ref[f]
+        raw[f, 0:16] = lo(f)
         raw[f, 16:48] = own_ref[f]
-        raw[f, 48:64] = hi_ref[f]
+        raw[f, 48:64] = hi(f)
     for i in range(8):
         r = block(i)
         parts = derived(*[raw[f, r] for f in range(5)])
@@ -267,9 +273,9 @@
         a2_ref[q] = s0[0, q, 16:48]
     stacked = [rows.coarsen(s0[0, q, 16:48]) for q in range(2)]
     for q in range(2):
-        s0[0, q, 0:16] = jnp.where(last, lo_ref[7 + q], s0[0, q, 0:16])
+        s0[0, q, 0:16] = jnp.where(last, lo(7 + q), s0[0, q, 0:16])
         s0[0, q, 16:48] = jnp.where(last, own_ref[7 + q], s0[0, q, 16:48])
-        s0[0, q, 48:64] = jnp.where(last, hi_ref[7 + q], s0[0, q, 48:64])
+        s0[0, q, 48:64] = jnp.where(last, hi(7 + q), s0[0, q, 48:64])
     for q in range(2):
         for c in range(2):
             a01_ref[c, q, 0:48] = s0[c, q, 8:56]
@@ -327,11 +333,17 @@
         advance(load, store, lambda i: [mid_coef[n, block(i)] for n in range(6)], (0, 4))
 
 
-def wide_mid_coefs(raw, coef_ref, lo_ref, hi_ref, mid_coef):
+def wide_raw(raw, coef_ref, first_ref, second_ref):
+    odd = is_odd()
     for f in range(5):
-        raw[f, 0:16] = lo_ref[6 + f]
+        first, second = first_ref[6 + f], second_ref[6 + f]
+        raw[f, 0:16] = jnp.where(odd, second, first)
         raw[f, 16:32] = coef_ref[6 + f]
-        raw[f, 32:48] = hi_ref[6 + f]
+        raw[f, 32:48] = jnp.where(odd, first, second)
+
+
+def wide_mid_coefs(raw, coef_ref, first_ref, second_ref, mid_coef):
+    wide_raw(raw, coef_ref, first_ref, second_ref)
     at = [raw[f, 4:44] for f in range(5)]
     parts = derived(2.0 * at[0], 2.0 * at[1], 8.0 * at[2], 8.0 * at[3], 8.0 * at[4])
     for n in range(6):
@@ -339,10 +351,10 @@
 
 
 def mid_kernel(
-    gathered_ref, own_ref, lo_ref, hi_ref, out_ref, coef_out_ref, raw, state, cells,
+    gathered_ref, own_ref, first_ref, second_ref, out_ref, coef_out_ref, raw, state, cells,
 ):
     rows = Rows(cells)
-    wide_mid_coefs(raw, own_ref, lo_ref, hi_ref, coef_out_ref)
+    wide_mid_coefs(raw, own_ref, first_ref, second_ref, coef_out_ref)
 
     def coeffs(i):
         return [coef_out_ref[n, block(i)] for n in range(6)]
@@ -369,17 +381,14 @@
 
 
 def final_kernel(
-    gathered_ref, top_ref, pred_ref, mid_coef, own_ref, lo_ref, hi_ref,
+    gathered_ref, top_ref, pred_ref, mid_coef, own_ref, first_ref, second_ref,
     a01_ref, a2_ref, w2_ref, fine_ref,
     result_ref,
     raw, low_coef, yz, series, cells, fine, w01, out_ref, sems,
 ):
     rows = Rows(cells)
     k, m = lax.axis_index("k"), lax.axis_index("m")
-    for f in range(5):
-        raw[f, 0:16] = lo_ref[6 + f]
-        raw[f, 16:32] = own_ref[6 + f]
-        raw[f, 32:48] = hi_ref[6 + f]
+    wide_raw(raw, own_ref, first_ref, second_ref)
     down = down_matrix(256)
     up_low = up_matrix(256)
     stacked = jnp.concatenate([rows.coarsen(raw[f]) for f in range(5)], axis=0)
@@ -517,14 +526,25 @@
     return t * N_SPACE + s
 
 
-def send(x, dt, ds):
+def shift(x):
     pairs = [
-        (device(t, s), device((t + dt) % N_TM, s + ds))
-        for t in range(N_TM)
-        for s in range(N_SPACE)
-        if 0 <= s + ds < N_SPACE
+        (device(t, s), device((t + 1) % N_TM, s)) for t in range(N_TM) for s in range(N_SPACE)
     ]
     return lax.ppermute(x, AXES, pairs)
+
+
+def swap(x, dt, first):
+    pairs = []
+    for t in range(N_TM):
+        for s in range(N_SPACE):
+            beside = s + 1 if (s % 2 == 1) == first else s - 1
+            if 0 <= beside < N_SPACE:
+                pairs.append((device(t, s), device((t + dt) % N_TM, beside)))
+    return lax.ppermute(x, AXES, pairs)
+
+
+def is_odd():
+    return lax.axis_index("space") % 2 == 1
 
 
 SENDER = (3, 2, 1)
@@ -543,7 +563,7 @@
 
 
 def local(initial, guess, kappa, feed, kill, react):
-    own, low_edge, high_edge = pl.pallas_call(
+    own, first_edge, second_edge = pl.pallas_call(
         pack_kernel,
         out_shape=(struct(9, 32, 512), struct(9, 16, 512), struct(9, 16, 512)),
         in_specs=[HBM] * 6,
@@ -551,8 +571,8 @@
         scratch_shapes=[pltpu.SemaphoreType.DMA((18,))],
         compiler_params=limit(4),
     )(*[far(x) for x in (initial, guess, kappa, feed, kill, react)])
-    lo = send(low_edge, 0, 1)
-    hi = send(high_edge, 0, -1)
+    first = swap(first_edge, 0, True)
+    second = swap(second_edge, 0, False)
     a01, a2, w2, held, packed, fine = pl.pallas_call(
         fine_kernel,
         out_shape=(
@@ -567,14 +587,22 @@
             scratch(60, 64, 128),
         ],
         compiler_params=limit(14),
-    )(near(own), near(lo), near(hi))
-    lo = send(packed, 1, 1)
-    hi = send(packed, 1, -1)
-    middle = send(held, 1, 0)
-    window = jnp.concatenate([lo[:6, 4:], middle, hi[:6, :12]], axis=1)
+    )(near(own), near(first), near(second))
+    first = swap(packed, 1, True)
+    second = swap(packed, 1, False)
+    middle = shift(held)
+    odd = is_odd()
+    window = jnp.concatenate(
+        [
+            jnp.where(odd, second[:6, 4:], first[:6, 4:]),
+            middle,
+            jnp.where(odd, first[:6, :12], second[:6, :12]),
+        ],
+        axis=1,
+    )
     gathered = lax.all_gather(window, "m", axis=0, tiled=False)
     gathered, a01 = lax.optimization_barrier((gathered, a01))
-    a01 = send(a01, 1, 0)
+    a01 = shift(a01)
     pred, mid_coef = pl.pallas_call(
         mid_kernel,
         out_shape=(struct(4, 8, 128), struct(6, 40, 256)),
@@ -582,7 +610,7 @@
         out_specs=(VMEM,) * 2,
         scratch_shapes=[scratch(5, 48, 256), scratch(2, 40, 256), scratch(8, 16, 128)],
         compiler_params=limit(8),
-    )(near(gathered), near(packed), near(lo), near(hi))
+    )(near(gathered), near(packed), near(first), near(second))
     pieces = [from_group_behind(pred, ds) for ds in (-1, 0, 1)]
     top = lax.all_gather(jnp.stack(pieces), "m", axis=0, tiled=False)
     return pl.pallas_call(
@@ -596,7 +624,7 @@
             scratch(2, 2, 24, 256), scratch(16, 2, 32, 512), pltpu.SemaphoreType.DMA((16,)),
         ],
         compiler_params=limit(18),
-    )(*[near(x) for x in (gathered, top, pred, mid_coef, packed, lo, hi, a01, a2, w2, fine)])
+    )(*[near(x) for x in (gathered, top, pred, mid_coef, packed, first, second, a01, a2, w2, fine)])
 
 
 def solution(mesh):

time: 72.7 us -> 67.7 us (0.931)
  the two profiles are of different devices: /device:TPU:145 before, /device:TPU:153 now
where the time goes in v5:
time: 67.7 us; the launch traced here: 67.5 us
  waiting for transfers between devices  22.2 us (33%)
  blocking collectives  17.2 us (25%)
  starting transfers between devices  16 us (24%)
  Pallas kernels  11.9 us (18%)
    ppermute x4, waiting for transfers between devices, swap(): return lax.ppermute(x, AXES, pairs)  14.6 us
    ppermute x4, starting transfers between devices, swap(): return lax.ppermute(x, AXES, pairs)  10.8 us
    all_gather x1, blocking collectives, local(): gathered = lax.all_gather(window, 'm', axis=0, tiled=False)  9.78 us
    ppermute x3, waiting for transfers between devices, from_group_behind(): return lax.ppermute(x, AXES, pairs)  7.52 us
    all_gather x1, blocking collectives, local(): top = lax.all_gather(jnp.stack(pieces), 'm', axis=0, tiled=False)  7.47 us
    pallas_call x1, Pallas kernels, local(): pl.pallas_call(fine_kernel, out_shape=(struct(2, 2, 60, 512), struct(2, 3...  5.54 us
    pallas_call x1, Pallas kernels, local(): pl.pallas_call(final_kernel, out_shape=jax.ShapeDtypeStruct((16, 2, 32, 5...  4.11 us
    ppermute x3, starting transfers between devices, from_group_behind(): return lax.ppermute(x, AXES, pairs)  3.88 us
  transfers between devices with their start and end apart: 9, of which 7 were waited for; matrix products, arithmetic and copies ran while one was open for 0% of the time, Pallas kernels for 1%

profile of v5, /device:TPU:153, one launch (start us, length us, event | category | flops | bytes accessed | tf_op | source)
XLA Modules:
  0.0 67.5 jit_solution(6050651717516025076)
XLA Ops:
  0.0 1.5 %shard_map.64 = (f32[9,32,512]{2,1,0:T(8,128)S(1)}, f32[9,16,512]{2,1,0:T(8,128)S(1)}, f32[9,16,512]{2,1,0:T(8,128)S(1)}) custom-call(f32[2,32,512]{2,1,0:T(8,128)} %initial_ref.1, f32[16,2,32,512]{3,2,1,0:T(8,128)} %guess_ref.1, f32[2,32,512]{2,1,0:T(8,128)} %kappa_ref.1, f32[32,512]{1,0:T(8,128)} %feed_ref.1, f32[32,512]{1,0:T(8,128)} %kill_ref.1, ...), custom_call_target="tpu_custom_call" | custom-call | tf_op jit(solution)/shard_map/pallas_call | solution.py:566
  1.5 4.6 %collective-permute-start = (f32[9,16,512]{2,1,0:T(8,128)S(1)}, f32[9,16,512]{2,1,0:T(8,128)S(1)}, u32[]{:S(2)}, u32[]{:S(2)}) collective-permute-start(f32[9,16,512]{2,1,0:T(8,128)S(1)} %get-tuple-element.19), channel_id=1, source_target_pairs={{1,2},{2,1},{3,4},{4,3},{5,6},{6,5},{7,8},{8,7},{9,10},{10,9},{11,... | collective-permute-start | bytes 884744 | tf_op jit(solution)/shard_map/ppermute | solution.py:543
  6.1 0.1 collective-permute-start.1
  6.2 7.2 %collective-permute-done.first_ref = f32[9,16,512]{2,1,0:T(8,128)S(1)} collective-permute-done((f32[9,16,512]{2,1,0:T(8,128)S(1)}, f32[9,16,512]{2,1,0:T(8,128)S(1)}, u32[]{:S(2)}, u32[]{:S(2)}) %collective-permute-start) | collective-permute-done | bytes 294944 | tf_op jit(solution)/shard_map/ppermute | solution.py:543
  13.4 0.4 collective-permute-done.1.second_ref
  13.8 5.5 %shard_map.65 = (f32[2,2,60,512]{3,2,1,0:T(8,128)S(1)}, f32[2,32,512]{2,1,0:T(8,128)S(1)}, f32[2,16,256]{2,1,0:T(8,128)S(1)}, f32[6,16,256]{2,1,0:T(8,128)S(1)},...) custom-call(f32[9,32,512]{2,1,0:T(8,128)S(1)} %get-tuple-element.18.own_ref, ...), custom_call_target="tpu_custom_call" | custom-call | tf_op jit(solution)/shard_map/pallas_call | solution.py:576
  19.3 6.1 %collective-permute-start.3 = (f32[11,16,256]{2,1,0:T(8,128)S(1)}, f32[11,16,256]{2,1,0:T(8,128)S(1)}, u32[]{:S(2)}, u32[]{:S(2)}) collective-permute-start(f32[11,16,256]{2,1,0:T(8,128)S(1)} %get-tuple-element.21.own_ref), channel_id=1, source_target_pairs={{1,18},{2,17},{3,20},{4,19},{5,22},{6,21},{7,24},{8,23},{9,26},{10... | collective-permute-start | bytes 540680 | tf_op jit(solution)/shard_map/ppermute | solution.py:543
  25.4 0.1 collective-permute-start.2
  25.5 0.0 collective-permute-start.4
  25.5 2.7 %collective-permute-done.3.first_ref = f32[11,16,256]{2,1,0:T(8,128)S(1)} collective-permute-done((f32[11,16,256]{2,1,0:T(8,128)S(1)}, f32[11,16,256]{2,1,0:T(8,128)S(1)}, u32[]{:S(2)}, u32[]{:S(2)}) %collective-permute-start.3) | collective-permute-done | bytes 180256 | tf_op jit(solution)/shard_map/ppermute | solution.py:543
  28.2 4.3 %collective-permute-done.2.second_ref = f32[11,16,256]{2,1,0:T(8,128)S(1)} collective-permute-done((f32[11,16,256]{2,1,0:T(8,128)S(1)}, f32[11,16,256]{2,1,0:T(8,128)S(1)}, u32[]{:S(2)}, u32[]{:S(2)}) %collective-permute-start.2) | collective-permute-done | bytes 180256 | tf_op jit(solution)/shard_map/ppermute | solution.py:543
  32.6 0.0 collective-permute-done.4
  32.6 9.8 %all-gather = f32[24,40,256]{2,1,0:T(8,128)S(1)} all-gather(f32[6,40,256]{2,1,0:T(8,128)S(1)} %pad_maximum_fusion), channel_id=2, replica_groups=mesh['k'=4,'m'=4,'space'=16] {'m'}, dimensions={0}, use_global_device_ids=true | all-gather | bytes 1228800 | tf_op jit(solution)/shard_map/all_gather | solution.py:603
  42.4 1.3 %collective-permute-start.8 = (f32[2,2,60,512]{3,2,1,0:T(8,128)S(1)}, f32[2,2,60,512]{3,2,1,0:T(8,128)S(1)}, u32[]{:S(2)}, u32[]{:S(2)}) collective-permute-start(f32[2,2,60,512]{3,2,1,0:T(8,128)S(1)} %get-tuple-element.27), channel_id=1, source_target_pairs={{0,16},{1,17},{2,18},{3,19},{4,20},{5,21},{6,22},{7,23},{8,24},{9,... | collective-permute-start | bytes 1474568 | tf_op jit(solution)/shard_map/ppermute | solution.py:533
  43.7 0.8 %shard_map.66 = (f32[4,8,128]{2,1,0:T(8,128)S(1)}, f32[6,40,256]{2,1,0:T(8,128)S(1)}) custom-call(f32[4,6,40,256]{3,2,1,0:T(8,128)S(1)} %bitcast.5, f32[11,16,256]{2,1,0:T(8,128)S(1)} %get-tuple-element.21.own_ref, f32[11,16,256]{2,1,0:T(8,128)S(1)} %collective-permute-done.3.first_ref, f32[11,16,256]{2,1,0:T(8,128)S(1)} %collective-permute-done.2.second_ref), custom_call_target="tpu_custom_call" | custom-call | tf_op jit(solution)/shard_map/pallas_call | solution.py:606
  44.5 1.3 %collective-permute-start.7 = (f32[4,8,128]{2,1,0:T(8,128)S(1)}, f32[4,8,128]{2,1,0:T(8,128)S(1)}, u32[]{:S(2)}, u32[]{:S(2)}) collective-permute-start(f32[4,8,128]{2,1,0:T(8,128)S(1)} %get-tuple-element.25.pred_ref), channel_id=1, source_target_pairs={{49,80},{50,81},{51,82},{52,83},{53,84},{54,85},{55,86},{56,87},{5... | collective-permute-start | bytes 49160 | tf_op jit(solution)/shard_map/ppermute | solution.py:562
  45.8 1.3 %collective-permute-start.6 = (f32[4,8,128]{2,1,0:T(8,128)S(1)}, f32[4,8,128]{2,1,0:T(8,128)S(1)}, u32[]{:S(2)}, u32[]{:S(2)}) collective-permute-start(f32[4,8,128]{2,1,0:T(8,128)S(1)} %get-tuple-element.25.pred_ref), channel_id=1, source_target_pairs={{48,80},{49,81},{50,82},{51,83},{52,84},{53,85},{54,86},{55,87},{5... | collective-permute-start | bytes 49160 | tf_op jit(solution)/shard_map/ppermute | solution.py:562
  47.1 1.3 %collective-permute-start.5 = (f32[4,8,128]{2,1,0:T(8,128)S(1)}, f32[4,8,128]{2,1,0:T(8,128)S(1)}, u32[]{:S(2)}, u32[]{:S(2)}) collective-permute-start(f32[4,8,128]{2,1,0:T(8,128)S(1)} %get-tuple-element.25.pred_ref), channel_id=1, source_target_pairs={{48,81},{49,82},{50,83},{51,84},{52,85},{53,86},{54,87},{55,88},{5... | collective-permute-start | bytes 49160 | tf_op jit(solution)/shard_map/ppermute | solution.py:562
  48.4 2.9 %collective-permute-done.7 = f32[4,8,128]{2,1,0:T(8,128)S(1)} collective-permute-done((f32[4,8,128]{2,1,0:T(8,128)S(1)}, f32[4,8,128]{2,1,0:T(8,128)S(1)}, u32[]{:S(2)}, u32[]{:S(2)}) %collective-permute-start.7) | collective-permute-done | bytes 16416 | tf_op jit(solution)/shard_map/ppermute | solution.py:562
  51.3 1.8 %collective-permute-done.6 = f32[4,8,128]{2,1,0:T(8,128)S(1)} collective-permute-done((f32[4,8,128]{2,1,0:T(8,128)S(1)}, f32[4,8,128]{2,1,0:T(8,128)S(1)}, u32[]{:S(2)}, u32[]{:S(2)}) %collective-permute-start.6) | collective-permute-done | bytes 16416 | tf_op jit(solution)/shard_map/ppermute | solution.py:562
  53.0 2.9 %collective-permute-done.5 = f32[4,8,128]{2,1,0:T(8,128)S(1)} collective-permute-done((f32[4,8,128]{2,1,0:T(8,128)S(1)}, f32[4,8,128]{2,1,0:T(8,128)S(1)}, u32[]{:S(2)}, u32[]{:S(2)}) %collective-permute-start.5) | collective-permute-done | bytes 16416 | tf_op jit(solution)/shard_map/ppermute | solution.py:562
  55.9 7.5 %all-gather.1 = f32[12,4,8,128]{3,2,1,0:T(8,128)S(1)} all-gather(f32[3,4,8,128]{3,2,1,0:T(8,128)S(1)} %pad_maximum_fusion.1), channel_id=3, replica_groups=mesh['k'=4,'m'=4,'space'=16] {'m'}, dimensions={0}, use_global_device_ids=true | all-gather | bytes 245760 | tf_op jit(solution)/shard_map/all_gather | solution.py:615
  63.4 0.0 collective-permute-done.8.a01_ref
  63.4 4.1 %shard_map.67 = f32[16,2,32,512]{3,2,1,0:T(8,128)} custom-call(f32[4,6,40,256]{3,2,1,0:T(8,128)S(1)} %bitcast.6, f32[4,3,4,8,128]{4,3,2,1,0:T(8,128)S(1)} %bitcast.7, f32[4,8,128]{2,1,0:T(8,128)S(1)} %get-tuple-element.25.pred_ref, f32[6,40,256]{2,1,0:T(8,128)S(1)} %get-tuple-element.26.mid_coef, f32[11,16,256]{2,1,0:T(8,128)S(1)} %get-tuple-element.21.own_ref, ...), custom_call_target="tpu_custom_call" | custom-call | tf_op jit(solution)/shard_map/pallas_call | solution.py:616
  (3 shorter events, 0.1 us)
Async XLA Ops:
  1.5 11.9 %collective-permute-start = (f32[9,16,512]{2,1,0:T(8,128)S(1)}, f32[9,16,512]{2,1,0:T(8,128)S(1)}, u32[]{:S(2)}, u32[]{:S(2)}) collective-permute-start(f32[9,16,512]{2,1,0:T(8,128)S(1)} %get-tuple-element.19), channel_id=1, source_target_pairs={{1,2},{2,1},{3,4},{4,3},{5,6},{6,5},{7,8},{8,7},{9,10},{10,9},{11,... | collective-permute-start | bytes 884744 | tf_op jit(solution)/shard_map/ppermute | solution.py:543
  6.1 7.7 %collective-permute-start.1 = (f32[9,16,512]{2,1,0:T(8,128)S(1)}, f32[9,16,512]{2,1,0:T(8,128)S(1)}, u32[]{:S(2)}, u32[]{:S(2)}) collective-permute-start(f32[9,16,512]{2,1,0:T(8,128)S(1)} %get-tuple-element.20), channel_id=1, source_target_pairs={{0,1},{1,0},{2,3},{3,2},{4,5},{5,4},{6,7},{7,6},{8,9},{9,8},{10,11... | collective-permute-start | bytes 884744 | tf_op jit(solution)/shard_map/ppermute | solution.py:543
  19.3 8.9 %collective-permute-start.3 = (f32[11,16,256]{2,1,0:T(8,128)S(1)}, f32[11,16,256]{2,1,0:T(8,128)S(1)}, u32[]{:S(2)}, u32[]{:S(2)}) collective-permute-start(f32[11,16,256]{2,1,0:T(8,128)S(1)} %get-tuple-element.21.own_ref), channel_id=1, source_target_pairs={{1,18},{2,17},{3,20},{4,19},{5,22},{6,21},{7,24},{8,23},{9,26},{10... | collective-permute-start | bytes 540680 | tf_op jit(solution)/shard_map/ppermute | solution.py:543
  25.4 7.2 %collective-permute-start.2 = (f32[11,16,256]{2,1,0:T(8,128)S(1)}, f32[11,16,256]{2,1,0:T(8,128)S(1)}, u32[]{:S(2)}, u32[]{:S(2)}) collective-permute-start(f32[11,16,256]{2,1,0:T(8,128)S(1)} %get-tuple-element.21.own_ref), channel_id=1, source_target_pairs={{0,17},{1,16},{2,19},{3,18},{4,21},{5,20},{6,23},{7,22},{8,25},{9,... | collective-permute-start | bytes 540680 | tf_op jit(solution)/shard_map/ppermute | solution.py:543
  25.5 7.1 %collective-permute-start.4 = (f32[6,16,256]{2,1,0:T(8,128)S(1)}, f32[6,16,256]{2,1,0:T(8,128)S(1)}, u32[]{:S(2)}, u32[]{:S(2)}) collective-permute-start(f32[6,16,256]{2,1,0:T(8,128)S(1)} %get-tuple-element.22), channel_id=1, source_target_pairs={{0,16},{1,17},{2,18},{3,19},{4,20},{5,21},{6,22},{7,23},{8,24},{9,... | collective-permute-start | bytes 294920 | tf_op jit(solution)/shard_map/ppermute | solution.py:533
  42.4 21.0 %collective-permute-start.8 = (f32[2,2,60,512]{3,2,1,0:T(8,128)S(1)}, f32[2,2,60,512]{3,2,1,0:T(8,128)S(1)}, u32[]{:S(2)}, u32[]{:S(2)}) collective-permute-start(f32[2,2,60,512]{3,2,1,0:T(8,128)S(1)} %get-tuple-element.27), channel_id=1, source_target_pairs={{0,16},{1,17},{2,18},{3,19},{4,20},{5,21},{6,22},{7,23},{8,24},{9,... | collective-permute-start | bytes 1474568 | tf_op jit(solution)/shard_map/ppermute | solution.py:533
  44.5 6.8 %collective-permute-start.7 = (f32[4,8,128]{2,1,0:T(8,128)S(1)}, f32[4,8,128]{2,1,0:T(8,128)S(1)}, u32[]{:S(2)}, u32[]{:S(2)}) collective-permute-start(f32[4,8,128]{2,1,0:T(8,128)S(1)} %get-tuple-element.25.pred_ref), channel_id=1, source_target_pairs={{49,80},{50,81},{51,82},{52,83},{53,84},{54,85},{55,86},{56,87},{5... | collective-permute-start | bytes 49160 | tf_op jit(solution)/shard_map/ppermute | solution.py:562
  45.8 7.2 %collective-permute-start.6 = (f32[4,8,128]{2,1,0:T(8,128)S(1)}, f32[4,8,128]{2,1,0:T(8,128)S(1)}, u32[]{:S(2)}, u32[]{:S(2)}) collective-permute-start(f32[4,8,128]{2,1,0:T(8,128)S(1)} %get-tuple-element.25.pred_ref), channel_id=1, source_target_pairs={{48,80},{49,81},{50,82},{51,83},{52,84},{53,85},{54,86},{55,87},{5... | collective-permute-start | bytes 49160 | tf_op jit(solution)/shard_map/ppermute | solution.py:562
  47.1 8.8 %collective-permute-start.5 = (f32[4,8,128]{2,1,0:T(8,128)S(1)}, f32[4,8,128]{2,1,0:T(8,128)S(1)}, u32[]{:S(2)}, u32[]{:S(2)}) collective-permute-start(f32[4,8,128]{2,1,0:T(8,128)S(1)} %get-tuple-element.25.pred_ref), channel_id=1, source_target_pairs={{48,81},{49,82},{50,83},{51,84},{52,85},{53,86},{54,87},{55,88},{5... | collective-permute-start | bytes 49160 | tf_op jit(solution)/shard_map/ppermute | solution.py:562

commit v6 on v5

--- a/solution.py
+++ b/solution.py
@@ -216,7 +216,7 @@
 
 def fine_kernel(
     own_ref, first_ref, second_ref,
-    a01_ref, a2_ref, w2_ref, packed_ref, send_ref, fine_ref,
+    a01_ref, a2_ref, w2_ref, packed_ref, coarse_ref, to_first_ref, to_second_ref, fine_ref,
     s0, s1, raw, tall, mid_state, mid_coef, cells,
 ):
     rows = Rows(cells)
@@ -288,7 +288,14 @@
         w2_ref[q] = coarse[16 * q : 16 * q + 16]
     base = 32
     for f in range(5):
-        send_ref[6 + f] = coarse[base + 32 * f + 8 : base + 32 * f + 24]
+        n = base + 32 * f
+        coarse_ref[f] = coarse[n : n + 32]
+        low, high = coarse[n + 8 : n + 16], coarse[n + 16 : n + 24]
+        slot, r = 6 + f // 2, block(f % 2)
+        to_first_ref[slot, r] = jnp.where(odd, low, high)
+        to_second_ref[slot, r] = jnp.where(odd, high, low)
+    for ref in (to_first_ref, to_second_ref):
+        ref[8, 8:16] = jnp.zeros((8, 256), F32)
     for i in range(4):
         at = [coarse[base + 32 * f + 8 * i : base + 32 * f + 8 * i + 8] for f in range(5)]
         parts = derived(2.0 * at[0], 2.0 * at[1], 8.0 * at[2], 8.0 * at[3], 8.0 * at[4])
@@ -302,7 +309,8 @@
             a01_ref[c, q, 48:60, 0:256] = coarse[n + 4 : n + 16]
             a01_ref[c, q, 48:60, 256:512] = coarse[n + 16 : n + 28]
     for q in range(2):
-        send_ref[4 + q] = mid_state[0, q, 8:24]
+        to_first_ref[4 + q] = mid_state[0, q, 8:24]
+        to_second_ref[4 + q] = mid_state[0, q, 8:24]
         packed_ref[4 + q] = mid_state[0, q, 8:24]
 
     def second_pair(n, carry):
@@ -327,7 +335,8 @@
                 for q in range(2):
                     n = 16 * (2 * c + q) + 8 * (i - 1)
                     forcing = coarse[n : n + 8] - values[q]
-                    send_ref[2 * c + q, block(i - 1)] = forcing
+                    to_first_ref[2 * c + q, block(i - 1)] = forcing
+                    to_second_ref[2 * c + q, block(i - 1)] = forcing
                     packed_ref[2 * c + q, block(i - 1)] = forcing
 
         advance(load, store, lambda i: [mid_coef[n, block(i)] for n in range(6)], (0, 4))
@@ -336,10 +345,11 @@
 def wide_raw(raw, coef_ref, first_ref, second_ref):
     odd = is_odd()
     for f in range(5):
-        first, second = first_ref[6 + f], second_ref[6 + f]
-        raw[f, 0:16] = jnp.where(odd, second, first)
-        raw[f, 16:32] = coef_ref[6 + f]
-        raw[f, 32:48] = jnp.where(odd, first, second)
+        slot, r = 6 + f // 2, block(f % 2)
+        first, second = first_ref[slot, r], second_ref[slot, r]
+        raw[f, 0:8] = jnp.where(odd, second, first)
+        raw[f, 8:40] = coef_ref[f]
+        raw[f, 40:48] = jnp.where(odd, first, second)
 
 
 def wide_mid_coefs(raw, coef_ref, first_ref, second_ref, mid_coef):
@@ -573,14 +583,15 @@
     )(*[far(x) for x in (initial, guess, kappa, feed, kill, react)])
     first = swap(first_edge, 0, True)
     second = swap(second_edge, 0, False)
-    a01, a2, w2, held, packed, fine = pl.pallas_call(
+    a01, a2, w2, held, coarse, to_first, to_second, fine = pl.pallas_call(
         fine_kernel,
         out_shape=(
             struct(2, 2, 60, 512), struct(2, 32, 512), struct(2, 16, 256),
-            struct(6, 16, 256), struct(11, 16, 256), struct(6, 48, 512),
+            struct(6, 16, 256), struct(5, 32, 256), struct(9, 16, 256), struct(9, 16, 256),
+            struct(6, 48, 512),
         ),
         in_specs=[VMEM] * 3,
-        out_specs=(VMEM,) * 6,
+        out_specs=(VMEM,) * 8,
         scratch_shapes=[
             scratch(2, 2, 64, 512), scratch(2, 2, 64, 512), scratch(5, 64, 512),
             scratch(6, 64, 512), scratch(2, 2, 32, 256), scratch(6, 32, 256),
@@ -588,8 +599,8 @@
         ],
         compiler_params=limit(14),
     )(near(own), near(first), near(second))
-    first = swap(packed, 1, True)
-    second = swap(packed, 1, False)
+    first = swap(to_first, 1, True)
+    second = swap(to_second, 1, False)
     middle = shift(held)
     odd = is_odd()
     window = jnp.concatenate(
@@ -610,7 +621,7 @@
         out_specs=(VMEM,) * 2,
         scratch_shapes=[scratch(5, 48, 256), scratch(2, 40, 256), scratch(8, 16, 128)],
         compiler_params=limit(8),
-    )(near(gathered), near(packed), near(first), near(second))
+    )(near(gathered), near(coarse), near(first), near(second))
     pieces = [from_group_behind(pred, ds) for ds in (-1, 0, 1)]
     top = lax.all_gather(jnp.stack(pieces), "m", axis=0, tiled=False)
     return pl.pallas_call(
@@ -624,7 +635,7 @@
             scratch(2, 2, 24, 256), scratch(16, 2, 32, 512), pltpu.SemaphoreType.DMA((16,)),
         ],
         compiler_params=limit(18),
-    )(*[near(x) for x in (gathered, top, pred, mid_coef, packed, first, second, a01, a2, w2, fine)])
+    )(*[near(x) for x in (gathered, top, pred, mid_coef, coarse, first, second, a01, a2, w2, fine)])
 
 
 def solution(mesh):

time: 67.7 us -> 66.9 us (0.988)
  waiting for transfers between devices: 22.2 us -> 21.2 us
  blocking collectives: 17.2 us -> 18 us
    ppermute x4, waiting for transfers between devices: 14.6 us -> 13.8 us  [swap(): return lax.ppermute(x, AXES, pairs)]
    all_gather x1, blocking collectives: 7.47 us -> 8.2 us  [local(): top = lax.all_gather(jnp.stack(pieces), 'm', axis=0, tiled=False)]
  transfers between devices with their start and end apart: 9 -> 9, of which waited for: 7 -> 6; matrix products, arithmetic and copies ran while one was open for 0% -> 0% of each run, Pallas kernels for 1% -> 1%
where the time goes in v6:
time: 66.9 us; the launch traced here: 66.6 us
  waiting for transfers between devices  21.2 us (32%)
  blocking collectives  18 us (27%)
  starting transfers between devices  15.4 us (23%)
  Pallas kernels  11.9 us (18%)
    ppermute x4, waiting for transfers between devices, swap(): return lax.ppermute(x, AXES, pairs)  13.8 us
    ppermute x4, starting transfers between devices, swap(): return lax.ppermute(x, AXES, pairs)  10.8 us
    all_gather x1, blocking collectives, local(): gathered = lax.all_gather(window, 'm', axis=0, tiled=False)  9.78 us
    all_gather x1, blocking collectives, local(): top = lax.all_gather(jnp.stack(pieces), 'm', axis=0, tiled=False)  8.2 us
    ppermute x3, waiting for transfers between devices, from_group_behind(): return lax.ppermute(x, AXES, pairs)  7.4 us
    pallas_call x1, Pallas kernels, local(): pl.pallas_call(fine_kernel, out_shape=(struct(2, 2, 60, 512), struct(2, 3...  5.53 us
    pallas_call x1, Pallas kernels, local(): pl.pallas_call(final_kernel, out_shape=jax.ShapeDtypeStruct((16, 2, 32, 5...  4.12 us
    ppermute x3, starting transfers between devices, from_group_behind(): return lax.ppermute(x, AXES, pairs)  3.88 us
  transfers between devices with their start and end apart: 9, of which 6 were waited for; matrix products, arithmetic and copies ran while one was open for 0% of the time, Pallas kernels for 1%

profile of v6, /device:TPU:153, one launch (start us, length us, event | category | flops | bytes accessed | tf_op | source)
XLA Modules:
  0.0 66.6 jit_solution(16580649582973227829)
XLA Ops:
  0.0 1.5 %shard_map.64 = (f32[9,32,512]{2,1,0:T(8,128)S(1)}, f32[9,16,512]{2,1,0:T(8,128)S(1)}, f32[9,16,512]{2,1,0:T(8,128)S(1)}) custom-call(f32[2,32,512]{2,1,0:T(8,128)} %initial_ref.1, f32[16,2,32,512]{3,2,1,0:T(8,128)} %guess_ref.1, f32[2,32,512]{2,1,0:T(8,128)} %kappa_ref.1, f32[32,512]{1,0:T(8,128)} %feed_ref.1, f32[32,512]{1,0:T(8,128)} %kill_ref.1, ...), custom_call_target="tpu_custom_call" | custom-call | tf_op jit(solution)/shard_map/pallas_call | solution.py:576
  1.5 4.6 %collective-permute-start = (f32[9,16,512]{2,1,0:T(8,128)S(1)}, f32[9,16,512]{2,1,0:T(8,128)S(1)}, u32[]{:S(2)}, u32[]{:S(2)}) collective-permute-start(f32[9,16,512]{2,1,0:T(8,128)S(1)} %get-tuple-element.21), channel_id=1, source_target_pairs={{1,2},{2,1},{3,4},{4,3},{5,6},{6,5},{7,8},{8,7},{9,10},{10,9},{11,... | collective-permute-start | bytes 884744 | tf_op jit(solution)/shard_map/ppermute | solution.py:553
  6.1 0.1 collective-permute-start.1
  6.2 7.2 %collective-permute-done.first_ref = f32[9,16,512]{2,1,0:T(8,128)S(1)} collective-permute-done((f32[9,16,512]{2,1,0:T(8,128)S(1)}, f32[9,16,512]{2,1,0:T(8,128)S(1)}, u32[]{:S(2)}, u32[]{:S(2)}) %collective-permute-start) | collective-permute-done | bytes 294944 | tf_op jit(solution)/shard_map/ppermute | solution.py:553
  13.4 0.4 collective-permute-done.1.second_ref
  13.8 5.5 %shard_map.65 = (f32[2,2,60,512]{3,2,1,0:T(8,128)S(1)}, f32[2,32,512]{2,1,0:T(8,128)S(1)}, f32[2,16,256]{2,1,0:T(8,128)S(1)}, f32[6,16,256]{2,1,0:T(8,128)S(1)},...) custom-call(f32[9,32,512]{2,1,0:T(8,128)S(1)} %get-tuple-element.20., ...), custom_call_target="tpu_custom_call" | custom-call | tf_op jit(solution)/shard_map/pallas_call | solution.py:586
  19.3 2.2 %collective-permute-start.2 = (f32[9,16,256]{2,1,0:T(8,128)S(1)}, f32[9,16,256]{2,1,0:T(8,128)S(1)}, u32[]{:S(2)}, u32[]{:S(2)}) collective-permute-start(f32[9,16,256]{2,1,0:T(8,128)S(1)} %get-tuple-element.23), channel_id=1, source_target_pairs={{0,17},{1,16},{2,19},{3,18},{4,21},{5,20},{6,23},{7,22},{8,25},{9,... | collective-permute-start | bytes 442376 | tf_op jit(solution)/shard_map/ppermute | solution.py:553
  21.5 3.9 %collective-permute-start.3 = (f32[9,16,256]{2,1,0:T(8,128)S(1)}, f32[9,16,256]{2,1,0:T(8,128)S(1)}, u32[]{:S(2)}, u32[]{:S(2)}) collective-permute-start(f32[9,16,256]{2,1,0:T(8,128)S(1)} %get-tuple-element.24), channel_id=1, source_target_pairs={{1,18},{2,17},{3,20},{4,19},{5,22},{6,21},{7,24},{8,23},{9,26},{10... | collective-permute-start | bytes 442376 | tf_op jit(solution)/shard_map/ppermute | solution.py:553
  25.5 0.0 collective-permute-start.4
  25.5 0.0 collective-permute-done.2.second_ref
  25.5 6.2 %collective-permute-done.3.first_ref = f32[9,16,256]{2,1,0:T(8,128)S(1)} collective-permute-done((f32[9,16,256]{2,1,0:T(8,128)S(1)}, f32[9,16,256]{2,1,0:T(8,128)S(1)}, u32[]{:S(2)}, u32[]{:S(2)}) %collective-permute-start.3) | collective-permute-done | bytes 147488 | tf_op jit(solution)/shard_map/ppermute | solution.py:553
  31.7 0.0 collective-permute-done.4
  31.7 9.8 %all-gather = f32[24,40,256]{2,1,0:T(8,128)S(1)} all-gather(f32[6,40,256]{2,1,0:T(8,128)S(1)} %pad_maximum_fusion), channel_id=2, replica_groups=mesh['k'=4,'m'=4,'space'=16] {'m'}, dimensions={0}, use_global_device_ids=true | all-gather | bytes 1228800 | tf_op jit(solution)/shard_map/all_gather | solution.py:614
  41.5 0.7 %collective-permute-start.8 = (f32[2,2,60,512]{3,2,1,0:T(8,128)S(1)}, f32[2,2,60,512]{3,2,1,0:T(8,128)S(1)}, u32[]{:S(2)}, u32[]{:S(2)}) collective-permute-start(f32[2,2,60,512]{3,2,1,0:T(8,128)S(1)} %get-tuple-element.31), channel_id=1, source_target_pairs={{0,16},{1,17},{2,18},{3,19},{4,20},{5,21},{6,22},{7,23},{8,24},{9,... | collective-permute-start | bytes 1474568 | tf_op jit(solution)/shard_map/ppermute | solution.py:543
  42.2 0.8 %shard_map.66 = (f32[4,8,128]{2,1,0:T(8,128)S(1)}, f32[6,40,256]{2,1,0:T(8,128)S(1)}) custom-call(f32[4,6,40,256]{3,2,1,0:T(8,128)S(1)} %bitcast.5, f32[5,32,256]{2,1,0:T(8,128)S(1)} %get-tuple-element.28.own_ref, f32[9,16,256]{2,1,0:T(8,128)S(1)} %collective-permute-done.3.first_ref, f32[9,16,256]{2,1,0:T(8,128)S(1)} %collective-permute-done.2.second_ref), custom_call_target="tpu_custom_call" | custom-call | tf_op jit(solution)/shard_map/pallas_call | solution.py:617
  43.0 1.3 %collective-permute-start.7 = (f32[4,8,128]{2,1,0:T(8,128)S(1)}, f32[4,8,128]{2,1,0:T(8,128)S(1)}, u32[]{:S(2)}, u32[]{:S(2)}) collective-permute-start(f32[4,8,128]{2,1,0:T(8,128)S(1)} %get-tuple-element.29.pred_ref), channel_id=1, source_target_pairs={{49,80},{50,81},{51,82},{52,83},{53,84},{54,85},{55,86},{56,87},{5... | collective-permute-start | bytes 49160 | tf_op jit(solution)/shard_map/ppermute | solution.py:572
  44.3 1.3 %collective-permute-start.6 = (f32[4,8,128]{2,1,0:T(8,128)S(1)}, f32[4,8,128]{2,1,0:T(8,128)S(1)}, u32[]{:S(2)}, u32[]{:S(2)}) collective-permute-start(f32[4,8,128]{2,1,0:T(8,128)S(1)} %get-tuple-element.29.pred_ref), channel_id=1, source_target_pairs={{48,80},{49,81},{50,82},{51,83},{52,84},{53,85},{54,86},{55,87},{5... | collective-permute-start | bytes 49160 | tf_op jit(solution)/shard_map/ppermute | solution.py:572
  45.6 1.3 %collective-permute-start.5 = (f32[4,8,128]{2,1,0:T(8,128)S(1)}, f32[4,8,128]{2,1,0:T(8,128)S(1)}, u32[]{:S(2)}, u32[]{:S(2)}) collective-permute-start(f32[4,8,128]{2,1,0:T(8,128)S(1)} %get-tuple-element.29.pred_ref), channel_id=1, source_target_pairs={{48,81},{49,82},{50,83},{51,84},{52,85},{53,86},{54,87},{55,88},{5... | collective-permute-start | bytes 49160 | tf_op jit(solution)/shard_map/ppermute | solution.py:572
  46.9 2.8 %collective-permute-done.7 = f32[4,8,128]{2,1,0:T(8,128)S(1)} collective-permute-done((f32[4,8,128]{2,1,0:T(8,128)S(1)}, f32[4,8,128]{2,1,0:T(8,128)S(1)}, u32[]{:S(2)}, u32[]{:S(2)}) %collective-permute-start.7) | collective-permute-done | bytes 16416 | tf_op jit(solution)/shard_map/ppermute | solution.py:572
  49.7 2.1 %collective-permute-done.6 = f32[4,8,128]{2,1,0:T(8,128)S(1)} collective-permute-done((f32[4,8,128]{2,1,0:T(8,128)S(1)}, f32[4,8,128]{2,1,0:T(8,128)S(1)}, u32[]{:S(2)}, u32[]{:S(2)}) %collective-permute-start.6) | collective-permute-done | bytes 16416 | tf_op jit(solution)/shard_map/ppermute | solution.py:572
  51.8 2.5 %collective-permute-done.5 = f32[4,8,128]{2,1,0:T(8,128)S(1)} collective-permute-done((f32[4,8,128]{2,1,0:T(8,128)S(1)}, f32[4,8,128]{2,1,0:T(8,128)S(1)}, u32[]{:S(2)}, u32[]{:S(2)}) %collective-permute-start.5) | collective-permute-done | bytes 16416 | tf_op jit(solution)/shard_map/ppermute | solution.py:572
  54.3 8.2 %all-gather.1 = f32[12,4,8,128]{3,2,1,0:T(8,128)S(1)} all-gather(f32[3,4,8,128]{3,2,1,0:T(8,128)S(1)} %pad_maximum_fusion.1), channel_id=3, replica_groups=mesh['k'=4,'m'=4,'space'=16] {'m'}, dimensions={0}, use_global_device_ids=true | all-gather | bytes 245760 | tf_op jit(solution)/shard_map/all_gather | solution.py:626
  62.5 0.0 collective-permute-done.8.a01_ref
  62.5 4.1 %shard_map.67 = f32[16,2,32,512]{3,2,1,0:T(8,128)} custom-call(f32[4,6,40,256]{3,2,1,0:T(8,128)S(1)} %bitcast.6, f32[4,3,4,8,128]{4,3,2,1,0:T(8,128)S(1)} %bitcast.7, f32[4,8,128]{2,1,0:T(8,128)S(1)} %get-tuple-element.29.pred_ref, f32[6,40,256]{2,1,0:T(8,128)S(1)} %get-tuple-element.30.mid_coef, f32[5,32,256]{2,1,0:T(8,128)S(1)} %get-tuple-element.28.own_ref, ...), custom_call_target="tpu_custom_call" | custom-call | tf_op jit(solution)/shard_map/pallas_call | solution.py:627
  (3 shorter events, 0.1 us)
Async XLA Ops:
  1.5 11.9 %collective-permute-start = (f32[9,16,512]{2,1,0:T(8,128)S(1)}, f32[9,16,512]{2,1,0:T(8,128)S(1)}, u32[]{:S(2)}, u32[]{:S(2)}) collective-permute-start(f32[9,16,512]{2,1,0:T(8,128)S(1)} %get-tuple-element.21), channel_id=1, source_target_pairs={{1,2},{2,1},{3,4},{4,3},{5,6},{6,5},{7,8},{8,7},{9,10},{10,9},{11,... | collective-permute-start | bytes 884744 | tf_op jit(solution)/shard_map/ppermute | solution.py:553
  6.1 7.7 %collective-permute-start.1 = (f32[9,16,512]{2,1,0:T(8,128)S(1)}, f32[9,16,512]{2,1,0:T(8,128)S(1)}, u32[]{:S(2)}, u32[]{:S(2)}) collective-permute-start(f32[9,16,512]{2,1,0:T(8,128)S(1)} %get-tuple-element.22), channel_id=1, source_target_pairs={{0,1},{1,0},{2,3},{3,2},{4,5},{5,4},{6,7},{7,6},{8,9},{9,8},{10,11... | collective-permute-start | bytes 884744 | tf_op jit(solution)/shard_map/ppermute | solution.py:553
  19.3 6.2 %collective-permute-start.2 = (f32[9,16,256]{2,1,0:T(8,128)S(1)}, f32[9,16,256]{2,1,0:T(8,128)S(1)}, u32[]{:S(2)}, u32[]{:S(2)}) collective-permute-start(f32[9,16,256]{2,1,0:T(8,128)S(1)} %get-tuple-element.23), channel_id=1, source_target_pairs={{0,17},{1,16},{2,19},{3,18},{4,21},{5,20},{6,23},{7,22},{8,25},{9,... | collective-permute-start | bytes 442376 | tf_op jit(solution)/shard_map/ppermute | solution.py:553
  21.5 10.1 %collective-permute-start.3 = (f32[9,16,256]{2,1,0:T(8,128)S(1)}, f32[9,16,256]{2,1,0:T(8,128)S(1)}, u32[]{:S(2)}, u32[]{:S(2)}) collective-permute-start(f32[9,16,256]{2,1,0:T(8,128)S(1)} %get-tuple-element.24), channel_id=1, source_target_pairs={{1,18},{2,17},{3,20},{4,19},{5,22},{6,21},{7,24},{8,23},{9,26},{10... | collective-permute-start | bytes 442376 | tf_op jit(solution)/shard_map/ppermute | solution.py:553
  25.5 6.2 %collective-permute-start.4 = (f32[6,16,256]{2,1,0:T(8,128)S(1)}, f32[6,16,256]{2,1,0:T(8,128)S(1)}, u32[]{:S(2)}, u32[]{:S(2)}) collective-permute-start(f32[6,16,256]{2,1,0:T(8,128)S(1)} %get-tuple-element.25), channel_id=1, source_target_pairs={{0,16},{1,17},{2,18},{3,19},{4,20},{5,21},{6,22},{7,23},{8,24},{9,... | collective-permute-start | bytes 294920 | tf_op jit(solution)/shard_map/ppermute | solution.py:543
  41.5 21.0 %collective-permute-start.8 = (f32[2,2,60,512]{3,2,1,0:T(8,128)S(1)}, f32[2,2,60,512]{3,2,1,0:T(8,128)S(1)}, u32[]{:S(2)}, u32[]{:S(2)}) collective-permute-start(f32[2,2,60,512]{3,2,1,0:T(8,128)S(1)} %get-tuple-element.31), channel_id=1, source_target_pairs={{0,16},{1,17},{2,18},{3,19},{4,20},{5,21},{6,22},{7,23},{8,24},{9,... | collective-permute-start | bytes 1474568 | tf_op jit(solution)/shard_map/ppermute | solution.py:543
  43.0 6.7 %collective-permute-start.7 = (f32[4,8,128]{2,1,0:T(8,128)S(1)}, f32[4,8,128]{2,1,0:T(8,128)S(1)}, u32[]{:S(2)}, u32[]{:S(2)}) collective-permute-start(f32[4,8,128]{2,1,0:T(8,128)S(1)} %get-tuple-element.29.pred_ref), channel_id=1, source_target_pairs={{49,80},{50,81},{51,82},{52,83},{53,84},{54,85},{55,86},{56,87},{5... | collective-permute-start | bytes 49160 | tf_op jit(solution)/shard_map/ppermute | solution.py:572
  44.3 7.5 %collective-permute-start.6 = (f32[4,8,128]{2,1,0:T(8,128)S(1)}, f32[4,8,128]{2,1,0:T(8,128)S(1)}, u32[]{:S(2)}, u32[]{:S(2)}) collective-permute-start(f32[4,8,128]{2,1,0:T(8,128)S(1)} %get-tuple-element.29.pred_ref), channel_id=1, source_target_pairs={{48,80},{49,81},{50,82},{51,83},{52,84},{53,85},{54,86},{55,87},{5... | collective-permute-start | bytes 49160 | tf_op jit(solution)/shard_map/ppermute | solution.py:572
  45.6 8.7 %collective-permute-start.5 = (f32[4,8,128]{2,1,0:T(8,128)S(1)}, f32[4,8,128]{2,1,0:T(8,128)S(1)}, u32[]{:S(2)}, u32[]{:S(2)}) collective-permute-start(f32[4,8,128]{2,1,0:T(8,128)S(1)} %get-tuple-element.29.pred_ref), channel_id=1, source_target_pairs={{48,81},{49,82},{50,83},{51,84},{52,85},{53,86},{54,87},{55,88},{5... | collective-permute-start | bytes 49160 | tf_op jit(solution)/shard_map/ppermute | solution.py:572
